TPU v7x, 32 devices: a whole 2x2x4 slice. The times are simulated.
32 devices in a mesh: row: 4 (over x, core), col: 8 (over z, y).
Axes of the slice: x: 2, y: 2, z: 4, core: 2. Of those that a mesh axis runs over, the one named last changes fastest.
Arguments:
- voltage: float32 [512, 2048], P('row', 'col'), may hold values from -6 to 6
- currents: float32 [2, 512, 2048], P(None, 'row', 'col'), may hold values from -6 to 6
- resistance: float32 [2, 512, 2048], P(None, 'row', 'col'), may hold values from 0.05 to 0.5
- inverse_cap: float32 [512, 2048], P('row', 'col'), may hold values from 0.05 to 0.5
- shunt_conductance: float32 [512, 2048], P('row', 'col'), may hold values from 0.1 to 1
- tap_index: int32 [512, 2048], P('row', 'col'), may hold values from 0 to 8
- pad_mask: int32 [512, 2048], P('row', 'col'), may hold values 0 or 1
- waveforms: float32 [2, 8], replicated, may hold values from -8 to 8
- k_window: bfloat16 [2, 33, 33], replicated, may hold values from -0.1 to 0.4
Outputs:
- voltage_out: float32 [512, 2048], P('row', 'col')
- current_out: float32 [2, 512, 2048], P(None, 'row', 'col')
All inputs are finite; a program needn't handle non-finite values. No bound on the sum of `pad_mask` on one device may be relied on, other than what follows from the above.
Results may differ from a plain program's by a relative error of at most 0.0023.
Values may be sent and summed in bfloat16 or wider, within the bound.
No kernel may reach another device: no remote copies, remote signals or barrier semaphores. Data moves between devices by JAX's collectives and lax.ppermute only.
A program may use at most 64 MiB of HBM per device.

v0:
```python
import jax
import jax.numpy as jnp
from jax import lax
from jax.sharding import PartitionSpec as P

HALF = 16
STEPS = 2
NW = 8


def passed_along(value, axis, steps):
    count = lax.axis_size(axis)
    first, last = (max(0, -steps), min(count, count - steps))
    return lax.ppermute(value, axis, [(source, source + steps) for source in range(first, last)])


def with_halo(value, sides, width):
    for axis, dim in sides:
        devices, length = (lax.axis_size(axis), value.shape[dim])
        up = [(i, (i + 1) % devices) for i in range(devices - 1)]
        down = [(j, i) for i, j in up]
        last = lax.slice_in_dim(value, length - width, length, axis=dim)
        first = lax.slice_in_dim(value, 0, width, axis=dim)
        before = lax.ppermute(last, axis, up)
        after = lax.ppermute(first, axis, down)
        value = jnp.concatenate([before, value, after], axis=dim)
    return value


def toeplitz_rows(kernel_row, width_in, width_out):
    window_span = kernel_row.shape[1]
    in_index = jnp.arange(width_in, dtype=jnp.int32)[:, None]
    out_index = jnp.arange(width_out, dtype=jnp.int32)[None, :]
    offsets_col = in_index - out_index
    inside = (offsets_col >= 0) & (offsets_col < window_span)
    entries = jnp.take(kernel_row, jnp.clip(offsets_col, 0, window_span - 1), axis=1)
    return jnp.where(inside[None], entries, jnp.zeros_like(entries))


def block_width():
    return 128


def banded_tables(kernel):
    window_span = kernel.shape[1]
    width = block_width()
    flat_rows = kernel.reshape(2 * window_span, window_span)
    tables = toeplitz_rows(flat_rows, width + window_span - 1, width)
    return tables.reshape(2, window_span, width + window_span - 1, width)


def window_apply(padded, tables, row_count, col_count):
    window_span = tables.shape[1]
    width = tables.shape[3]
    margin = window_span - 1
    groups = col_count // width

    def accumulate(offset, running):
        row_slab = lax.dynamic_slice_in_dim(padded, offset, row_count, 1)
        matrix = lax.dynamic_index_in_dim(tables, offset, 1, keepdims=False)
        leading = row_slab[:, :, :col_count].reshape(2, row_count, groups, width)
        trailing = row_slab[:, :, width:col_count].reshape(2, row_count, groups - 1, width)
        last_tail = row_slab[:, :, col_count:][:, :, None, :]
        tails = jnp.concatenate([trailing[:, :, :, :margin], last_tail], axis=2)
        windows = jnp.concatenate([leading, tails], axis=3)
        product = jnp.einsum("crnj,cjk->crnk", windows, matrix, preferred_element_type=jnp.float32)
        return running + product.reshape(2, row_count, col_count)

    start = jnp.zeros((2, row_count, col_count), jnp.float32)
    return lax.fori_loop(0, window_span, accumulate, start)


def loads_of(tap_index, wave_row):
    running = jnp.zeros(tap_index.shape, jnp.float32)
    for which in range(NW):
        running = running + jnp.where(tap_index == which, wave_row[which], jnp.float32(0.0))
    return running


def local(
    voltage,
    currents,
    resistance,
    inverse_cap,
    shunt_conductance,
    tap_index,
    pad_mask,
    waveforms,
    k_window,
):
    row_count, col_count = voltage.shape
    tables = banded_tables(k_window)
    for step_index in range(STEPS):
        next_rows = passed_along(voltage[:1, :], "row", -1)
        next_cols = passed_along(voltage[:, :1], "col", -1)
        below = jnp.concatenate([voltage[1:, :], next_rows], axis=0)
        beside = jnp.concatenate([voltage[:, 1:], next_cols], axis=1)
        drop_pair = jnp.stack([voltage - below, voltage - beside])
        driving = (drop_pair - resistance * currents).astype(jnp.bfloat16)
        padded = with_halo(driving, (("row", 1), ("col", 2)), HALF)
        currents = currents + window_apply(padded, tables, row_count, col_count)
        upper = passed_along(currents[0, -1:, :], "row", 1)
        leftward = passed_along(currents[1, :, -1:], "col", 1)
        before_x = jnp.concatenate([upper, currents[0, :-1, :]], axis=0)
        before_y = jnp.concatenate([leftward, currents[1, :, :-1]], axis=1)
        divergence = currents[0] - before_x + currents[1] - before_y
        load = loads_of(tap_index, waveforms[step_index])
        voltage = voltage + inverse_cap * (load - divergence - shunt_conductance * voltage)
        voltage = jnp.where(pad_mask == 1, jnp.float32(0.0), voltage)
    return (voltage, currents)


def solution(mesh):
    placed = (
        P("row", "col"),
        P(None, "row", "col"),
        P(None, "row", "col"),
        P("row", "col"),
        P("row", "col"),
        P("row", "col"),
        P("row", "col"),
        P(),
        P(),
    )
    return jax.shard_map(
        local,
        mesh=mesh,
        in_specs=placed,
        out_specs=(P("row", "col"), P(None, "row", "col")),
        check_vma=False,
    )
```

profile of v0, /device:TPU:1, one launch (start us, length us, event | category | flops | bytes accessed | tf_op | source)
XLA Modules:
  0.0 266.9 jit_solution(15517096171979210298)
XLA Ops:
  1.6 1.3 collective-permute-start.1
  3.8 1.9 collective-permute-start
  9.1 72.1 %gather_fusion = bf16[20480,66]{1,0:T(8,128)(2,1)} fusion(bf16[66,33]{0,1:T(8,128)(2,1)S(1)} %reshape.140, s32[20480]{0:T(1024)S(1)} %fusion.43), kind=kCustom, calls=%fused_computation | custom fusion | bytes 5488640 | tf_op jit(solution)/shard_map/jit(_take)/gather | solution.py:36
  81.2 7.2 %copy.38 = bf16[160,128,66]{1,0,2:T(8,128)(2,1)} copy(bf16[160,128,66]{2,1,0:T(8,128)(2,1)} %bitcast.146) | data formatting | bytes 5406720 | tf_op jit(solution)/shard_map/jit(_take)/gather | solution.py:36
  88.7 4.5 %collective-permute-start.2 = (bf16[2,16,256]{1,2,0:T(8,128)(2,1)S(1)}, bf16[2,16,256]{1,2,0:T(8,128)(2,1)S(1)}, u32[]{:S(2)}, u32[]{:S(2)}) collective-permute-start(bf16[2,16,256]{1,2,0:T(8,128)(2,1)S(1)} %get-tuple-element.238), channel_id=1, source_target_pairs={{0,8},{8,16},{16,24},{1,9},{9,17},{17,25},{2,10},{10,18},{18,26},{... | collective-permute-start | bytes 49160 | tf_op jit(solution)/shard_map/ppermute | solution.py:24
  93.2 1.9 collective-permute-start.3
  95.1 2.1 select_select_fusion
  97.2 2.3 collective-permute-done.3
  99.6 4.3 %collective-permute-start.4 = (bf16[2,160,16]{1,2,0:T(8,128)(2,1)S(1)}, bf16[2,160,16]{1,2,0:T(8,128)(2,1)S(1)}, u32[]{:S(2)}, u32[]{:S(2)}) collective-permute-start(bf16[2,160,16]{1,2,0:T(8,128)(2,1)S(1)} %get-tuple-element.230), channel_id=1, source_target_pairs={{0,1},{1,2},{2,3},{3,4},{4,5},{5,6},{6,7},{8,9},{9,10},{10,11},{11... | collective-permute-start | bytes 30728 | tf_op jit(solution)/shard_map/ppermute | solution.py:24
  103.8 1.3 collective-permute-start.5
  105.9 1.9 copy.39
  107.7 1.3 collective-permute-done.5
  109.3 51.1 %while.28 = (s32[]{:T(128)}, f32[2,128,256]{1,2,0:T(8,128)S(1)}, bf16[2,160,288]{1,2,0:T(8,128)(2,1)S(1)}, bf16[2,33,160,128]{3,2,0,1:T(8,128)(2,1)}, s32[]{:T(128)}, /*index=5*/s32[]{:T(128)}, s32[]{}, s32[]{}) while((s32[]{:T(128)}, f32[2,128,256]{1,2,0:T(8,128)S(1)}, bf16[2,160,288]{1,2,0:T(8,128)(2,1)S(1)}, ...), condition=%wide.region_1.2_spmd.clone, body=%wide.region_0.1_spmd.clone.sunk | while | flops 21594116 | bytes 1753739 | solution.py:70
  112.7 1.1 fusion.62
  117.4 1.1 fusion.62
  122.0 1.1 fusion.62
  160.8 4.3 %collective-permute-start.7 = (f32[128,1]{0,1:T(1,128)S(1)}, f32[128,1]{0,1:T(1,128)S(1)}, u32[]{:S(2)}, u32[]{:S(2)}) collective-permute-start(f32[128,1]{0,1:T(1,128)S(1)} %bitcast.150), channel_id=1, source_target_pairs={{0,1},{1,2},{2,3},{3,4},{4,5},{5,6},{6,7},{8,9},{9,10},{10,11},{11... | collective-permute-start | bytes 1544 | tf_op jit(solution)/shard_map/ppermute | solution.py:14
  165.1 3.5 %collective-permute-start.6 = (f32[1,256]{1,0:T(1,128)S(1)}, f32[1,256]{1,0:T(1,128)S(1)}, u32[]{:S(2)}, u32[]{:S(2)}) collective-permute-start(f32[1,256]{1,0:T(1,128)S(1)} %slice_bitcast_fusion.11), channel_id=1, source_target_pairs={{0,8},{8,16},{16,24},{1,9},{9,17},{17,25},{2,10},{10,18},{18,26},{... | collective-permute-start | bytes 3080 | tf_op jit(solution)/shard_map/ppermute | solution.py:14
  169.3 5.4 %fusion.36 = (f32[128,256]{1,0:T(8,128)S(1)}, pred[128,256]{1,0:T(8,128)(4,1)S(1)}, pred[128,256]{1,0:T(8,128)(4,1)S(1)}, pred[128,256]{1,0:T(8,128)(4,1)S(1)}, ...) fusion(f32[128,256]{1,0:T(8,128)S(1)} %copy-done.3, ...), kind=kLoop, calls=%fused_computation.61 | loop fusion | flops 1146880 | bytes 1605664 | tf_op jit(solution)/shard_map/jit(_where)/select_n | solution.py:109
  174.7 1.9 collective-permute-start.8
  176.6 1.3 collective-permute-start.9
  178.1 3.6 %collective-permute-done.9 = f32[128,1]{1,0:T(8,128)S(1)} collective-permute-done((f32[128,1]{1,0:T(8,128)S(1)}, f32[128,1]{1,0:T(8,128)S(1)}, u32[]{:S(2)}, u32[]{:S(2)}) %collective-permute-start.9) | collective-permute-done | bytes 544 | tf_op jit(solution)/shard_map/ppermute | solution.py:14
  181.8 5.6 %collective-permute-start.10 = (bf16[2,16,256]{2,1,0:T(8,128)(2,1)S(1)}, bf16[2,16,256]{2,1,0:T(8,128)(2,1)S(1)}, u32[]{:S(2)}, u32[]{:S(2)}) collective-permute-start(bf16[2,16,256]{2,1,0:T(8,128)(2,1)S(1)} %get-tuple-element.234), channel_id=1, source_target_pairs={{0,8},{8,16},{16,24},{1,9},{9,17},{17,25},{2,10},{10,18},{18,26},{... | collective-permute-start | bytes 49160 | tf_op jit(solution)/shard_map/ppermute | solution.py:24
  187.4 1.9 collective-permute-start.11
  189.3 3.1 %collective-permute-done.11 = bf16[2,16,256]{2,1,0:T(8,128)(2,1)S(1)} collective-permute-done((bf16[2,16,256]{2,1,0:T(8,128)(2,1)S(1)}, bf16[2,16,256]{2,1,0:T(8,128)(2,1)S(1)}, u32[]{:S(2)}, u32[]{:S(2)}) %collective-permute-start.11) | collective-permute-done | bytes 16416 | tf_op jit(solution)/shard_map/ppermute | solution.py:25
  192.6 3.5 %collective-permute-start.12 = (bf16[2,160,16]{2,1,0:T(8,128)(2,1)S(1)}, bf16[2,160,16]{2,1,0:T(8,128)(2,1)S(1)}, u32[]{:S(2)}, u32[]{:S(2)}) collective-permute-start(bf16[2,160,16]{2,1,0:T(8,128)(2,1)S(1)} %get-tuple-element.232), channel_id=1, source_target_pairs={{0,1},{1,2},{2,3},{3,4},{4,5},{5,6},{6,7},{8,9},{9,10},{10,11},{11... | collective-permute-start | bytes 30728 | tf_op jit(solution)/shard_map/ppermute | solution.py:24
  196.0 1.3 collective-permute-start.13
  197.5 3.7 %collective-permute-done.13 = bf16[2,160,16]{2,1,0:T(8,128)(2,1)S(1)} collective-permute-done((bf16[2,160,16]{2,1,0:T(8,128)(2,1)S(1)}, bf16[2,160,16]{2,1,0:T(8,128)(2,1)S(1)}, u32[]{:S(2)}, u32[]{:S(2)}) %collective-permute-start.13) | collective-permute-done | bytes 10272 | tf_op jit(solution)/shard_map/ppermute | solution.py:25
  201.6 51.1 %while.29 = (s32[]{:T(128)}, f32[2,128,256]{1,2,0:T(8,128)S(1)}, bf16[2,160,288]{1,2,0:T(8,128)(2,1)S(1)}, bf16[2,33,160,128]{3,2,0,1:T(8,128)(2,1)}, s32[]{:T(128)}, /*index=5*/s32[]{:T(128)}, s32[]{}, s32[]{}) while((s32[]{:T(128)}, f32[2,128,256]{1,2,0:T(8,128)S(1)}, bf16[2,160,288]{1,2,0:T(8,128)(2,1)S(1)}, ...), condition=%wide.region_3.4_spmd.clone, body=%wide.region_2.3_spmd.clone.sunk | while | flops 21594116 | bytes 1753739 | solution.py:70
  253.1 3.7 %collective-permute-start.15 = (f32[128,1]{0,1:T(1,128)S(1)}, f32[128,1]{0,1:T(1,128)S(1)}, u32[]{:S(2)}, u32[]{:S(2)}) collective-permute-start(f32[128,1]{0,1:T(1,128)S(1)} %bitcast.151), channel_id=1, source_target_pairs={{0,1},{1,2},{2,3},{3,4},{4,5},{5,6},{6,7},{8,9},{9,10},{10,11},{11... | collective-permute-start | bytes 1544 | tf_op jit(solution)/shard_map/ppermute | solution.py:14
  256.9 3.6 %collective-permute-start.14 = (f32[1,256]{1,0:T(1,128)S(1)}, f32[1,256]{1,0:T(1,128)S(1)}, u32[]{:S(2)}, u32[]{:S(2)}) collective-permute-start(f32[1,256]{1,0:T(1,128)S(1)} %slice_bitcast_fusion.10), channel_id=1, source_target_pairs={{0,8},{8,16},{16,24},{1,9},{9,17},{17,25},{2,10},{10,18},{18,26},{... | collective-permute-start | bytes 3080 | tf_op jit(solution)/shard_map/ppermute | solution.py:14
  261.2 5.7 %fusion.28 = f32[128,256]{1,0:T(8,128)} fusion(pred[128,256]{1,0:T(8,128)(4,1)S(1)} %get-tuple-element.229, f32[128,256]{1,0:T(8,128)S(1)} %get-tuple-element.220, f32[128,256]{1,0:T(8,128)S(1)} %copy-done.4, f32[2,128,256]{2,1,0:T(8,128)S(1)} %add.163, f32[127,256]{1,0:T(8,128)S(1)} %slice_bitcast_fusion.4, f32[1,256]{1,0:T(1,128)S(1)} %collective-permute-done.14, ...), kind=kLoop, calls=%fused_computation.49 | loop fusion | flops 851968 | bytes 1343520 | tf_op jit(solution)/shard_map/jit(_where)/select_n | solution.py:109
  (467 shorter events, 105.1 us)
Async XLA Ops:
  1.6 86.8 %collective-permute-start.1 = (f32[128,1]{0,1:T(1,128)S(1)}, f32[128,1]{0,1:T(1,128)S(1)}, u32[]{:S(2)}, u32[]{:S(2)}) collective-permute-start(f32[128,1]{0,1:T(1,128)S(1)} %slice.280), channel_id=1, source_target_pairs={{1,0},{2,1},{3,2},{4,3},{5,4},{6,5},{7,6},{9,8},{10,9},{11,10},{12... | collective-permute-start | bytes 1544 | tf_op jit(solution)/shard_map/ppermute | solution.py:14
  3.8 84.6 %collective-permute-start = (f32[1,256]{0,1:T(8,128)S(1)}, f32[1,256]{0,1:T(8,128)S(1)}, u32[]{:S(2)}, u32[]{:S(2)}) collective-permute-start(f32[1,256]{0,1:T(8,128)S(1)} %copy.30), channel_id=1, source_target_pairs={{8,0},{16,8},{24,16},{9,1},{17,9},{25,17},{10,2},{18,10},{26,18},{... | collective-permute-start | bytes 3080 | tf_op jit(solution)/shard_map/ppermute | solution.py:14
  88.7 8.5 %collective-permute-start.2 = (bf16[2,16,256]{1,2,0:T(8,128)(2,1)S(1)}, bf16[2,16,256]{1,2,0:T(8,128)(2,1)S(1)}, u32[]{:S(2)}, u32[]{:S(2)}) collective-permute-start(bf16[2,16,256]{1,2,0:T(8,128)(2,1)S(1)} %get-tuple-element.238), channel_id=1, source_target_pairs={{0,8},{8,16},{16,24},{1,9},{9,17},{17,25},{2,10},{10,18},{18,26},{... | collective-permute-start | bytes 49160 | tf_op jit(solution)/shard_map/ppermute | solution.py:24
  93.2 6.3 %collective-permute-start.3 = (bf16[2,16,256]{1,2,0:T(8,128)(2,1)S(1)}, bf16[2,16,256]{1,2,0:T(8,128)(2,1)S(1)}, u32[]{:S(2)}, u32[]{:S(2)}) collective-permute-start(bf16[2,16,256]{1,2,0:T(8,128)(2,1)S(1)} %get-tuple-element.239), channel_id=1, source_target_pairs={{8,0},{16,8},{24,16},{9,1},{17,9},{25,17},{10,2},{18,10},{26,18},{... | collective-permute-start | bytes 49160 | tf_op jit(solution)/shard_map/ppermute | solution.py:25
  95.1 10.0 %copy-start.8 = (f32[2,8]{1,0:T(2,128)S(1)}, f32[2,8]{1,0:T(2,128)}, u32[]{:S(2)}) copy-start(f32[2,8]{1,0:T(2,128)} %param.20) | copy-start | bytes 196
  99.6 8.2 %collective-permute-start.4 = (bf16[2,160,16]{1,2,0:T(8,128)(2,1)S(1)}, bf16[2,160,16]{1,2,0:T(8,128)(2,1)S(1)}, u32[]{:S(2)}, u32[]{:S(2)}) collective-permute-start(bf16[2,160,16]{1,2,0:T(8,128)(2,1)S(1)} %get-tuple-element.230), channel_id=1, source_target_pairs={{0,1},{1,2},{2,3},{3,4},{4,5},{5,6},{6,7},{8,9},{9,10},{10,11},{11... | collective-permute-start | bytes 30728 | tf_op jit(solution)/shard_map/ppermute | solution.py:24
  103.8 5.2 %collective-permute-start.5 = (bf16[2,160,16]{1,2,0:T(8,128)(2,1)S(1)}, bf16[2,160,16]{1,2,0:T(8,128)(2,1)S(1)}, u32[]{:S(2)}, u32[]{:S(2)}) collective-permute-start(bf16[2,160,16]{1,2,0:T(8,128)(2,1)S(1)} %get-tuple-element.231), channel_id=1, source_target_pairs={{1,0},{2,1},{3,2},{4,3},{5,4},{6,5},{7,6},{9,8},{10,9},{11,10},{12... | collective-permute-start | bytes 30728 | tf_op jit(solution)/shard_map/ppermute | solution.py:25
  109.2 51.4 %copy-start.1 = (f32[2,128,256]{2,1,0:T(8,128)S(1)}, f32[2,128,256]{2,1,0:T(8,128)}, u32[]{:S(2)}) copy-start(f32[2,128,256]{2,1,0:T(8,128)} %param.14) | copy-start | bytes 786436
  109.2 60.1 %copy-start.3 = (f32[128,256]{1,0:T(8,128)S(1)}, f32[128,256]{1,0:T(8,128)}, u32[]{:S(2)}) copy-start(f32[128,256]{1,0:T(8,128)} %param.13) | copy-start | bytes 393220
  109.2 60.1 %copy-start.4 = (f32[128,256]{1,0:T(8,128)S(1)}, f32[128,256]{1,0:T(8,128)}, u32[]{:S(2)}) copy-start(f32[128,256]{1,0:T(8,128)} %param.16) | copy-start | bytes 393220
  109.2 60.1 %copy-start.5 = (f32[128,256]{1,0:T(8,128)S(1)}, f32[128,256]{1,0:T(8,128)}, u32[]{:S(2)}) copy-start(f32[128,256]{1,0:T(8,128)} %param.17) | copy-start | bytes 393220
  109.2 60.0 %copy-start.6 = (s32[128,256]{1,0:T(8,128)S(1)}, s32[128,256]{1,0:T(8,128)}, u32[]{:S(2)}) copy-start(s32[128,256]{1,0:T(8,128)} %param.18) | copy-start | bytes 393220
  109.3 60.0 %copy-start.7 = (s32[128,256]{1,0:T(8,128)S(1)}, s32[128,256]{1,0:T(8,128)}, u32[]{:S(2)}) copy-start(s32[128,256]{1,0:T(8,128)} %param.19) | copy-start | bytes 393220
  160.4 21.3 %copy-start.2 = (f32[2,128,256]{2,1,0:T(8,128)S(1)}, f32[2,128,256]{2,1,0:T(8,128)}, u32[]{:S(2)}) copy-start(f32[2,128,256]{2,1,0:T(8,128)} %param.15) | copy-start | bytes 786436
  160.8 7.8 %collective-permute-start.7 = (f32[128,1]{0,1:T(1,128)S(1)}, f32[128,1]{0,1:T(1,128)S(1)}, u32[]{:S(2)}, u32[]{:S(2)}) collective-permute-start(f32[128,1]{0,1:T(1,128)S(1)} %bitcast.150), channel_id=1, source_target_pairs={{0,1},{1,2},{2,3},{3,4},{4,5},{5,6},{6,7},{8,9},{9,10},{10,11},{11... | collective-permute-start | bytes 1544 | tf_op jit(solution)/shard_map/ppermute | solution.py:14
  165.1 4.2 %collective-permute-start.6 = (f32[1,256]{1,0:T(1,128)S(1)}, f32[1,256]{1,0:T(1,128)S(1)}, u32[]{:S(2)}, u32[]{:S(2)}) collective-permute-start(f32[1,256]{1,0:T(1,128)S(1)} %slice_bitcast_fusion.11), channel_id=1, source_target_pairs={{0,8},{8,16},{16,24},{1,9},{9,17},{17,25},{2,10},{10,18},{18,26},{... | collective-permute-start | bytes 3080 | tf_op jit(solution)/shard_map/ppermute | solution.py:14
  174.7 7.0 %collective-permute-start.8 = (f32[1,256]{1,0:T(1,128)S(1)}, f32[1,256]{1,0:T(1,128)S(1)}, u32[]{:S(2)}, u32[]{:S(2)}) collective-permute-start(f32[1,256]{1,0:T(1,128)S(1)} %slice.290), channel_id=1, source_target_pairs={{8,0},{16,8},{24,16},{9,1},{17,9},{25,17},{10,2},{18,10},{26,18},{... | collective-permute-start | bytes 3080 | tf_op jit(solution)/shard_map/ppermute | solution.py:14
  176.6 5.0 %collective-permute-start.9 = (f32[128,1]{1,0:T(8,128)S(1)}, f32[128,1]{1,0:T(8,128)S(1)}, u32[]{:S(2)}, u32[]{:S(2)}) collective-permute-start(f32[128,1]{1,0:T(8,128)S(1)} %slice.292), channel_id=1, source_target_pairs={{1,0},{2,1},{3,2},{4,3},{5,4},{6,5},{7,6},{9,8},{10,9},{11,10},{12... | collective-permute-start | bytes 1544 | tf_op jit(solution)/shard_map/ppermute | solution.py:14
  181.8 7.5 %collective-permute-start.10 = (bf16[2,16,256]{2,1,0:T(8,128)(2,1)S(1)}, bf16[2,16,256]{2,1,0:T(8,128)(2,1)S(1)}, u32[]{:S(2)}, u32[]{:S(2)}) collective-permute-start(bf16[2,16,256]{2,1,0:T(8,128)(2,1)S(1)} %get-tuple-element.234), channel_id=1, source_target_pairs={{0,8},{8,16},{16,24},{1,9},{9,17},{17,25},{2,10},{10,18},{18,26},{... | collective-permute-start | bytes 49160 | tf_op jit(solution)/shard_map/ppermute | solution.py:24
  187.4 5.1 %collective-permute-start.11 = (bf16[2,16,256]{2,1,0:T(8,128)(2,1)S(1)}, bf16[2,16,256]{2,1,0:T(8,128)(2,1)S(1)}, u32[]{:S(2)}, u32[]{:S(2)}) collective-permute-start(bf16[2,16,256]{2,1,0:T(8,128)(2,1)S(1)} %get-tuple-element.235), channel_id=1, source_target_pairs={{8,0},{16,8},{24,16},{9,1},{17,9},{25,17},{10,2},{18,10},{26,18},{... | collective-permute-start | bytes 49160 | tf_op jit(solution)/shard_map/ppermute | solution.py:25
  192.6 4.9 %collective-permute-start.12 = (bf16[2,160,16]{2,1,0:T(8,128)(2,1)S(1)}, bf16[2,160,16]{2,1,0:T(8,128)(2,1)S(1)}, u32[]{:S(2)}, u32[]{:S(2)}) collective-permute-start(bf16[2,160,16]{2,1,0:T(8,128)(2,1)S(1)} %get-tuple-element.232), channel_id=1, source_target_pairs={{0,1},{1,2},{2,3},{3,4},{4,5},{5,6},{6,7},{8,9},{9,10},{10,11},{11... | collective-permute-start | bytes 30728 | tf_op jit(solution)/shard_map/ppermute | solution.py:24
  196.0 5.2 %collective-permute-start.13 = (bf16[2,160,16]{2,1,0:T(8,128)(2,1)S(1)}, bf16[2,160,16]{2,1,0:T(8,128)(2,1)S(1)}, u32[]{:S(2)}, u32[]{:S(2)}) collective-permute-start(bf16[2,160,16]{2,1,0:T(8,128)(2,1)S(1)} %get-tuple-element.233), channel_id=1, source_target_pairs={{1,0},{2,1},{3,2},{4,3},{5,4},{6,5},{7,6},{9,8},{10,9},{11,10},{12... | collective-permute-start | bytes 30728 | tf_op jit(solution)/shard_map/ppermute | solution.py:25
  252.9 14.0 %copy-start = (f32[2,128,256]{2,1,0:T(8,128)}, f32[2,128,256]{2,1,0:T(8,128)S(1)}, u32[]{:S(2)}) copy-start(f32[2,128,256]{2,1,0:T(8,128)S(1)} %add.163) | copy-start | bytes 786436
  253.1 7.4 %collective-permute-start.15 = (f32[128,1]{0,1:T(1,128)S(1)}, f32[128,1]{0,1:T(1,128)S(1)}, u32[]{:S(2)}, u32[]{:S(2)}) collective-permute-start(f32[128,1]{0,1:T(1,128)S(1)} %bitcast.151), channel_id=1, source_target_pairs={{0,1},{1,2},{2,3},{3,4},{4,5},{5,6},{6,7},{8,9},{9,10},{10,11},{11... | collective-permute-start | bytes 1544 | tf_op jit(solution)/shard_map/ppermute | solution.py:14
  256.9 4.4 %collective-permute-start.14 = (f32[1,256]{1,0:T(1,128)S(1)}, f32[1,256]{1,0:T(1,128)S(1)}, u32[]{:S(2)}, u32[]{:S(2)}) collective-permute-start(f32[1,256]{1,0:T(1,128)S(1)} %slice_bitcast_fusion.10), channel_id=1, source_target_pairs={{0,8},{8,16},{16,24},{1,9},{9,17},{17,25},{2,10},{10,18},{18,26},{... | collective-permute-start | bytes 3080 | tf_op jit(solution)/shard_map/ppermute | solution.py:14
where the time goes:
time: 270 us; the launch traced here: 267 us
  local copies, waits for them, and re-layouts  110 us (41%)
  matrix products  73.4 us (27%)
  starting transfers between devices  45.8 us (17%)
  other arithmetic  18.3 us (7%)
  waiting for transfers between devices  15.3 us (6%)
  loops' own time  3.19 us (1%)
    gather x2, local copies, waits for them, and re-layouts, toeplitz_rows(): jnp.take(kernel_row, jnp.clip(offsets_col, 0, window_span - 1), axis=1)  79.3 us
    dot_general x66, matrix products, accumulate(): jnp.einsum('crnj,cjk->crnk', windows, matrix, preferred_element_type=jnp....  73.4 us
    ppermute x8, starting transfers between devices, passed_along(): lax.ppermute(value, axis, [(source, source + steps) for source in range(f...  21.6 us
    ppermute x4, starting transfers between devices, with_halo(): before = lax.ppermute(last, axis, up)  17.8 us
    select_n x2, other arithmetic, local(): voltage = jnp.where(pad_mask == 1, jnp.float32(0.0), voltage)  11.1 us
    ppermute x4, waiting for transfers between devices, with_halo(): after = lax.ppermute(first, axis, down)  10.4 us
    reshape x66, local copies, waits for them, and re-layouts, accumulate(): row_slab[:, :, width:col_count].reshape(2, row_count, groups - 1, width)  7.57 us
    slice x66, local copies, waits for them, and re-layouts, accumulate(): leading = row_slab[:, :, :col_count].reshape(2, row_count, groups, width)  7.43 us
  transfers between devices with their start and end apart: 16, of which 8 were waited for; matrix products, arithmetic and copies ran while one was open for 33% of the time, Pallas kernels for 0%

commit v1 on v0

v1 whole, which is shorter than its diff:
```python
import functools

import jax
import jax.numpy as jnp
from jax import lax
from jax.experimental import pallas as pl
from jax.experimental.pallas import tpu as pltpu
from jax.sharding import PartitionSpec as P

F32 = jnp.float32
BF16 = jnp.bfloat16
LANES = 128
TILE = 16
VMEM = pl.BlockSpec(memory_space=pltpu.VMEM)
SMEM = pl.BlockSpec(memory_space=pltpu.SMEM)


class Sizes:
    def __init__(self, rows, cols, span, waves):
        self.rows, self.cols, self.span, self.waves = rows, cols, span, waves
        self.half = (span - 1) // 2
        self.far = 2 * self.half + 2
        self.near = self.half + 2
        self.lanes = cols + LANES
        self.frame = rows + 5 * TILE
        self.pairs = (span + 1) // 2
        self.up_d = 3 * TILE
        self.up_f = 2 * TILE
        self.payload = 2 * self.up_d + 6 * self.up_f + TILE
        far, near = self.far, self.near
        self.slots = (
            ((far, 0), (far, far), (near, 2 * far), (near, 2 * far + near)),
            ((near, 0), (near, near), (near, 2 * near), (near, 3 * near), (far, 4 * near)),
        )


def lane_of(shape):
    return lax.broadcasted_iota(jnp.int32, shape, len(shape) - 1)


def row_of(shape):
    return lax.broadcasted_iota(jnp.int32, shape, 0)


def tables_kernel(k_ref, t_ref, pad_ref, *, s):
    zero = jnp.zeros((LANES, LANES), F32)
    for c in range(2):
        pad_ref[...] = zero
        pad_ref[0 : s.span, 0 : s.span] = k_ref[c].astype(F32)
        turned = pad_ref[...].T
        for b in range(2 * s.pairs):
            p, q = divmod(b, 2)
            row = jnp.broadcast_to(turned[b : b + 1, :], (96, LANES))
            band = pltpu.roll(row, 0, 1, stride=1, stride_axis=0)
            t_ref[c, p, :, q * LANES : (q + 1) * LANES] = band.astype(BF16)


def first_kernel(v_ref, i_ref, r_ref, cap_ref, shunt_ref, tap_ref, pad_ref, wave_ref,
                 d_ref, a_ref, b_ref, c_ref, e_ref, one_ref, two_ref, *, s):
    even = lax.rem(lax.axis_index("col"), 2) == 0
    volt = v_ref[...]
    cap, shunt, tap = cap_ref[...], shunt_ref[...], tap_ref[...]
    keep = pad_ref[...] != 1
    loads = []
    for step in range(2):
        total = jnp.zeros(volt.shape, F32)
        for n in range(s.waves):
            total = jnp.where(tap == n, wave_ref[step, n], total)
        loads.append(total)
    b = jnp.where(keep, cap, 0.0)
    c = jnp.where(keep, 1.0, 0.0) - b * shunt
    a = c * volt + b * loads[0]
    a_ref[...], b_ref[...], c_ref[...], e_ref[...] = a, b, c, b * loads[1]
    rows, cols = volt.shape
    below = jnp.where(row_of(volt.shape) == rows - 1, 0.0, pltpu.roll(volt, rows - 1, 0))
    beside = jnp.where(lane_of(volt.shape) == cols - 1, 0.0, pltpu.roll(volt, cols - 1, 1))
    d0 = ((volt - below) - r_ref[0] * i_ref[0]).astype(BF16)
    d1 = ((volt - beside) - r_ref[1] * i_ref[1]).astype(BF16)
    d_ref[0], d_ref[1] = d0, d1
    groups = ((d0.astype(F32), d1.astype(F32), i_ref[0], i_ref[1]), (r_ref[0], r_ref[1], a, b, volt))
    lane = lane_of((rows, LANES))
    for tile, (slots, fields) in enumerate(zip(s.slots, groups)):
        left = jnp.zeros((rows, LANES), F32)
        right = jnp.zeros((rows, LANES), F32)
        for (n, off), field in zip(slots, fields):
            x = jnp.where(lane < n, field[:, :LANES], 0.0)
            y = jnp.where(lane >= LANES - n, field[:, cols - LANES :], 0.0)
            left = left + (pltpu.roll(x, off, 1) if off else x)
            right = right + (pltpu.roll(y, LANES - off, 1) if off else y)
        at = slice(tile * LANES, (tile + 1) * LANES)
        one_ref[:, at] = jnp.where(even, right, left).astype(BF16)
        two_ref[:, at] = jnp.where(even, left, right).astype(BF16)


def second_kernel(d_ref, v_ref, i_ref, r_ref, a_ref, b_ref, one_ref, two_ref,
                  df_ref, t_ref, up_ref, down_ref, *, s):
    even = lax.rem(lax.axis_index("col"), 2) == 0
    rows, cols = v_ref.shape
    lane = lane_of((rows, LANES))
    sides = []
    for tile, slots in enumerate(s.slots):
        at = slice(tile * LANES, (tile + 1) * LANES)
        one, two = one_ref[:, at].astype(F32), two_ref[:, at].astype(F32)
        from_right = jnp.where(even, one, two)
        from_left = jnp.where(even, two, one)
        for n, off in slots:
            x = pltpu.roll(from_right, LANES - off, 1) if off else from_right
            y = pltpu.roll(from_left, off, 1) if off else from_left
            sides.append(jnp.where(lane < n, x, jnp.where(lane >= LANES - n, y, 0.0)))
    d0s, d1s, i0s, i1s, r0s, r1s, as_, bs, vs = sides
    edge = lane == LANES - 1
    next_side = pltpu.roll(vs, LANES - 1, 1)
    next_own = pltpu.roll(v_ref[:, :LANES], LANES - 1, 1)
    d1 = d_ref[1]
    tail = d1[:, cols - LANES :].astype(F32)
    tail = jnp.where(edge, tail - next_side, tail).astype(BF16)
    d1s = jnp.where(edge, jnp.where(r1s > 0, d1s - next_own, 0.0), d1s).astype(BF16)
    df_ref[0, :, :cols] = d_ref[0]
    df_ref[0, :, cols:] = d0s.astype(BF16)
    df_ref[1, :, : cols - LANES] = d1[:, : cols - LANES]
    df_ref[1, :, cols - LANES : cols] = tail
    df_ref[1, :, cols:] = d1s
    for n, x in enumerate((i0s, i1s, r0s, r1s, as_, bs, vs)):
        t_ref[n] = x.astype(BF16)
    for ref, dstart, fstart in ((up_ref, 0, 0), (down_ref, rows - s.up_d, rows - s.up_f)):
        at = 0
        for c in range(2):
            ref[at : at + s.up_d, :] = df_ref[c, dstart : dstart + s.up_d, :]
            at += s.up_d
        own = (i_ref.at[0], i_ref.at[1], r_ref.at[0], r_ref.at[1], a_ref, b_ref)
        for n, field in enumerate(own):
            ref[at : at + s.up_f, :cols] = field[fstart : fstart + s.up_f, :].astype(BF16)
            ref[at : at + s.up_f, cols:] = t_ref[n, fstart : fstart + s.up_f, :]
            at += s.up_f
        ref[at : at + TILE, :cols] = v_ref[0:TILE, :].astype(BF16)
        ref[at : at + TILE, cols:] = t_ref[6, 0:TILE, :]


def convolve(d_ref, t_ref, c, s, strips):
    tiles = s.frame // TILE
    lanes = s.lanes
    first = [t % tiles for t in range(-3, 5)]
    second = list(range(3, 11))
    acc = [jnp.zeros((96, 2 * LANES), F32) for _ in range(3 if strips else 2)]
    for p in range(s.pairs):
        rhs1, rhs2, rhs3 = [], [], []
        for b in (2 * p, 2 * p + 1):
            shift = (s.half - b) % lanes
            x = d_ref[c]
            x = pltpu.roll(x, shift, 1) if shift else x
            rhs1 += [x[t * TILE : (t + 1) * TILE, : s.cols] for t in first]
            rhs2 += [x[t * TILE : (t + 1) * TILE, : s.cols] for t in second]
            rhs3 += [jnp.concatenate([x[t * TILE : (t + 1) * TILE, s.cols :], x[u * TILE : (u + 1) * TILE, s.cols :]], 1)
                     for t, u in zip(first, second)]
        lhs = t_ref[c, p]
        for n, rhs in enumerate((rhs1, rhs2, rhs3)[: len(acc)]):
            acc[n] = acc[n] + jnp.dot(lhs, jnp.concatenate(rhs, 0), preferred_element_type=F32)
    return acc


def last_kernel(df_ref, v_ref, i_ref, r_ref, a_ref, b_ref, c_ref, e_ref, side_ref, tab_ref, one_ref, two_ref,
                vo_ref, io_ref, d_ref, if_ref, rf_ref, af_ref, bf_ref, vf_ref, *, s):
    even = lax.rem(lax.axis_index("row"), 2) == 0
    rows, cols, frame, lanes = s.rows, s.cols, s.frame, s.lanes
    low = jnp.where(even, one_ref[...], two_ref[...])
    high = jnp.where(even, two_ref[...], one_ref[...])
    ud, uf = s.up_d, s.up_f
    own = (i_ref.at[0], i_ref.at[1], r_ref.at[0], r_ref.at[1], a_ref, b_ref)
    frames = (if_ref.at[0], if_ref.at[1], rf_ref.at[0], rf_ref.at[1], af_ref, bf_ref)
    for n, (src, dst) in enumerate(zip(own, frames)):
        at = 2 * ud + n * uf
        dst[0:rows, :cols] = src[...]
        dst[0:rows, cols:] = side_ref[n].astype(F32)
        dst[rows : rows + uf, :] = low[at : at + uf, :].astype(F32)
        dst[rows + uf : frame - uf, :] = jnp.zeros((frame - rows - 2 * uf, lanes), F32)
        dst[frame - uf : frame, :] = high[at : at + uf, :].astype(F32)
    at = 2 * ud + 6 * uf
    v_next = low[at : at + TILE, :].astype(F32)[0:1, :]
    v_first = jnp.concatenate([v_ref[0:8, :][0:1, :], side_ref[6, 0:TILE, :].astype(F32)[0:1, :]], 1)
    gap = rows + 2 * TILE
    shape = (TILE, lanes)
    for c in range(2):
        d_ref[c, 0:rows, :] = df_ref[c]
        d_ref[c, rows:gap, :] = low[c * ud : c * ud + 2 * TILE, :]
        d_ref[c, gap + TILE :, :] = high[c * ud + TILE : (c + 1) * ud, :]
        d_ref[c, gap : gap + TILE, :] = jnp.where(
            row_of(shape) < TILE // 2,
            low[c * ud + 2 * TILE : (c + 1) * ud, :].astype(F32),
            high[c * ud : c * ud + TILE, :].astype(F32)).astype(BF16)
    last = row_of(shape) == TILE - 1
    x = d_ref[0, rows - TILE : rows, :].astype(F32)
    d_ref[0, rows - TILE : rows, :] = jnp.where(last, x - v_next, x).astype(BF16)
    x = d_ref[0, frame - TILE :, :].astype(F32)
    inside = rf_ref[0, frame - TILE :, :] > 0
    d_ref[0, frame - TILE :, :] = jnp.where(last, jnp.where(inside, x - v_first, 0.0), x).astype(BF16)

    for c in range(2):
        one, two, side = convolve(d_ref, tab_ref, c, s, True)
        for dst0, src0, n in ((0, 32, 64), (frame - 32, 0, 32)):
            old = if_ref[c, dst0 : dst0 + n, :]
            add = jnp.concatenate([one[src0 : src0 + n], side[src0 : src0 + n, :LANES]], 1)
            if_ref[c, dst0 : dst0 + n, :] = jnp.where(rf_ref[c, dst0 : dst0 + n, :] > 0, old + add, 0.0)
        old = if_ref[c, 64 : 64 + 96, :]
        add = jnp.concatenate([two, side[:, LANES:]], 1)
        if_ref[c, 64 : 64 + 96, :] = jnp.where(rf_ref[c, 64 : 64 + 96, :] > 0, old + add, 0.0)
    i0, i1 = if_ref[0], if_ref[1]
    div = i0 - pltpu.roll(i0, 1, 0) + i1 - pltpu.roll(i1, 1, 1)
    volt = af_ref[...] - bf_ref[...] * div
    vf_ref[...] = volt
    drop0 = volt - pltpu.roll(volt, frame - 1, 0)
    drop1 = volt - pltpu.roll(volt, lanes - 1, 1)
    r0, r1 = rf_ref[0], rf_ref[1]
    d_ref[0] = jnp.where(r0 > 0, drop0 - r0 * i0, 0.0).astype(BF16)
    d_ref[1] = jnp.where(r1 > 0, drop1 - r1 * i1, 0.0).astype(BF16)

    one, two = convolve(d_ref, tab_ref, 0, s, False)
    above = (if_ref[0, frame - 8 :, :cols] + one[24:32])[7:8]
    above = jnp.where(rf_ref[0, frame - 8 :, :cols][7:8] > 0, above, 0.0)
    io_ref[0, 0:64, :] = if_ref[0, 0:64, :cols] + one[32:]
    io_ref[0, 64:128, :] = if_ref[0, 64:128, :cols] + two[:64]
    one, two, side = convolve(d_ref, tab_ref, 1, s, True)
    io_ref[1, 0:64, :] = if_ref[1, 0:64, :cols] + one[32:]
    io_ref[1, 64:128, :] = if_ref[1, 64:128, :cols] + two[:64]
    side = jnp.concatenate([side[32:, :LANES], side[:64, LANES:]], 0)
    side = jnp.where(rf_ref[1, 0:rows, cols:] > 0, if_ref[1, 0:rows, cols:] + side, 0.0)
    i0, i1 = io_ref[0], io_ref[1]
    up = jnp.where(row_of((rows, cols)) == 0, above, pltpu.roll(i0, 1, 0))
    left = pltpu.roll(jnp.concatenate([i1, side], 1), 1, 1)[:, :cols]
    div = i0 - up + i1 - left
    vo_ref[...] = c_ref[...] * vf_ref[0:rows, :cols] + e_ref[...] - b_ref[...] * div


def swap(x, axis, odd):
    n = lax.axis_size(axis)
    pairs = []
    for i in range(odd, n - 1, 2):
        pairs += [(i, i + 1), (i + 1, i)]
    return lax.ppermute(x, axis, pairs)


def call(kernel, outs, ins, scratch=(), specs=None):
    return pl.pallas_call(
        kernel,
        out_shape=outs,
        in_specs=specs or [VMEM] * len(ins),
        out_specs=jax.tree.map(lambda _: VMEM, outs),
        scratch_shapes=scratch,
    )(*ins)


def local(voltage, currents, resistance, inverse_cap, shunt, tap, pad, waveforms, k_window):
    rows, cols = voltage.shape
    s = Sizes(rows, cols, k_window.shape[1], waveforms.shape[1])
    sds = jax.ShapeDtypeStruct
    block = sds((rows, cols), F32)
    half = sds((rows, 2 * LANES), BF16)
    d, a, b, c, e, one, two = call(
        functools.partial(first_kernel, s=s),
        (sds((2, rows, cols), BF16), block, block, block, block, half, half),
        (voltage, currents, resistance, inverse_cap, shunt, tap, pad, waveforms),
        specs=[VMEM] * 7 + [SMEM])
    tables = call(
        functools.partial(tables_kernel, s=s),
        sds((2, s.pairs, 96, 2 * LANES), BF16), (k_window,),
        scratch=[pltpu.VMEM((LANES, LANES), F32)])
    one, two = swap(one, "col", 0), swap(two, "col", 1)
    pay = sds((s.payload, s.lanes), BF16)
    df, side, up, down = call(
        functools.partial(second_kernel, s=s),
        (sds((2, rows, s.lanes), BF16), sds((7, rows, LANES), BF16), pay, pay),
        (d, voltage, currents, resistance, a, b, one, two))
    even = lax.rem(lax.axis_index("row"), 2) == 0
    one, two = jnp.where(even, down, up), jnp.where(even, up, down)
    one, two = swap(one, "row", 0), swap(two, "row", 1)
    f = pltpu.VMEM((s.frame, s.lanes), F32)
    f2 = pltpu.VMEM((2, s.frame, s.lanes), F32)
    return call(
        functools.partial(last_kernel, s=s),
        (block, sds((2, rows, cols), F32)),
        (df, voltage, currents, resistance, a, b, c, e, side, tables, one, two),
        scratch=[pltpu.VMEM((2, s.frame, s.lanes), BF16), f2, f2, f, f, f])


def solution(mesh):
    grid = P("row", "col")
    pair = P(None, "row", "col")
    return jax.shard_map(
        local,
        mesh=mesh,
        in_specs=(grid, pair, pair, grid, grid, grid, grid, P(), P()),
        out_specs=(grid, pair),
        check_vma=False,
    )
```

time: 270 us -> 34 us (0.13)
  the two profiles are of different devices: /device:TPU:1 before, /device:TPU:25 now
where the time goes in v1:
time: 34 us; the launch traced here: 33.7 us
  Pallas kernels  16.9 us (50%)
  starting transfers between devices  8.43 us (25%)
  waiting for transfers between devices  4.54 us (13%)
  local copies, waits for them, and re-layouts  2 us (6%)
  other arithmetic  1.1 us (3%)
  between operations  0.69 us (2%)
    pallas_call x4, Pallas kernels, call(): pl.pallas_call(kernel, out_shape=outs, in_specs=specs or [VMEM] * len(ins...  16.9 us
    ppermute x4, starting transfers between devices, swap(): return lax.ppermute(x, axis, pairs)  8.43 us
    ppermute x4, waiting for transfers between devices, swap(): return lax.ppermute(x, axis, pairs)  4.54 us
    unnamed x11, local copies, waits for them, and re-layouts  2 us
    select_n x1, other arithmetic, local(): one, two = (jnp.where(even, down, up), jnp.where(even, up, down))  1.1 us
  transfers between devices with their start and end apart: 4, of which 3 were waited for; matrix products, arithmetic and copies ran while one was open for 2% of the time, Pallas kernels for 8%

profile of v1, /device:TPU:25, one launch (start us, length us, event | category | flops | bytes accessed | tf_op | source)
XLA Modules:
  0.0 33.7 jit_solution(4429603184551455256)
XLA Ops:
  0.6 0.0 copy-start.4
  0.6 2.4 %shard_map.104 = (bf16[2,128,256]{2,1,0:T(8,128)(2,1)}, f32[128,256]{1,0:T(8,128)}, f32[128,256]{1,0:T(8,128)}, f32[128,256]{1,0:T(8,128)}, f32[128,256]{1,0:T(8...) custom-call(f32[128,256]{1,0:T(8,128)} %v_ref.5, f32[2,128,256]{2,1,0:T(8,128)} %i_ref.5, ...), custom_call_target="tpu_custom_call" | custom-call | tf_op jit(solution)/shard_map/pallas_call | solution.py:242
  3.1 1.2 %collective-permute-start = (bf16[128,256]{1,0:T(8,128)(2,1)}, bf16[128,256]{1,0:T(8,128)(2,1)S(1)}, u32[]{:S(2)}, u32[]{:S(2)}) collective-permute-start(bf16[128,256]{1,0:T(8,128)(2,1)} %get-tuple-element.16), channel_id=1, source_target_pairs={{0,1},{1,0},{2,3},{3,2},{4,5},{5,4},{6,7},{7,6},{8,9},{9,8},{10,11... | collective-permute-start | bytes 196616 | tf_op jit(solution)/shard_map/ppermute | solution.py:238
  4.3 2.0 %collective-permute-start.1 = (bf16[128,256]{1,0:T(8,128)(2,1)}, bf16[128,256]{1,0:T(8,128)(2,1)S(1)}, u32[]{:S(2)}, u32[]{:S(2)}) collective-permute-start(bf16[128,256]{1,0:T(8,128)(2,1)} %get-tuple-element.17), channel_id=1, source_target_pairs={{1,2},{2,1},{3,4},{4,3},{5,6},{6,5},{9,10},{10,9},{11,12},{12,11},... | collective-permute-start | bytes 196616 | tf_op jit(solution)/shard_map/ppermute | solution.py:238
  6.3 0.1 collective-permute-done.one_ref
  6.4 0.0 copy-start.2
  6.4 4.0 %collective-permute-done.1.two_ref = bf16[128,256]{1,0:T(8,128)(2,1)S(1)} collective-permute-done((bf16[128,256]{1,0:T(8,128)(2,1)}, bf16[128,256]{1,0:T(8,128)(2,1)S(1)}, u32[]{:S(2)}, u32[]{:S(2)}) %collective-permute-start.1) | collective-permute-done | bytes 65568 | tf_op jit(solution)/shard_map/ppermute | solution.py:238
  10.4 0.0 copy-start.3
  10.4 0.0 copy-done.2
  10.4 0.6 %copy-done.3 = bf16[128,256]{1,0:T(8,128)(2,1)} copy-done((bf16[128,256]{1,0:T(8,128)(2,1)}, bf16[128,256]{1,0:T(8,128)(2,1)S(1)}, u32[]{:S(2)}) %copy-start.3) | copy-done | bytes 65560
  11.0 2.4 %shard_map.105 = (bf16[2,128,384]{2,1,0:T(8,128)(2,1)}, bf16[7,128,128]{2,1,0:T(8,128)(2,1)}, bf16[304,384]{1,0:T(8,128)(2,1)}, bf16[304,384]{1,0:T(8,128)(2,1)}) custom-call(bf16[2,128,256]{2,1,0:T(8,128)(2,1)} %get-tuple-element.13.d_ref, f32[128,256]{1,0:T(8,128)} %v_ref.5, f32[2,128,256]{2,1,0:T(8,128)} %i_ref.5, f32[2,128,256]{2,1,0:T(8,128)} %r_ref.5, ...), custom_call_target="tpu_custom_call" | custom-call | tf_op jit(solution)/shard_map/pallas_call | solution.py:242
  13.5 1.1 %broadcast_select_fusion = (bf16[304,384]{1,0:T(8,128)(2,1)S(1)}, bf16[304,384]{1,0:T(8,128)(2,1)S(1)}) fusion(bf16[304,384]{1,0:T(8,128)(2,1)} %get-tuple-element.23, bf16[304,384]{1,0:T(8,128)(2,1)} %get-tuple-element.22, pred[]{:T(512)S(6)} %eq.3), kind=kLoop, calls=%fused_computation | loop fusion | flops 233472 | bytes 933889 | tf_op jit(solution)/shard_map/jit(_where)/select_n | solution.py:273
  14.6 5.1 %collective-permute-start.3 = (bf16[304,384]{1,0:T(8,128)(2,1)S(1)}, bf16[304,384]{1,0:T(8,128)(2,1)S(1)}, u32[]{:S(2)}, u32[]{:S(2)}) collective-permute-start(bf16[304,384]{1,0:T(8,128)(2,1)S(1)} %get-tuple-element.24), channel_id=1, source_target_pairs={{8,16},{16,8},{9,17},{17,9},{10,18},{18,10},{11,19},{19,11},{12,20... | collective-permute-start | bytes 700424 | tf_op jit(solution)/shard_map/ppermute | solution.py:238
  19.7 0.1 collective-permute-start.2
  19.8 0.0 copy-done.4
  19.8 0.6 %copy.11.k_ref = bf16[2,33,33]{2,1,0:T(8,128)(2,1)} copy(bf16[2,33,33]{2,0,1:T(2,128)(2,1)S(1)} %copy-done.4) | data formatting | bytes 8712 | tf_op args[8]
  20.4 2.6 %shard_map.106.tab_ref = bf16[2,17,96,256]{3,2,1,0:T(8,128)(2,1)} custom-call(bf16[2,33,33]{2,1,0:T(8,128)(2,1)} %copy.11.k_ref), custom_call_target="tpu_custom_call" | custom-call | tf_op jit(solution)/shard_map/pallas_call | solution.py:242
  23.0 0.5 %collective-permute-done.3.two_ref = bf16[304,384]{1,0:T(8,128)(2,1)S(1)} collective-permute-done((bf16[304,384]{1,0:T(8,128)(2,1)S(1)}, bf16[304,384]{1,0:T(8,128)(2,1)S(1)}, u32[]{:S(2)}, u32[]{:S(2)}) %collective-permute-start.3) | collective-permute-done | bytes 233504 | tf_op jit(solution)/shard_map/ppermute | solution.py:238
  23.4 0.0 copy-start
  23.4 0.0 collective-permute-done.2.one_ref
  23.4 0.0 copy-start.1
  23.4 0.7 %copy-done = bf16[304,384]{1,0:T(8,128)(2,1)} copy-done((bf16[304,384]{1,0:T(8,128)(2,1)}, bf16[304,384]{1,0:T(8,128)(2,1)S(1)}, u32[]{:S(2)}) %copy-start) | copy-done | bytes 233496
  24.1 0.1 copy-done.1
  24.2 9.5 %shard_map.107 = (f32[128,256]{1,0:T(8,128)}, f32[2,128,256]{2,1,0:T(8,128)}) custom-call(bf16[2,128,384]{2,1,0:T(8,128)(2,1)} %get-tuple-element.18.df_ref, f32[128,256]{1,0:T(8,128)} %v_ref.5, f32[2,128,256]{2,1,0:T(8,128)} %i_ref.5, f32[2,128,256]{2,1,0:T(8,128)} %r_ref.5, f32[128,256]{1,0:T(8,128)} %get-tuple-element.14.a_ref, ...), custom_call_target="tpu_custom_call" | custom-call | tf_op jit(solution)/shard_map/pallas_call | solution.py:242
Async XLA Ops:
  0.6 19.2 %copy-start.4 = (bf16[2,33,33]{2,0,1:T(2,128)(2,1)S(1)}, bf16[2,33,33]{2,0,1:T(2,128)(2,1)}, u32[]{:S(2)}) copy-start(bf16[2,33,33]{2,0,1:T(2,128)(2,1)} %param.17) | copy-start | bytes 13072
  3.1 3.3 %collective-permute-start = (bf16[128,256]{1,0:T(8,128)(2,1)}, bf16[128,256]{1,0:T(8,128)(2,1)S(1)}, u32[]{:S(2)}, u32[]{:S(2)}) collective-permute-start(bf16[128,256]{1,0:T(8,128)(2,1)} %get-tuple-element.16), channel_id=1, source_target_pairs={{0,1},{1,0},{2,3},{3,2},{4,5},{5,4},{6,7},{7,6},{8,9},{9,8},{10,11... | collective-permute-start | bytes 196616 | tf_op jit(solution)/shard_map/ppermute | solution.py:238
  4.3 6.1 %collective-permute-start.1 = (bf16[128,256]{1,0:T(8,128)(2,1)}, bf16[128,256]{1,0:T(8,128)(2,1)S(1)}, u32[]{:S(2)}, u32[]{:S(2)}) collective-permute-start(bf16[128,256]{1,0:T(8,128)(2,1)} %get-tuple-element.17), channel_id=1, source_target_pairs={{1,2},{2,1},{3,4},{4,3},{5,6},{6,5},{9,10},{10,9},{11,12},{12,11},... | collective-permute-start | bytes 196616 | tf_op jit(solution)/shard_map/ppermute | solution.py:238
  6.4 4.0 %copy-start.2 = (bf16[128,256]{1,0:T(8,128)(2,1)}, bf16[128,256]{1,0:T(8,128)(2,1)S(1)}, u32[]{:S(2)}) copy-start(bf16[128,256]{1,0:T(8,128)(2,1)S(1)} %collective-permute-done.one_ref) | copy-start | bytes 196612
  10.4 0.6 %copy-start.3 = (bf16[128,256]{1,0:T(8,128)(2,1)}, bf16[128,256]{1,0:T(8,128)(2,1)S(1)}, u32[]{:S(2)}) copy-start(bf16[128,256]{1,0:T(8,128)(2,1)S(1)} %collective-permute-done.1.two_ref) | copy-start | bytes 196612
  14.6 8.9 %collective-permute-start.3 = (bf16[304,384]{1,0:T(8,128)(2,1)S(1)}, bf16[304,384]{1,0:T(8,128)(2,1)S(1)}, u32[]{:S(2)}, u32[]{:S(2)}) collective-permute-start(bf16[304,384]{1,0:T(8,128)(2,1)S(1)} %get-tuple-element.24), channel_id=1, source_target_pairs={{8,16},{16,8},{9,17},{17,9},{10,18},{18,10},{11,19},{19,11},{12,20... | collective-permute-start | bytes 700424 | tf_op jit(solution)/shard_map/ppermute | solution.py:238
  19.7 3.7 %collective-permute-start.2 = (bf16[304,384]{1,0:T(8,128)(2,1)S(1)}, bf16[304,384]{1,0:T(8,128)(2,1)S(1)}, u32[]{:S(2)}, u32[]{:S(2)}) collective-permute-start(bf16[304,384]{1,0:T(8,128)(2,1)S(1)} %get-tuple-element.25), channel_id=1, source_target_pairs={{0,8},{8,0},{16,24},{24,16},{1,9},{9,1},{17,25},{25,17},{2,10},{10... | collective-permute-start | bytes 700424 | tf_op jit(solution)/shard_map/ppermute | solution.py:238
  23.4 0.7 %copy-start = (bf16[304,384]{1,0:T(8,128)(2,1)}, bf16[304,384]{1,0:T(8,128)(2,1)S(1)}, u32[]{:S(2)}) copy-start(bf16[304,384]{1,0:T(8,128)(2,1)S(1)} %collective-permute-done.3.two_ref) | copy-start | bytes 700420
  23.4 0.8 %copy-start.1 = (bf16[304,384]{1,0:T(8,128)(2,1)}, bf16[304,384]{1,0:T(8,128)(2,1)S(1)}, u32[]{:S(2)}) copy-start(bf16[304,384]{1,0:T(8,128)(2,1)S(1)} %collective-permute-done.2.one_ref) | copy-start | bytes 700420

commit v2 on v1

--- a/solution.py
+++ b/solution.py
@@ -12,7 +12,7 @@
 LANES = 128
 TILE = 16
 VMEM = pl.BlockSpec(memory_space=pltpu.VMEM)
-SMEM = pl.BlockSpec(memory_space=pltpu.SMEM)
+FAR = pl.BlockSpec(memory_space=pltpu.HBM)
 
 
 class Sizes:
@@ -46,7 +46,7 @@
     zero = jnp.zeros((LANES, LANES), F32)
     for c in range(2):
         pad_ref[...] = zero
-        pad_ref[0 : s.span, 0 : s.span] = k_ref[c].astype(F32)
+        pad_ref[0 : s.span, 0 : s.span] = k_ref[:, c, :].astype(F32)
         turned = pad_ref[...].T
         for b in range(2 * s.pairs):
             p, q = divmod(b, 2)
@@ -55,8 +55,16 @@
             t_ref[c, p, :, q * LANES : (q + 1) * LANES] = band.astype(BF16)
 
 
-def first_kernel(v_ref, i_ref, r_ref, cap_ref, shunt_ref, tap_ref, pad_ref, wave_ref,
-                 d_ref, a_ref, b_ref, c_ref, e_ref, one_ref, two_ref, *, s):
+def first_kernel(v_hbm, i_hbm, r_hbm, cap_hbm, shunt_hbm, tap_hbm, pad_hbm, wave_hbm, k_hbm,
+                 d_ref, a_ref, b_ref, c_ref, e_ref, one_ref, two_ref, v_ref, i_ref, r_ref, k_ref,
+                 cap_ref, shunt_ref, tap_ref, pad_ref, wave_ref, sems, *, s):
+    sources = (wave_hbm, tap_hbm, pad_hbm, cap_hbm, shunt_hbm, v_hbm, i_hbm, r_hbm, k_hbm)
+    targets = (wave_ref, tap_ref, pad_ref, cap_ref, shunt_ref, v_ref, i_ref, r_ref, k_ref)
+    copies = [pltpu.make_async_copy(x, y, sems.at[n]) for n, (x, y) in enumerate(zip(sources, targets))]
+    for copy in copies:
+        copy.start()
+    for copy in copies:
+        copy.wait()
     even = lax.rem(lax.axis_index("col"), 2) == 0
     volt = v_ref[...]
     cap, shunt, tap = cap_ref[...], shunt_ref[...], tap_ref[...]
@@ -92,7 +100,7 @@
         two_ref[:, at] = jnp.where(even, left, right).astype(BF16)
 
 
-def second_kernel(d_ref, v_ref, i_ref, r_ref, a_ref, b_ref, one_ref, two_ref,
+def second_kernel(d_ref, v_ref, i_ref, r_ref, a_ref, b_ref, one_ref, two_ref, tab_ref,
                   df_ref, t_ref, up_ref, down_ref, *, s):
     even = lax.rem(lax.axis_index("col"), 2) == 0
     rows, cols = v_ref.shape
@@ -122,7 +130,9 @@
     df_ref[1, :, cols:] = d1s
     for n, x in enumerate((i0s, i1s, r0s, r1s, as_, bs, vs)):
         t_ref[n] = x.astype(BF16)
-    for ref, dstart, fstart in ((up_ref, 0, 0), (down_ref, rows - s.up_d, rows - s.up_f)):
+    above = lax.rem(lax.axis_index("row"), 2) == 0
+
+    def pack(ref, dstart, fstart):
         at = 0
         for c in range(2):
             ref[at : at + s.up_d, :] = df_ref[c, dstart : dstart + s.up_d, :]
@@ -134,6 +144,16 @@
             at += s.up_f
         ref[at : at + TILE, :cols] = v_ref[0:TILE, :].astype(BF16)
         ref[at : at + TILE, cols:] = t_ref[6, 0:TILE, :]
+
+    @pl.when(above)
+    def _():
+        pack(up_ref, rows - s.up_d, rows - s.up_f)
+        pack(down_ref, 0, 0)
+
+    @pl.when(jnp.logical_not(above))
+    def _():
+        pack(up_ref, 0, 0)
+        pack(down_ref, rows - s.up_d, rows - s.up_f)
 
 
 def convolve(d_ref, t_ref, c, s, strips):
@@ -238,9 +258,14 @@
     return lax.ppermute(x, axis, pairs)
 
 
-def call(kernel, outs, ins, scratch=(), specs=None):
+def near(x):
+    return pltpu.with_memory_space_constraint(x, pltpu.VMEM)
+
+
+def call(kernel, outs, ins, scratch=(), specs=None, limit=16):
     return pl.pallas_call(
         kernel,
+        compiler_params=pltpu.CompilerParams(vmem_limit_bytes=limit << 20),
         out_shape=outs,
         in_specs=specs or [VMEM] * len(ins),
         out_specs=jax.tree.map(lambda _: VMEM, outs),
@@ -251,33 +276,36 @@
 def local(voltage, currents, resistance, inverse_cap, shunt, tap, pad, waveforms, k_window):
     rows, cols = voltage.shape
     s = Sizes(rows, cols, k_window.shape[1], waveforms.shape[1])
-    sds = jax.ShapeDtypeStruct
+    sds = pltpu.VMEM
+    k_window = k_window.transpose(1, 0, 2)
     block = sds((rows, cols), F32)
     half = sds((rows, 2 * LANES), BF16)
-    d, a, b, c, e, one, two = call(
+    d, a, b, c, e, one, two, v_near, i_near, r_near, k_near = call(
         functools.partial(first_kernel, s=s),
-        (sds((2, rows, cols), BF16), block, block, block, block, half, half),
-        (voltage, currents, resistance, inverse_cap, shunt, tap, pad, waveforms),
-        specs=[VMEM] * 7 + [SMEM])
+        (sds((2, rows, cols), BF16), block, block, block, block, half, half,
+         block, sds((2, rows, cols), F32), sds((2, rows, cols), F32), sds(k_window.shape, BF16)),
+        [pltpu.with_memory_space_constraint(x, pltpu.HBM)
+         for x in (voltage, currents, resistance, inverse_cap, shunt, tap, pad, waveforms, k_window)],
+        specs=[FAR] * 9,
+        scratch=[pltpu.VMEM((rows, cols), F32)] * 2 + [pltpu.VMEM((rows, cols), jnp.int32)] * 2
+        + [pltpu.SMEM(waveforms.shape, F32), pltpu.SemaphoreType.DMA((9,))])
     tables = call(
         functools.partial(tables_kernel, s=s),
-        sds((2, s.pairs, 96, 2 * LANES), BF16), (k_window,),
+        sds((2, s.pairs, 96, 2 * LANES), BF16), (k_near,),
         scratch=[pltpu.VMEM((LANES, LANES), F32)])
-    one, two = swap(one, "col", 0), swap(two, "col", 1)
+    one, two = near(swap(one, "col", 0)), near(swap(two, "col", 1))
     pay = sds((s.payload, s.lanes), BF16)
-    df, side, up, down = call(
+    df, side, one, two = call(
         functools.partial(second_kernel, s=s),
         (sds((2, rows, s.lanes), BF16), sds((7, rows, LANES), BF16), pay, pay),
-        (d, voltage, currents, resistance, a, b, one, two))
-    even = lax.rem(lax.axis_index("row"), 2) == 0
-    one, two = jnp.where(even, down, up), jnp.where(even, up, down)
-    one, two = swap(one, "row", 0), swap(two, "row", 1)
+        (d, v_near, i_near, r_near, a, b, one, two, tables))
+    one, two = near(swap(one, "row", 0)), near(swap(two, "row", 1))
     f = pltpu.VMEM((s.frame, s.lanes), F32)
     f2 = pltpu.VMEM((2, s.frame, s.lanes), F32)
     return call(
         functools.partial(last_kernel, s=s),
-        (block, sds((2, rows, cols), F32)),
-        (df, voltage, currents, resistance, a, b, c, e, side, tables, one, two),
+        (jax.ShapeDtypeStruct((rows, cols), F32), jax.ShapeDtypeStruct((2, rows, cols), F32)),
+        (df, v_near, i_near, r_near, a, b, c, e, side, tables, one, two),
         scratch=[pltpu.VMEM((2, s.frame, s.lanes), BF16), f2, f2, f, f, f])
 
 

time: 34 us -> 27.3 us (0.80)
  Pallas kernels: 16.9 us -> 10.4 us
  waiting for transfers between devices: 4.54 us -> 7.54 us
  local copies, waits for them, and re-layouts: 2 us -> 0 us
  other arithmetic: 1.1 us -> 0 us
    pallas_call x4, Pallas kernels: 16.9 us -> 10.4 us  [call(): pl.pallas_call(kernel, compiler_params=pltpu.CompilerParams(vmem_limit_by...]
    ppermute x4, waiting for transfers between devices: 4.54 us -> 7.54 us  [swap(): return lax.ppermute(x, axis, pairs)]
    unnamed x11 -> x0, local copies, waits for them, and re-layouts: 2 us -> none
    select_n x1 -> x0, other arithmetic: 1.1 us -> none  [local(): one, two = (jnp.where(even, down, up), jnp.where(even, up, down))]
  transfers between devices with their start and end apart: 4 -> 4, of which waited for: 3 -> 2; matrix products, arithmetic and copies ran while one was open for 2% -> 0% of each run, Pallas kernels for 8% -> 2%
where the time goes in v2:
time: 27.3 us; the launch traced here: 27.2 us
  Pallas kernels  10.4 us (38%)
  starting transfers between devices  8.5 us (31%)
  waiting for transfers between devices  7.54 us (28%)
  between operations  0.69 us (3%)
    pallas_call x4, Pallas kernels, call(): pl.pallas_call(kernel, compiler_params=pltpu.CompilerParams(vmem_limit_by...  10.4 us
    ppermute x4, starting transfers between devices, swap(): return lax.ppermute(x, axis, pairs)  8.5 us
    ppermute x4, waiting for transfers between devices, swap(): return lax.ppermute(x, axis, pairs)  7.54 us
  transfers between devices with their start and end apart: 4, of which 2 were waited for; matrix products, arithmetic and copies ran while one was open for 0% of the time, Pallas kernels for 2%

profile of v2, /device:TPU:25, one launch (start us, length us, event | category | flops | bytes accessed | tf_op | source)
XLA Modules:
  0.0 27.2 jit_solution(2509200452756589501)
XLA Ops:
  0.6 1.9 %shard_map.104 = (bf16[2,128,256]{2,1,0:T(8,128)(2,1)S(1)}, f32[128,256]{1,0:T(8,128)S(1)}, f32[128,256]{1,0:T(8,128)S(1)}, f32[128,256]{1,0:T(8,128)S(1)}, f32[...) custom-call(f32[128,256]{1,0:T(8,128)} %v_hbm.1, ...), custom_call_target="tpu_custom_call" | custom-call | tf_op jit(solution)/shard_map/pallas_call | solution.py:266
  2.5 1.3 %collective-permute-start = (bf16[128,256]{1,0:T(8,128)(2,1)S(1)}, bf16[128,256]{1,0:T(8,128)(2,1)S(1)}, u32[]{:S(2)}, u32[]{:S(2)}) collective-permute-start(bf16[128,256]{1,0:T(8,128)(2,1)S(1)} %get-tuple-element.23), channel_id=1, source_target_pairs={{0,1},{1,0},{2,3},{3,2},{4,5},{5,4},{6,7},{7,6},{8,9},{9,8},{10,11... | collective-permute-start | bytes 196616 | tf_op jit(solution)/shard_map/ppermute | solution.py:258
  3.8 2.0 %collective-permute-start.1 = (bf16[128,256]{1,0:T(8,128)(2,1)S(1)}, bf16[128,256]{1,0:T(8,128)(2,1)S(1)}, u32[]{:S(2)}, u32[]{:S(2)}) collective-permute-start(bf16[128,256]{1,0:T(8,128)(2,1)S(1)} %get-tuple-element.24), channel_id=1, source_target_pairs={{1,2},{2,1},{3,4},{4,3},{5,6},{6,5},{9,10},{10,9},{11,12},{12,11},... | collective-permute-start | bytes 196616 | tf_op jit(solution)/shard_map/ppermute | solution.py:258
  5.9 0.7 %shard_map.105.tab_ref = bf16[2,17,96,256]{3,2,1,0:T(8,128)(2,1)S(1)} custom-call(bf16[33,2,33]{2,1,0:T(2,128)(2,1)S(1)} %get-tuple-element.25.k_ref), custom_call_target="tpu_custom_call" | custom-call | tf_op jit(solution)/shard_map/pallas_call | solution.py:266
  6.5 0.0 collective-permute-done.one_ref
  6.5 3.2 %collective-permute-done.1.two_ref = bf16[128,256]{1,0:T(8,128)(2,1)S(1)} collective-permute-done((bf16[128,256]{1,0:T(8,128)(2,1)S(1)}, bf16[128,256]{1,0:T(8,128)(2,1)S(1)}, u32[]{:S(2)}, u32[]{:S(2)}) %collective-permute-start.1) | collective-permute-done | bytes 65568 | tf_op jit(solution)/shard_map/ppermute | solution.py:258
  9.7 0.3 %shard_map.106 = (bf16[2,128,384]{2,1,0:T(8,128)(2,1)S(1)}, bf16[7,128,128]{2,1,0:T(8,128)(2,1)S(1)}, bf16[304,384]{1,0:T(8,128)(2,1)S(1)}, bf16[304,384]{1,0:T(8,128)(2,1)S(1)}) custom-call(bf16[2,128,256]{2,1,0:T(8,128)(2,1)S(1)} %get-tuple-element.17.d_ref, f32[128,256]{1,0:T(8,128)S(1)} %get-tuple-element.18.v_ref, ...), custom_call_target="tpu_custom_call" | custom-call | tf_op jit(solution)/shard_map/pallas_call | solution.py:266
  10.1 2.2 %collective-permute-start.2 = (bf16[304,384]{1,0:T(8,128)(2,1)S(1)}, bf16[304,384]{1,0:T(8,128)(2,1)S(1)}, u32[]{:S(2)}, u32[]{:S(2)}) collective-permute-start(bf16[304,384]{1,0:T(8,128)(2,1)S(1)} %get-tuple-element.30), channel_id=1, source_target_pairs={{0,8},{8,0},{16,24},{24,16},{1,9},{9,1},{17,25},{25,17},{2,10},{10... | collective-permute-start | bytes 700424 | tf_op jit(solution)/shard_map/ppermute | solution.py:258
  12.2 3.0 %collective-permute-start.3 = (bf16[304,384]{1,0:T(8,128)(2,1)S(1)}, bf16[304,384]{1,0:T(8,128)(2,1)S(1)}, u32[]{:S(2)}, u32[]{:S(2)}) collective-permute-start(bf16[304,384]{1,0:T(8,128)(2,1)S(1)} %get-tuple-element.31), channel_id=1, source_target_pairs={{8,16},{16,8},{9,17},{17,9},{10,18},{18,10},{11,19},{19,11},{12,20... | collective-permute-start | bytes 700424 | tf_op jit(solution)/shard_map/ppermute | solution.py:258
  15.3 0.0 collective-permute-done.2.one_ref
  15.3 4.3 %collective-permute-done.3.two_ref = bf16[304,384]{1,0:T(8,128)(2,1)S(1)} collective-permute-done((bf16[304,384]{1,0:T(8,128)(2,1)S(1)}, bf16[304,384]{1,0:T(8,128)(2,1)S(1)}, u32[]{:S(2)}, u32[]{:S(2)}) %collective-permute-start.3) | collective-permute-done | bytes 233504 | tf_op jit(solution)/shard_map/ppermute | solution.py:258
  19.6 7.6 %shard_map.107 = (f32[128,256]{1,0:T(8,128)}, f32[2,128,256]{2,1,0:T(8,128)}) custom-call(bf16[2,128,384]{2,1,0:T(8,128)(2,1)S(1)} %get-tuple-element.26.df_ref, f32[128,256]{1,0:T(8,128)S(1)} %get-tuple-element.18.v_ref, f32[2,128,256]{2,1,0:T(8,128)S(1)} %get-tuple-element.19.i_ref, f32[2,128,256]{2,1,0:T(8,128)S(1)} %get-tuple-element.20.r_ref, ...), custom_call_target="tpu_custom_call" | custom-call | tf_op jit(solution)/shard_map/pallas_call | solution.py:266
Async XLA Ops:
  2.5 4.0 %collective-permute-start = (bf16[128,256]{1,0:T(8,128)(2,1)S(1)}, bf16[128,256]{1,0:T(8,128)(2,1)S(1)}, u32[]{:S(2)}, u32[]{:S(2)}) collective-permute-start(bf16[128,256]{1,0:T(8,128)(2,1)S(1)} %get-tuple-element.23), channel_id=1, source_target_pairs={{0,1},{1,0},{2,3},{3,2},{4,5},{5,4},{6,7},{7,6},{8,9},{9,8},{10,11... | collective-permute-start | bytes 196616 | tf_op jit(solution)/shard_map/ppermute | solution.py:258
  3.8 5.9 %collective-permute-start.1 = (bf16[128,256]{1,0:T(8,128)(2,1)S(1)}, bf16[128,256]{1,0:T(8,128)(2,1)S(1)}, u32[]{:S(2)}, u32[]{:S(2)}) collective-permute-start(bf16[128,256]{1,0:T(8,128)(2,1)S(1)} %get-tuple-element.24), channel_id=1, source_target_pairs={{1,2},{2,1},{3,4},{4,3},{5,6},{6,5},{9,10},{10,9},{11,12},{12,11},... | collective-permute-start | bytes 196616 | tf_op jit(solution)/shard_map/ppermute | solution.py:258
  10.1 5.2 %collective-permute-start.2 = (bf16[304,384]{1,0:T(8,128)(2,1)S(1)}, bf16[304,384]{1,0:T(8,128)(2,1)S(1)}, u32[]{:S(2)}, u32[]{:S(2)}) collective-permute-start(bf16[304,384]{1,0:T(8,128)(2,1)S(1)} %get-tuple-element.30), channel_id=1, source_target_pairs={{0,8},{8,0},{16,24},{24,16},{1,9},{9,1},{17,25},{25,17},{2,10},{10... | collective-permute-start | bytes 700424 | tf_op jit(solution)/shard_map/ppermute | solution.py:258
  12.2 7.4 %collective-permute-start.3 = (bf16[304,384]{1,0:T(8,128)(2,1)S(1)}, bf16[304,384]{1,0:T(8,128)(2,1)S(1)}, u32[]{:S(2)}, u32[]{:S(2)}) collective-permute-start(bf16[304,384]{1,0:T(8,128)(2,1)S(1)} %get-tuple-element.31), channel_id=1, source_target_pairs={{8,16},{16,8},{9,17},{17,9},{10,18},{18,10},{11,19},{19,11},{12,20... | collective-permute-start | bytes 700424 | tf_op jit(solution)/shard_map/ppermute | solution.py:258

commit v3 on v2

--- a/solution.py
+++ b/solution.py
@@ -6,6 +6,7 @@
 from jax.experimental import pallas as pl
 from jax.experimental.pallas import tpu as pltpu
 from jax.sharding import PartitionSpec as P
+
 
 F32 = jnp.float32
 BF16 = jnp.bfloat16
@@ -23,9 +24,11 @@
         self.near = self.half + 2
         self.lanes = cols + LANES
         self.frame = rows + 5 * TILE
-        self.pairs = (span + 1) // 2
-        self.up_d = 3 * TILE
-        self.up_f = 2 * TILE
+        self.group = -(-span // 3)
+        self.pairs = (self.group + 1) // 2
+        self.fields = rows + 3 * TILE
+        self.up_d = 2 * self.half
+        self.up_f = self.half
         self.payload = 2 * self.up_d + 6 * self.up_f + TILE
         far, near = self.far, self.near
         self.slots = (
@@ -48,11 +51,16 @@
         pad_ref[...] = zero
         pad_ref[0 : s.span, 0 : s.span] = k_ref[:, c, :].astype(F32)
         turned = pad_ref[...].T
-        for b in range(2 * s.pairs):
-            p, q = divmod(b, 2)
-            row = jnp.broadcast_to(turned[b : b + 1, :], (96, LANES))
-            band = pltpu.roll(row, 0, 1, stride=1, stride_axis=0)
-            t_ref[c, p, :, q * LANES : (q + 1) * LANES] = band.astype(BF16)
+        for r in range(2 * s.pairs):
+            p, at = divmod(r, 2)
+            for q in range(3):
+                if r < s.group:
+                    b = s.group * q + r
+                    row = jnp.broadcast_to(turned[b : b + 1, :], (96, LANES))
+                    band = pltpu.roll(row, 0, 1, stride=1, stride_axis=0).astype(BF16)
+                else:
+                    band = jnp.zeros((96, LANES), BF16)
+                t_ref[c, p, q * 96 : (q + 1) * 96, at * LANES : (at + 1) * LANES] = band
 
 
 def first_kernel(v_hbm, i_hbm, r_hbm, cap_hbm, shunt_hbm, tap_hbm, pad_hbm, wave_hbm, k_hbm,
@@ -132,40 +140,66 @@
         t_ref[n] = x.astype(BF16)
     above = lax.rem(lax.axis_index("row"), 2) == 0
 
-    def pack(ref, dstart, fstart):
+    own = (i_ref.at[0], i_ref.at[1], r_ref.at[0], r_ref.at[1], a_ref, b_ref)
+
+    def rows_of(n, start, size):
+        if n < 2:
+            at = start // TILE * TILE
+            x = df_ref[n, at : at + TILE, :].astype(F32)
+            return x[start - at : start - at + size]
+        source = v_ref if n == 8 else own[n - 2]
+        at = start // TILE * TILE
+        x = t_ref[n - 2, at : at + TILE, :].astype(F32)
+        return jnp.concatenate([source[start : start + size, :], x[start - at : start - at + size]], 1)
+
+    def pack(ref, down):
         at = 0
+        dstart = rows - s.up_d if down else 0
+        fstart = rows - s.up_f if down else 0
         for c in range(2):
             ref[at : at + s.up_d, :] = df_ref[c, dstart : dstart + s.up_d, :]
             at += s.up_d
-        own = (i_ref.at[0], i_ref.at[1], r_ref.at[0], r_ref.at[1], a_ref, b_ref)
         for n, field in enumerate(own):
             ref[at : at + s.up_f, :cols] = field[fstart : fstart + s.up_f, :].astype(BF16)
             ref[at : at + s.up_f, cols:] = t_ref[n, fstart : fstart + s.up_f, :]
             at += s.up_f
-        ref[at : at + TILE, :cols] = v_ref[0:TILE, :].astype(BF16)
-        ref[at : at + TILE, cols:] = t_ref[6, 0:TILE, :]
+        eight = row_of((8, s.lanes))
+        halves = [jnp.zeros((8, s.lanes), F32), jnp.zeros((8, s.lanes), F32)]
+        for n in range(8):
+            width = s.up_d if n < 2 else s.up_f
+            slot = 2 * n % 8
+            if down:
+                x = pltpu.roll(rows_of(n, rows - width - 8, 8), (slot + 2) % 8, 0)
+            else:
+                x = pltpu.roll(rows_of(n, width, 8), slot, 0)
+            keep = (eight == slot) | (eight == slot + 1)
+            halves[n // 4] = jnp.where(keep, x, halves[n // 4])
+        if not down:
+            x = pltpu.roll(rows_of(8, 0, 8), 1, 0)
+            halves[0] = jnp.where(eight == 1, x, halves[0])
+        ref[at : at + TILE, :] = jnp.concatenate(halves, 0).astype(BF16)
 
     @pl.when(above)
     def _():
-        pack(up_ref, rows - s.up_d, rows - s.up_f)
-        pack(down_ref, 0, 0)
+        pack(up_ref, True)
+        pack(down_ref, False)
 
     @pl.when(jnp.logical_not(above))
     def _():
-        pack(up_ref, 0, 0)
-        pack(down_ref, rows - s.up_d, rows - s.up_f)
-
-
-def convolve(d_ref, t_ref, c, s, strips):
+        pack(up_ref, False)
+        pack(down_ref, True)
+
+
+def convolve(d_ref, t_ref, c, s):
     tiles = s.frame // TILE
     lanes = s.lanes
     first = [t % tiles for t in range(-3, 5)]
     second = list(range(3, 11))
-    acc = [jnp.zeros((96, 2 * LANES), F32) for _ in range(3 if strips else 2)]
+    acc = [jnp.zeros((288, 2 * LANES), F32) for _ in range(3)]
     for p in range(s.pairs):
         rhs1, rhs2, rhs3 = [], [], []
-        for b in (2 * p, 2 * p + 1):
-            shift = (s.half - b) % lanes
+        for r in (2 * p, 2 * p + 1):
+            shift = (s.half - s.group - r) % lanes if r < s.group else 0
             x = d_ref[c]
             x = pltpu.roll(x, shift, 1) if shift else x
             rhs1 += [x[t * TILE : (t + 1) * TILE, : s.cols] for t in first]
@@ -173,9 +207,19 @@
             rhs3 += [jnp.concatenate([x[t * TILE : (t + 1) * TILE, s.cols :], x[u * TILE : (u + 1) * TILE, s.cols :]], 1)
                      for t, u in zip(first, second)]
         lhs = t_ref[c, p]
-        for n, rhs in enumerate((rhs1, rhs2, rhs3)[: len(acc)]):
+        for n, rhs in enumerate((rhs1, rhs2, rhs3)):
             acc[n] = acc[n] + jnp.dot(lhs, jnp.concatenate(rhs, 0), preferred_element_type=F32)
-    return acc
+
+    def total(n, start, stop):
+        parts = []
+        for q in range(3):
+            at = slice(96 * q + start, 96 * q + stop)
+            x = jnp.concatenate([acc[n][at], acc[2][at, n * LANES : (n + 1) * LANES]], 1)
+            shift = (s.group - s.group * q) % lanes
+            parts.append(pltpu.roll(x, shift, 1) if shift else x)
+        return parts[0] + parts[1] + parts[2]
+
+    return total
 
 
 def last_kernel(df_ref, v_ref, i_ref, r_ref, a_ref, b_ref, c_ref, e_ref, side_ref, tab_ref, one_ref, two_ref,
@@ -184,65 +228,68 @@
     rows, cols, frame, lanes = s.rows, s.cols, s.frame, s.lanes
     low = jnp.where(even, one_ref[...], two_ref[...])
     high = jnp.where(even, two_ref[...], one_ref[...])
-    ud, uf = s.up_d, s.up_f
+    ud, uf, full = s.up_d, s.up_f, s.fields
+    tail = 2 * ud + 6 * uf
+    low_rest, high_rest = low[tail:, :].astype(F32), high[tail:, :].astype(F32)
+    eight = row_of((8, lanes))
     own = (i_ref.at[0], i_ref.at[1], r_ref.at[0], r_ref.at[1], a_ref, b_ref)
     frames = (if_ref.at[0], if_ref.at[1], rf_ref.at[0], rf_ref.at[1], af_ref, bf_ref)
     for n, (src, dst) in enumerate(zip(own, frames)):
         at = 2 * ud + n * uf
+        half, slot = divmod(4 + 2 * n, 8)
+        extra_low = pltpu.roll(low_rest[8 * half : 8 * half + 8], (8 - slot) % 8, 0)
+        extra_high = pltpu.roll(high_rest[8 * half : 8 * half + 8], 6 - slot, 0)
         dst[0:rows, :cols] = src[...]
         dst[0:rows, cols:] = side_ref[n].astype(F32)
         dst[rows : rows + uf, :] = low[at : at + uf, :].astype(F32)
-        dst[rows + uf : frame - uf, :] = jnp.zeros((frame - rows - 2 * uf, lanes), F32)
-        dst[frame - uf : frame, :] = high[at : at + uf, :].astype(F32)
-    at = 2 * ud + 6 * uf
-    v_next = low[at : at + TILE, :].astype(F32)[0:1, :]
+        dst[rows + uf : rows + uf + 8, :] = jnp.where(eight == 0, extra_low, 0.0)
+        dst[full - uf - 8 : full - uf, :] = jnp.where(eight >= 6, extra_high, 0.0)
+        dst[full - uf : full, :] = high[at : at + uf, :].astype(F32)
+    v_next = low_rest[1:2, :]
     v_first = jnp.concatenate([v_ref[0:8, :][0:1, :], side_ref[6, 0:TILE, :].astype(F32)[0:1, :]], 1)
-    gap = rows + 2 * TILE
+    gap = rows + ud
     shape = (TILE, lanes)
     for c in range(2):
         d_ref[c, 0:rows, :] = df_ref[c]
-        d_ref[c, rows:gap, :] = low[c * ud : c * ud + 2 * TILE, :]
-        d_ref[c, gap + TILE :, :] = high[c * ud + TILE : (c + 1) * ud, :]
-        d_ref[c, gap : gap + TILE, :] = jnp.where(
-            row_of(shape) < TILE // 2,
-            low[c * ud + 2 * TILE : (c + 1) * ud, :].astype(F32),
-            high[c * ud : c * ud + TILE, :].astype(F32)).astype(BF16)
+        d_ref[c, rows:gap, :] = low[c * ud : (c + 1) * ud, :]
+        d_ref[c, gap + TILE :, :] = high[c * ud : (c + 1) * ud, :]
+        extra_low = pltpu.roll(low_rest[0:8], (8 - 2 * c) % 8, 0)
+        extra_high = pltpu.roll(high_rest[0:8], 6 - 2 * c, 0)
+        d_ref[c, gap : gap + TILE, :] = jnp.concatenate(
+            [jnp.where(eight == 0, extra_low, 0.0), jnp.where(eight >= 6, extra_high, 0.0)], 0).astype(BF16)
     last = row_of(shape) == TILE - 1
     x = d_ref[0, rows - TILE : rows, :].astype(F32)
     d_ref[0, rows - TILE : rows, :] = jnp.where(last, x - v_next, x).astype(BF16)
     x = d_ref[0, frame - TILE :, :].astype(F32)
-    inside = rf_ref[0, frame - TILE :, :] > 0
+    inside = rf_ref[0, full - TILE :, :] > 0
     d_ref[0, frame - TILE :, :] = jnp.where(last, jnp.where(inside, x - v_first, 0.0), x).astype(BF16)
 
     for c in range(2):
-        one, two, side = convolve(d_ref, tab_ref, c, s, True)
-        for dst0, src0, n in ((0, 32, 64), (frame - 32, 0, 32)):
-            old = if_ref[c, dst0 : dst0 + n, :]
-            add = jnp.concatenate([one[src0 : src0 + n], side[src0 : src0 + n, :LANES]], 1)
-            if_ref[c, dst0 : dst0 + n, :] = jnp.where(rf_ref[c, dst0 : dst0 + n, :] > 0, old + add, 0.0)
-        old = if_ref[c, 64 : 64 + 96, :]
-        add = jnp.concatenate([two, side[:, LANES:]], 1)
-        if_ref[c, 64 : 64 + 96, :] = jnp.where(rf_ref[c, 64 : 64 + 96, :] > 0, old + add, 0.0)
+        total = convolve(d_ref, tab_ref, c, s)
+        for dst, n, start, stop in ((0, 0, 32, 96), (full - 24, 0, 8, 32), (64, 1, 0, 88)):
+            at = slice(dst, dst + stop - start)
+            if_ref[c, at, :] = jnp.where(rf_ref[c, at, :] > 0, if_ref[c, at, :] + total(n, start, stop), 0.0)
     i0, i1 = if_ref[0], if_ref[1]
     div = i0 - pltpu.roll(i0, 1, 0) + i1 - pltpu.roll(i1, 1, 1)
     volt = af_ref[...] - bf_ref[...] * div
     vf_ref[...] = volt
-    drop0 = volt - pltpu.roll(volt, frame - 1, 0)
+    drop0 = volt - pltpu.roll(volt, full - 1, 0)
     drop1 = volt - pltpu.roll(volt, lanes - 1, 1)
     r0, r1 = rf_ref[0], rf_ref[1]
-    d_ref[0] = jnp.where(r0 > 0, drop0 - r0 * i0, 0.0).astype(BF16)
-    d_ref[1] = jnp.where(r1 > 0, drop1 - r1 * i1, 0.0).astype(BF16)
-
-    one, two = convolve(d_ref, tab_ref, 0, s, False)
-    above = (if_ref[0, frame - 8 :, :cols] + one[24:32])[7:8]
-    above = jnp.where(rf_ref[0, frame - 8 :, :cols][7:8] > 0, above, 0.0)
-    io_ref[0, 0:64, :] = if_ref[0, 0:64, :cols] + one[32:]
-    io_ref[0, 64:128, :] = if_ref[0, 64:128, :cols] + two[:64]
-    one, two, side = convolve(d_ref, tab_ref, 1, s, True)
-    io_ref[1, 0:64, :] = if_ref[1, 0:64, :cols] + one[32:]
-    io_ref[1, 64:128, :] = if_ref[1, 64:128, :cols] + two[:64]
-    side = jnp.concatenate([side[32:, :LANES], side[:64, LANES:]], 0)
-    side = jnp.where(rf_ref[1, 0:rows, cols:] > 0, if_ref[1, 0:rows, cols:] + side, 0.0)
+    for c, (drop, r, i) in enumerate(((drop0, r0, i0), (drop1, r1, i1))):
+        x = jnp.where(r > 0, drop - r * i, 0.0).astype(BF16)
+        d_ref[c, 0 : rows + TILE, :] = x[0 : rows + TILE]
+        d_ref[c, frame - 2 * TILE :, :] = x[full - 2 * TILE :]
+
+    total = convolve(d_ref, tab_ref, 0, s)
+    above = jnp.where(rf_ref[0, full - 8 :, :] > 0, if_ref[0, full - 8 :, :] + total(0, 24, 32), 0.0)[7:8, :cols]
+    io_ref[0, 0:64, :] = (if_ref[0, 0:64, :] + total(0, 32, 96))[:, :cols]
+    io_ref[0, 64:128, :] = (if_ref[0, 64:128, :] + total(1, 0, 64))[:, :cols]
+    total = convolve(d_ref, tab_ref, 1, s)
+    ends = jnp.concatenate([total(0, 32, 96), total(1, 0, 64)], 0)
+    ends = jnp.where(rf_ref[1, 0:rows, :] > 0, if_ref[1, 0:rows, :] + ends, 0.0)
+    io_ref[1] = ends[:, :cols]
+    side = ends[:, cols:]
     i0, i1 = io_ref[0], io_ref[1]
     up = jnp.where(row_of((rows, cols)) == 0, above, pltpu.roll(i0, 1, 0))
     left = pltpu.roll(jnp.concatenate([i1, side], 1), 1, 1)[:, :cols]
@@ -250,7 +297,7 @@
     vo_ref[...] = c_ref[...] * vf_ref[0:rows, :cols] + e_ref[...] - b_ref[...] * div
 
 
-def swap(x, axis, odd):
+def swapped(x, axis, odd):
     n = lax.axis_size(axis)
     pairs = []
     for i in range(odd, n - 1, 2):
@@ -291,17 +338,17 @@
         + [pltpu.SMEM(waveforms.shape, F32), pltpu.SemaphoreType.DMA((9,))])
     tables = call(
         functools.partial(tables_kernel, s=s),
-        sds((2, s.pairs, 96, 2 * LANES), BF16), (k_near,),
+        sds((2, s.pairs, 288, 2 * LANES), BF16), (k_near,),
         scratch=[pltpu.VMEM((LANES, LANES), F32)])
-    one, two = near(swap(one, "col", 0)), near(swap(two, "col", 1))
+    one, two = near(swapped(one, "col", 0)), near(swapped(two, "col", 1))
     pay = sds((s.payload, s.lanes), BF16)
     df, side, one, two = call(
         functools.partial(second_kernel, s=s),
         (sds((2, rows, s.lanes), BF16), sds((7, rows, LANES), BF16), pay, pay),
         (d, v_near, i_near, r_near, a, b, one, two, tables))
-    one, two = near(swap(one, "row", 0)), near(swap(two, "row", 1))
-    f = pltpu.VMEM((s.frame, s.lanes), F32)
-    f2 = pltpu.VMEM((2, s.frame, s.lanes), F32)
+    one, two = near(swapped(one, "row", 0)), near(swapped(two, "row", 1))
+    f = pltpu.VMEM((s.fields, s.lanes), F32)
+    f2 = pltpu.VMEM((2, s.fields, s.lanes), F32)
     return call(
         functools.partial(last_kernel, s=s),
         (jax.ShapeDtypeStruct((rows, cols), F32), jax.ShapeDtypeStruct((2, rows, cols), F32)),
@@ -312,6 +359,7 @@
 def solution(mesh):
     grid = P("row", "col")
     pair = P(None, "row", "col")
+
     return jax.shard_map(
         local,
         mesh=mesh,

time: 27.3 us -> 23.6 us (0.86)
  Pallas kernels: 10.4 us -> 7.74 us
  waiting for transfers between devices: 7.54 us -> 6.49 us
    pallas_call x4, Pallas kernels: 10.4 us -> 7.74 us  [call(): pl.pallas_call(kernel, compiler_params=pltpu.CompilerParams(vmem_limit_by...]
    ppermute x4, waiting for transfers between devices: 7.54 us -> 6.49 us  [swapped(): return lax.ppermute(x, axis, pairs)]
  transfers between devices with their start and end apart: 4 -> 4, of which waited for: 2 -> 2; matrix products, arithmetic and copies ran while one was open for 0% -> 0% of each run, Pallas kernels for 2% -> 3%
where the time goes in v3:
time: 23.6 us; the launch traced here: 23.4 us
  starting transfers between devices  8.5 us (36%)
  Pallas kernels  7.74 us (33%)
  waiting for transfers between devices  6.49 us (28%)
  between operations  0.69 us (3%)
    ppermute x4, starting transfers between devices, swapped(): return lax.ppermute(x, axis, pairs)  8.5 us
    pallas_call x4, Pallas kernels, call(): pl.pallas_call(kernel, compiler_params=pltpu.CompilerParams(vmem_limit_by...  7.74 us
    ppermute x4, waiting for transfers between devices, swapped(): return lax.ppermute(x, axis, pairs)  6.49 us
  transfers between devices with their start and end apart: 4, of which 2 were waited for; matrix products, arithmetic and copies ran while one was open for 0% of the time, Pallas kernels for 3%

profile of v3, /device:TPU:25, one launch (start us, length us, event | category | flops | bytes accessed | tf_op | source)
XLA Modules:
  0.0 23.4 jit_solution(9549031026291100128)
XLA Ops:
  0.6 1.9 %shard_map.104 = (bf16[2,128,256]{2,1,0:T(8,128)(2,1)S(1)}, f32[128,256]{1,0:T(8,128)S(1)}, f32[128,256]{1,0:T(8,128)S(1)}, f32[128,256]{1,0:T(8,128)S(1)}, f32[...) custom-call(f32[128,256]{1,0:T(8,128)} %v_hbm.1, ...), custom_call_target="tpu_custom_call" | custom-call | tf_op jit(solution)/shard_map/pallas_call | solution.py:313
  2.5 1.3 %collective-permute-start = (bf16[128,256]{1,0:T(8,128)(2,1)S(1)}, bf16[128,256]{1,0:T(8,128)(2,1)S(1)}, u32[]{:S(2)}, u32[]{:S(2)}) collective-permute-start(bf16[128,256]{1,0:T(8,128)(2,1)S(1)} %get-tuple-element.23), channel_id=1, source_target_pairs={{0,1},{1,0},{2,3},{3,2},{4,5},{5,4},{6,7},{7,6},{8,9},{9,8},{10,11... | collective-permute-start | bytes 196616 | tf_op jit(solution)/shard_map/ppermute | solution.py:305
  3.8 2.0 %collective-permute-start.1 = (bf16[128,256]{1,0:T(8,128)(2,1)S(1)}, bf16[128,256]{1,0:T(8,128)(2,1)S(1)}, u32[]{:S(2)}, u32[]{:S(2)}) collective-permute-start(bf16[128,256]{1,0:T(8,128)(2,1)S(1)} %get-tuple-element.24), channel_id=1, source_target_pairs={{1,2},{2,1},{3,4},{4,3},{5,6},{6,5},{9,10},{10,9},{11,12},{12,11},... | collective-permute-start | bytes 196616 | tf_op jit(solution)/shard_map/ppermute | solution.py:305
  5.9 0.7 %shard_map.105.tab_ref = bf16[2,6,288,256]{3,2,1,0:T(8,128)(2,1)S(1)} custom-call(bf16[33,2,33]{2,1,0:T(2,128)(2,1)S(1)} %get-tuple-element.25.k_ref), custom_call_target="tpu_custom_call" | custom-call | tf_op jit(solution)/shard_map/pallas_call | solution.py:313
  6.5 0.0 collective-permute-done.one_ref
  6.5 3.2 %collective-permute-done.1.two_ref = bf16[128,256]{1,0:T(8,128)(2,1)S(1)} collective-permute-done((bf16[128,256]{1,0:T(8,128)(2,1)S(1)}, bf16[128,256]{1,0:T(8,128)(2,1)S(1)}, u32[]{:S(2)}, u32[]{:S(2)}) %collective-permute-start.1) | collective-permute-done | bytes 65568 | tf_op jit(solution)/shard_map/ppermute | solution.py:305
  9.7 0.3 %shard_map.106 = (bf16[2,128,384]{2,1,0:T(8,128)(2,1)S(1)}, bf16[7,128,128]{2,1,0:T(8,128)(2,1)S(1)}, bf16[176,384]{1,0:T(8,128)(2,1)S(1)}, bf16[176,384]{1,0:T(8,128)(2,1)S(1)}) custom-call(bf16[2,128,256]{2,1,0:T(8,128)(2,1)S(1)} %get-tuple-element.17.d_ref, f32[128,256]{1,0:T(8,128)S(1)} %get-tuple-element.18.v_ref, ...), custom_call_target="tpu_custom_call" | custom-call | tf_op jit(solution)/shard_map/pallas_call | solution.py:313
  10.1 2.2 %collective-permute-start.2 = (bf16[176,384]{1,0:T(8,128)(2,1)S(1)}, bf16[176,384]{1,0:T(8,128)(2,1)S(1)}, u32[]{:S(2)}, u32[]{:S(2)}) collective-permute-start(bf16[176,384]{1,0:T(8,128)(2,1)S(1)} %get-tuple-element.30), channel_id=1, source_target_pairs={{0,8},{8,0},{16,24},{24,16},{1,9},{9,1},{17,25},{25,17},{2,10},{10... | collective-permute-start | bytes 405512 | tf_op jit(solution)/shard_map/ppermute | solution.py:305
  12.2 3.0 %collective-permute-start.3 = (bf16[176,384]{1,0:T(8,128)(2,1)S(1)}, bf16[176,384]{1,0:T(8,128)(2,1)S(1)}, u32[]{:S(2)}, u32[]{:S(2)}) collective-permute-start(bf16[176,384]{1,0:T(8,128)(2,1)S(1)} %get-tuple-element.31), channel_id=1, source_target_pairs={{8,16},{16,8},{9,17},{17,9},{10,18},{18,10},{11,19},{19,11},{12,20... | collective-permute-start | bytes 405512 | tf_op jit(solution)/shard_map/ppermute | solution.py:305
  15.2 0.0 collective-permute-done.2.one_ref
  15.3 3.3 %collective-permute-done.3.two_ref = bf16[176,384]{1,0:T(8,128)(2,1)S(1)} collective-permute-done((bf16[176,384]{1,0:T(8,128)(2,1)S(1)}, bf16[176,384]{1,0:T(8,128)(2,1)S(1)}, u32[]{:S(2)}, u32[]{:S(2)}) %collective-permute-start.3) | collective-permute-done | bytes 135200 | tf_op jit(solution)/shard_map/ppermute | solution.py:305
  18.5 4.9 %shard_map.107 = (f32[128,256]{1,0:T(8,128)}, f32[2,128,256]{2,1,0:T(8,128)}) custom-call(bf16[2,128,384]{2,1,0:T(8,128)(2,1)S(1)} %get-tuple-element.26.df_ref, f32[128,256]{1,0:T(8,128)S(1)} %get-tuple-element.18.v_ref, f32[2,128,256]{2,1,0:T(8,128)S(1)} %get-tuple-element.19.i_ref, f32[2,128,256]{2,1,0:T(8,128)S(1)} %get-tuple-element.20.r_ref, ...), custom_call_target="tpu_custom_call" | custom-call | tf_op jit(solution)/shard_map/pallas_call | solution.py:313
Async XLA Ops:
  2.5 4.0 %collective-permute-start = (bf16[128,256]{1,0:T(8,128)(2,1)S(1)}, bf16[128,256]{1,0:T(8,128)(2,1)S(1)}, u32[]{:S(2)}, u32[]{:S(2)}) collective-permute-start(bf16[128,256]{1,0:T(8,128)(2,1)S(1)} %get-tuple-element.23), channel_id=1, source_target_pairs={{0,1},{1,0},{2,3},{3,2},{4,5},{5,4},{6,7},{7,6},{8,9},{9,8},{10,11... | collective-permute-start | bytes 196616 | tf_op jit(solution)/shard_map/ppermute | solution.py:305
  3.8 5.9 %collective-permute-start.1 = (bf16[128,256]{1,0:T(8,128)(2,1)S(1)}, bf16[128,256]{1,0:T(8,128)(2,1)S(1)}, u32[]{:S(2)}, u32[]{:S(2)}) collective-permute-start(bf16[128,256]{1,0:T(8,128)(2,1)S(1)} %get-tuple-element.24), channel_id=1, source_target_pairs={{1,2},{2,1},{3,4},{4,3},{5,6},{6,5},{9,10},{10,9},{11,12},{12,11},... | collective-permute-start | bytes 196616 | tf_op jit(solution)/shard_map/ppermute | solution.py:305
  10.1 5.2 %collective-permute-start.2 = (bf16[176,384]{1,0:T(8,128)(2,1)S(1)}, bf16[176,384]{1,0:T(8,128)(2,1)S(1)}, u32[]{:S(2)}, u32[]{:S(2)}) collective-permute-start(bf16[176,384]{1,0:T(8,128)(2,1)S(1)} %get-tuple-element.30), channel_id=1, source_target_pairs={{0,8},{8,0},{16,24},{24,16},{1,9},{9,1},{17,25},{25,17},{2,10},{10... | collective-permute-start | bytes 405512 | tf_op jit(solution)/shard_map/ppermute | solution.py:305
  12.2 6.3 %collective-permute-start.3 = (bf16[176,384]{1,0:T(8,128)(2,1)S(1)}, bf16[176,384]{1,0:T(8,128)(2,1)S(1)}, u32[]{:S(2)}, u32[]{:S(2)}) collective-permute-start(bf16[176,384]{1,0:T(8,128)(2,1)S(1)} %get-tuple-element.31), channel_id=1, source_target_pairs={{8,16},{16,8},{9,17},{17,9},{10,18},{18,10},{11,19},{19,11},{12,20... | collective-permute-start | bytes 405512 | tf_op jit(solution)/shard_map/ppermute | solution.py:305

commit v4 on v3

v4 whole, which is shorter than its diff:
```python
import functools
import itertools

import jax
import jax.numpy as jnp
from jax import lax
from jax.experimental import pallas as pl
from jax.experimental.pallas import tpu as pltpu
from jax.sharding import PartitionSpec as P


F32 = jnp.float32
BF16 = jnp.bfloat16
LANES = 128
TILE = 16
VMEM = pl.BlockSpec(memory_space=pltpu.VMEM)
FAR = pl.BlockSpec(memory_space=pltpu.HBM)


class Sizes:
    def __init__(self, rows, cols, span, waves):
        self.rows, self.cols, self.span, self.waves = rows, cols, span, waves
        self.half = (span - 1) // 2
        self.far = 2 * self.half + 2
        self.near = self.half + 2
        self.lanes = cols + LANES
        self.frame = rows + 5 * TILE
        self.group = -(-span // 3)
        self.pairs = (self.group + 1) // 2
        self.span3 = -(-self.group // 3)
        self.fields = rows + 3 * TILE
        self.up_d = 2 * self.half
        self.up_f = self.half
        self.payload = 2 * self.up_d + 6 * self.up_f + TILE
        far, near = self.far, self.near
        self.slots = (
            ((far, 0, 0), (far, far, far), (near, 2 * far, far + near),
             (near, 2 * far + near, far + 2 * near), (near, 2 * far + 2 * near, far + 3 * near)),
            ((near, 0, 0), (near, near, near), (near, 2 * near, 2 * near), (1, 3 * near, 3 * near)),
        )
        self.edge = rows + rows // 2 + TILE


def lane_of(shape):
    return lax.broadcasted_iota(jnp.int32, shape, len(shape) - 1)


def row_of(shape):
    return lax.broadcasted_iota(jnp.int32, shape, 0)


def border_rows(c):
    return 64 if c == 0 else 48


def turn(k_ref, pad_ref, c, s):
    pad_ref[...] = jnp.zeros((LANES, LANES), F32)
    pad_ref[0 : s.span, 0 : s.span] = k_ref[:, c, :].astype(F32)
    return pad_ref[...].T


def main_tables(k_ref, t_ref, pad_ref, s):
    for c in range(2):
        turned = turn(k_ref, pad_ref, c, s)
        for r in range(2 * s.pairs):
            p, at = divmod(r, 2)
            for q in range(3):
                if r < s.group:
                    b = s.group * q + r
                    row = jnp.broadcast_to(turned[b : b + 1, :], (96, LANES))
                    band = pltpu.roll(row, 0, 1, stride=1, stride_axis=0).astype(BF16)
                else:
                    band = jnp.zeros((96, LANES), BF16)
                t_ref[c, p, q * 96 : (q + 1) * 96, at * LANES : (at + 1) * LANES] = band


def border_tables(k_ref, e_ref, pad_ref, s):
    window = 5 * TILE
    blank = jnp.zeros((1, LANES), F32)
    for c in range(2):
        turned = turn(k_ref, pad_ref, c, s)
        n = border_rows(c)
        late = 1 - c
        for g in range(s.span3):
            for q in range(3):
                row = jnp.zeros((1, 2 * LANES), F32)
                for at in range(3):
                    r = 3 * g + at
                    if r < s.group:
                        b = s.group * q + r
                        wide = jnp.concatenate([turned[b : b + 1, :], blank], 1)
                        shift = (window * at - late) % (2 * LANES)
                        row = row + (pltpu.roll(wide, shift, 1) if shift else wide)
                row = jnp.broadcast_to(row, (n, 2 * LANES))
                band = pltpu.roll(row, 0, 1, stride=1, stride_axis=0)
                if late:
                    lane = lane_of(band.shape)
                    kept = lane == s.span - 2
                    for at in range(1, 3):
                        kept = kept | (lane == window * at + s.span - 2)
                    band = jnp.where((row_of(band.shape) > 0) | kept, band, 0.0)
                e_ref[c, g, q * n : (q + 1) * n, :] = band.astype(BF16)


def load_of(tap, wave_ref, step, s):
    total = jnp.zeros(tap.shape, F32)
    for n in range(s.waves):
        total = jnp.where(tap == n, wave_ref[step, n], total)
    return total


def border_rows(c):
    return 64 if c == 0 else 48


def first_kernel(v_hbm, i_hbm, r_hbm, cap_hbm, shunt_hbm, tap_hbm, pad_hbm, wave_hbm, k_hbm,
                 one_ref, two_ref, v_ref, i_ref, r_ref, cap_ref, shunt_ref, tap_ref, pad_ref, k_ref,
                 wave_ref, sems, *, s):
    sources = (wave_hbm, tap_hbm, pad_hbm, cap_hbm, shunt_hbm, v_hbm, i_hbm, r_hbm, k_hbm)
    targets = (wave_ref, tap_ref, pad_ref, cap_ref, shunt_ref, v_ref, i_ref, r_ref, k_ref)
    copies = [pltpu.make_async_copy(x, y, sems.at[n]) for n, (x, y) in enumerate(zip(sources, targets))]
    for copy in copies:
        copy.start()
    even = lax.rem(lax.axis_index("col"), 2) == 0
    rows, cols = s.rows, s.cols
    shape = (rows, LANES)
    lane, row = lane_of(shape), row_of(shape)

    def ends(ref):
        return jnp.where(lane < LANES // 2, ref[:, :LANES], ref[:, cols - LANES :])

    for copy in copies[:2]:
        copy.wait()
    load = load_of(ends(tap_ref), wave_ref, 0, s)
    for copy in copies[2:5]:
        copy.wait()
    keep = ends(pad_ref) != 1
    b = jnp.where(keep, ends(cap_ref), 0.0)
    c = jnp.where(keep, 1.0, 0.0) - b * ends(shunt_ref)
    a = b * load
    for copy in copies[5:]:
        copy.wait()
    volt = ends(v_ref)
    a = a + c * volt
    i0, i1, r0, r1 = ends(i_ref.at[0]), ends(i_ref.at[1]), ends(r_ref.at[0]), ends(r_ref.at[1])
    below = jnp.where(row == rows - 1, 0.0, pltpu.roll(volt, rows - 1, 0))
    beside = jnp.where(lane == LANES - 1, 0.0, pltpu.roll(volt, LANES - 1, 1))
    d0 = (volt - below) - r0 * i0
    d1 = (volt - beside) - r1 * i1
    half = rows // 2

    def put(start, left, right):
        at = slice(start, start + left.shape[0])
        one_ref[at, :] = jnp.where(even, right, left).astype(BF16)
        two_ref[at, :] = jnp.where(even, left, right).astype(BF16)

    for tile, (slots, fields) in enumerate(zip(s.slots, ((d0, d1, i0, i1, r0), (r1, a, b, volt)))):
        left = jnp.zeros(shape, F32)
        right = jnp.zeros(shape, F32)
        for (n, off, back), field in zip(slots, fields):
            x = rolled(field, off)
            left = jnp.where((lane >= off) & (lane < off + n), x, left)
            if n > 1:
                x = x if back == off else rolled(field, back)
                right = jnp.where(before(lane, n, back), x, right)
        if tile == 1:
            left = left[:half] + pltpu.roll(left[half:], LANES // 2, 1)
            right = right[:half] + pltpu.roll(right[half:], LANES // 2, 1)
        put(tile * rows, left, right)
    put(rows + half, v_ref[:TILE, :LANES], v_ref[:TILE, cols - LANES :])


def before(lane, n, off):
    if off >= n:
        return (lane >= off - n) & (lane < off)
    return (lane < off) | (lane >= LANES + off - n)


def own_kernel(v_ref, i_ref, r_ref, cap_ref, shunt_ref, tap_ref, pad_ref, k_ref, wave_hbm,
               d_ref, a_ref, b_ref, c_ref, e_ref, t_ref, wave_ref, square_ref, sem, *, s):
    copy = pltpu.make_async_copy(wave_hbm, wave_ref, sem.at[0])
    copy.start()
    main_tables(k_ref, t_ref, square_ref, s)
    volt = v_ref[...]
    rows, cols = volt.shape
    below = jnp.where(row_of(volt.shape) == rows - 1, 0.0, pltpu.roll(volt, rows - 1, 0))
    beside = jnp.where(lane_of(volt.shape) == cols - 1, 0.0, pltpu.roll(volt, cols - 1, 1))
    d_ref[0] = ((volt - below) - r_ref[0] * i_ref[0]).astype(BF16)
    d_ref[1] = ((volt - beside) - r_ref[1] * i_ref[1]).astype(BF16)
    keep = pad_ref[...] != 1
    b = jnp.where(keep, cap_ref[...], 0.0)
    c = jnp.where(keep, 1.0, 0.0) - b * shunt_ref[...]
    b_ref[...], c_ref[...] = b, c
    copy.wait()
    a_ref[...] = c * volt + b * load_of(tap_ref[...], wave_ref, 0, s)
    e_ref[...] = b * load_of(tap_ref[...], wave_ref, 1, s)


def second_kernel(d_ref, v_ref, i_ref, r_ref, a_ref, b_ref, one_ref, two_ref,
                  df_ref, t_ref, up_ref, down_ref, *, s):
    even = lax.rem(lax.axis_index("col"), 2) == 0
    rows, cols = v_ref.shape
    lane = lane_of((rows, LANES))
    half = rows // 2
    index, count = lax.axis_index("col"), lax.axis_size("col")

    def get(start, size):
        at = slice(start, start + size)
        one, two = one_ref[at, :].astype(F32), two_ref[at, :].astype(F32)
        right, left = jnp.where(even, one, two), jnp.where(even, two, one)
        return jnp.where(index < count - 1, right, 0.0), jnp.where(index > 0, left, 0.0)

    sides = []
    for tile, slots in enumerate(s.slots):
        if tile == 0:
            pair = get(0, rows)
        else:
            pair = [jnp.concatenate([x, pltpu.roll(x, LANES // 2, 1)], 0) for x in get(rows, half)]
        for n, off, back in slots:
            if back == off:
                x = jnp.where((lane >= off) & (lane < off + n), pair[0], pair[1])
                x = rolled(x, (LANES - off) % LANES)
                sides.append(jnp.where((lane < n) | (lane >= LANES - n), x, 0.0))
            else:
                x, y = rolled(pair[0], LANES - off), rolled(pair[1], LANES - back)
                sides.append(jnp.where(lane < n, x, jnp.where(lane >= LANES - n, y, 0.0)))
    d0s, d1s, i0s, i1s, r0s, r1s, as_, bs, vs = sides
    x, y = get(rows + half, TILE)
    first = lane_of((TILE, LANES))
    corner = jnp.where(first < s.far, x, jnp.where(first >= LANES - s.far, y, 0.0))
    edge = lane == LANES - 1
    next_side = pltpu.roll(vs, LANES - 1, 1)
    next_own = pltpu.roll(v_ref[:, :LANES], LANES - 1, 1)
    d1 = d_ref[1]
    tail = d1[:, cols - LANES :].astype(F32)
    tail = jnp.where(edge, tail - next_side, tail).astype(BF16)
    d1s = jnp.where(edge, jnp.where(r1s > 0, d1s - next_own, 0.0), d1s).astype(BF16)
    df_ref[0, :, :cols] = d_ref[0]
    df_ref[0, :, cols:] = d0s.astype(BF16)
    df_ref[1, :, : cols - LANES] = d1[:, : cols - LANES]
    df_ref[1, :, cols - LANES : cols] = tail
    df_ref[1, :, cols:] = d1s
    for n, x in enumerate((i0s, i1s, r0s, r1s, as_, bs)):
        t_ref[n] = x.astype(BF16)
    t_ref[6, :TILE, :] = corner.astype(BF16)
    above = lax.rem(lax.axis_index("row"), 2) == 0

    own = (i_ref.at[0], i_ref.at[1], r_ref.at[0], r_ref.at[1], a_ref, b_ref)

    def rows_of(n, start, size):
        if n < 2:
            at = start // TILE * TILE
            x = df_ref[n, at : at + TILE, :].astype(F32)
            return x[start - at : start - at + size]
        source = v_ref if n == 8 else own[n - 2]
        at = start // TILE * TILE
        x = t_ref[n - 2, at : at + TILE, :].astype(F32)
        return jnp.concatenate([source[start : start + size, :], x[start - at : start - at + size]], 1)

    def pack(ref, down):
        at = 0
        dstart = rows - s.up_d if down else 0
        fstart = rows - s.up_f if down else 0
        for c in range(2):
            ref[at : at + s.up_d, :] = df_ref[c, dstart : dstart + s.up_d, :]
            at += s.up_d
        for n, field in enumerate(own):
            ref[at : at + s.up_f, :cols] = field[fstart : fstart + s.up_f, :].astype(BF16)
            ref[at : at + s.up_f, cols:] = t_ref[n, fstart : fstart + s.up_f, :]
            at += s.up_f
        eight = row_of((8, s.lanes))
        halves = [jnp.zeros((8, s.lanes), F32), jnp.zeros((8, s.lanes), F32)]
        for n in range(8):
            width = s.up_d if n < 2 else s.up_f
            slot = 2 * n % 8
            if down:
                x = pltpu.roll(rows_of(n, rows - width - 8, 8), (slot + 2) % 8, 0)
            else:
                x = pltpu.roll(rows_of(n, width, 8), slot, 0)
            keep = (eight == slot) | (eight == slot + 1)
            halves[n // 4] = jnp.where(keep, x, halves[n // 4])
        if not down:
            x = pltpu.roll(rows_of(8, 0, 8), 1, 0)
            halves[0] = jnp.where(eight == 1, x, halves[0])
        ref[at : at + TILE, :] = jnp.concatenate(halves, 0).astype(BF16)

    @pl.when(above)
    def _():
        pack(up_ref, True)
        pack(down_ref, False)

    @pl.when(jnp.logical_not(above))
    def _():
        pack(up_ref, False)
        pack(down_ref, True)


def convolve(d_ref, t_ref, c, s, second=range(3, 11), low=0):
    tiles = s.frame // TILE
    lanes = s.lanes
    first = [t % tiles for t in range(-3, 5)]
    high = 96 - low
    acc = [jnp.zeros((3 * high, 2 * LANES), F32) for _ in range(3)]
    for p in range(s.pairs):
        rhs1, rhs2, rhs3 = [], [], []
        for r in (2 * p, 2 * p + 1):
            shift = (s.half - s.group - r) % lanes if r < s.group else 0
            x = d_ref[c]
            x = pltpu.roll(x, shift, 1) if shift else x
            rhs1 += [x[t * TILE : (t + 1) * TILE, : s.cols] for t in first]
            rhs2 += [x[t * TILE : (t + 1) * TILE, : s.cols] for t in second]
            rhs3 += [jnp.concatenate([x[t * TILE : (t + 1) * TILE, s.cols :], x[u * TILE : (u + 1) * TILE, s.cols :]], 1)
                     for t, u in zip(first, second)]
        lhs = jnp.concatenate([t_ref[c, p, 96 * q + low : 96 * q + 96, :] for q in range(3)], 0)
        for n, rhs in enumerate((rhs1, rhs2, rhs3)):
            acc[n] = acc[n] + jnp.dot(lhs, jnp.concatenate(rhs, 0), preferred_element_type=F32)

    def total(n, start, stop):
        parts = []
        for q in range(3):
            at = slice(high * q + start - low, high * q + stop - low)
            x = jnp.concatenate([acc[n][at], acc[2][at, n * LANES : (n + 1) * LANES]], 1)
            shift = (s.group - s.group * q) % lanes
            parts.append(pltpu.roll(x, shift, 1) if shift else x)
        return parts[0] + parts[1] + parts[2]

    return total


def rolled(x, shift):
    return pltpu.roll(x, shift, 1) if shift else x


def gather(acc, n, high, start, stop, s):
    parts = []
    for q in range(3):
        at = slice(high * q + start, high * q + stop)
        side = acc[2][at, n * LANES : (n + 1) * LANES]
        parts.append(rolled(jnp.concatenate([acc[n][at], side], 1), (s.group - s.group * q) % s.lanes))
    return parts[0] + parts[1] + parts[2]


def middle_kernel(df_ref, i_ref, r_ref, a_ref, b_ref, side_ref, tab_ref, k_ref,
                  if_ref, rf_ref, af_ref, bf_ref, x_ref, bor_ref, z_ref, square_ref, *, s):
    border_tables(k_ref, bor_ref, square_ref, s)
    rows, cols, lanes = s.rows, s.cols, s.lanes
    own = (i_ref.at[0], i_ref.at[1], r_ref.at[0], r_ref.at[1], a_ref, b_ref)
    frames = (if_ref.at[0], if_ref.at[1], rf_ref.at[0], rf_ref.at[1], af_ref, bf_ref)
    for n, (src, dst) in enumerate(zip(own, frames)):
        dst[0:rows, :cols] = src[...]
        dst[0:rows, cols:] = side_ref[n].astype(F32)
    z_ref[...] = df_ref[...]
    end = z_ref[0, rows - TILE :, :]
    z_ref[0, rows - TILE :, :] = jnp.where(row_of(end.shape) == TILE - 1, 0.0, end.astype(F32)).astype(BF16)
    for c in range(2):
        acc = [jnp.zeros((288, cols), F32), None, jnp.zeros((288, LANES), F32)]
        for p in range(s.pairs):
            pieces = []
            for r in (2 * p, 2 * p + 1):
                if r < s.group:
                    x = rolled(z_ref[c], (s.half - s.group - r) % lanes)
                    x_ref[c, r, 0 : 2 * TILE, :] = x[0 : 2 * TILE]
                    x_ref[c, r, 2 * TILE :, :] = x[rows - 2 * TILE :]
                pieces.append(x)
            rhs = jnp.concatenate(pieces, 0)
            acc[0] = acc[0] + jnp.dot(tab_ref[c, p], rhs[:, :cols], preferred_element_type=F32)
            acc[2] = acc[2] + jnp.dot(tab_ref[c, p], rhs[:, cols:], preferred_element_type=F32)
        at = slice(s.half, rows - s.half)
        total = gather(acc, 0, 96, 0, 96, s)
        if_ref[c, at, :] = jnp.where(rf_ref[c, at, :] > 0, if_ref[c, at, :] + total, 0.0)


def border(d_ref, x_ref, e_ref, c, s):
    n = border_rows(c)
    acc = [jnp.zeros((3 * n, 2 * LANES), F32) for _ in range(3)]
    rows, lanes, cols = s.rows, s.lanes, s.cols
    for g in range(s.span3):
        tops, bottoms = [], []
        for at in range(3):
            r = 3 * g + at
            r = r if r < s.group else 0
            shift = (s.half - s.group - r) % lanes
            outer = rolled(d_ref[c, rows : s.frame, :], shift)
            start, stop = x_ref[c, r, 0 : 2 * TILE, :], x_ref[c, r, 2 * TILE :, :]
            if c == 0:
                stop = jnp.concatenate([stop[:TILE], rolled(d_ref[c, rows - TILE : rows, :], shift)], 0)
            top = jnp.concatenate([outer[2 * TILE :], start], 0)
            bottom = jnp.concatenate([stop, outer[: 3 * TILE]], 0)
            tops.append(top)
            bottoms.append(bottom)
        tops.append(tops[0][:TILE])
        bottoms.append(bottoms[0][:TILE])
        top, bottom = jnp.concatenate(tops, 0), jnp.concatenate(bottoms, 0)
        strip = jnp.concatenate([top[:, cols:], bottom[:, cols:]], 1)
        lhs = e_ref[c, g, 0 : 3 * n, :]
        for k, rhs in enumerate((top[:, :cols], bottom[:, :cols], strip)):
            acc[k] = acc[k] + jnp.dot(lhs, rhs, preferred_element_type=F32)
    return [gather(acc, k, n, 0, n, s) for k in range(2)]


def last_kernel(df_ref, v_ref, b_ref, c_ref, e_ref, side_ref, tab_ref, bor_ref, x_ref, one_ref, two_ref,
                if_in, rf_in, af_in, bf_in, vo_hbm, io_hbm, if_ref, rf_ref, af_ref, bf_ref,
                d_ref, vf_ref, vo_ref, io_ref, sems, *, s):
    even = lax.rem(lax.axis_index("row"), 2) == 0
    rows, cols, frame, lanes = s.rows, s.cols, s.frame, s.lanes
    index = lax.axis_index("row")
    low = jnp.where(even, one_ref[...], two_ref[...])
    high = jnp.where(even, two_ref[...], one_ref[...])
    low = jnp.where(index < lax.axis_size("row") - 1, low, jnp.zeros_like(low))
    high = jnp.where(index > 0, high, jnp.zeros_like(high))
    ud, uf, full = s.up_d, s.up_f, s.fields
    tail = 2 * ud + 6 * uf
    low_rest, high_rest = low[tail:, :].astype(F32), high[tail:, :].astype(F32)
    eight = row_of((8, lanes))
    frames = (if_ref.at[0], if_ref.at[1], rf_ref.at[0], rf_ref.at[1], af_ref, bf_ref)
    for n, dst in enumerate(frames):
        at = 2 * ud + n * uf
        half, slot = divmod(4 + 2 * n, 8)
        extra_low = pltpu.roll(low_rest[8 * half : 8 * half + 8], (8 - slot) % 8, 0)
        extra_high = pltpu.roll(high_rest[8 * half : 8 * half + 8], 6 - slot, 0)
        dst[rows : rows + uf, :] = low[at : at + uf, :].astype(F32)
        dst[rows + uf : rows + uf + 8, :] = jnp.where(eight == 0, extra_low, 0.0)
        dst[full - uf - 8 : full - uf, :] = jnp.where(eight >= 6, extra_high, 0.0)
        dst[full - uf : full, :] = high[at : at + uf, :].astype(F32)
    v_next = low_rest[1:2, :]
    v_first = jnp.concatenate([v_ref[0:8, :][0:1, :], side_ref[6, 0:TILE, :].astype(F32)[0:1, :]], 1)
    gap = rows + ud
    shape = (TILE, lanes)
    for c in range(2):
        d_ref[c, 0:rows, :] = df_ref[c]
        d_ref[c, rows:gap, :] = low[c * ud : (c + 1) * ud, :]
        d_ref[c, gap + TILE :, :] = high[c * ud : (c + 1) * ud, :]
        extra_low = pltpu.roll(low_rest[0:8], (8 - 2 * c) % 8, 0)
        extra_high = pltpu.roll(high_rest[0:8], 6 - 2 * c, 0)
        d_ref[c, gap : gap + TILE, :] = jnp.concatenate(
            [jnp.where(eight == 0, extra_low, 0.0), jnp.where(eight >= 6, extra_high, 0.0)], 0).astype(BF16)
    last = row_of(shape) == TILE - 1
    x = d_ref[0, rows - TILE : rows, :].astype(F32)
    d_ref[0, rows - TILE : rows, :] = jnp.where(last, x - v_next, x).astype(BF16)
    x = d_ref[0, frame - TILE :, :].astype(F32)
    inside = rf_ref[0, full - TILE :, :] > 0
    d_ref[0, frame - TILE :, :] = jnp.where(last, jnp.where(inside, x - v_first, 0.0), x).astype(BF16)

    for c in range(2):
        top, bottom = border(d_ref, x_ref, bor_ref, c, s)
        n = border_rows(c)
        pieces = []
        if c == 0:
            pieces.append((rows - 24, jnp.where(eight == 7, jnp.broadcast_to(bottom[0:1], (8, lanes)), 0.0)))
            top, bottom = pltpu.roll(top, n - 1, 0), pltpu.roll(bottom, n - 1, 0)
        pieces += [(full - 24, top[8:32]), (0, top[32:48]), (rows - TILE, bottom[0:40])]
        for dst, add in pieces:
            at = slice(dst, dst + add.shape[0])
            if_ref[c, at, :] = jnp.where(rf_ref[c, at, :] > 0, if_ref[c, at, :] + add, 0.0)
    i0, i1 = if_ref[0], if_ref[1]
    div = i0 - pltpu.roll(i0, 1, 0) + i1 - pltpu.roll(i1, 1, 1)
    volt = af_ref[...] - bf_ref[...] * div
    vf_ref[...] = volt
    drop0 = volt - pltpu.roll(volt, full - 1, 0)
    drop1 = volt - pltpu.roll(volt, lanes - 1, 1)
    r0, r1 = rf_ref[0], rf_ref[1]
    for c, (drop, r, i) in enumerate(((drop0, r0, i0), (drop1, r1, i1))):
        x = jnp.where(r > 0, drop - r * i, 0.0).astype(BF16)
        d_ref[c, 0 : rows + TILE, :] = x[0 : rows + TILE]
        d_ref[c, frame - 2 * TILE :, :] = x[full - 2 * TILE :]

    total = convolve(d_ref, tab_ref, 0, s, range(1, 9), 16)
    above = jnp.where(rf_ref[0, full - 8 :, :] > 0, if_ref[0, full - 8 :, :] + total(0, 24, 32), 0.0)[7:8, :cols]
    for n in range(2):
        at = slice(64 * n, 64 * n + 64)
        io_ref[0, at, :] = (if_ref[0, at, :] + total(n, 32, 96))[:, :cols]
    out0 = pltpu.make_async_copy(io_ref.at[0], io_hbm.at[0], sems.at[0])
    out0.start()
    total = convolve(d_ref, tab_ref, 1, s, range(1, 9), 32)
    ends = jnp.concatenate([total(0, 32, 96), total(1, 32, 96)], 0)
    ends = jnp.where(rf_ref[1, 0:rows, :] > 0, if_ref[1, 0:rows, :] + ends, 0.0)
    io_ref[1] = ends[:, :cols]
    out1 = pltpu.make_async_copy(io_ref.at[1], io_hbm.at[1], sems.at[1])
    out1.start()
    side = ends[:, cols:]
    i0, i1 = io_ref[0], io_ref[1]
    up = jnp.where(row_of((rows, cols)) == 0, above, pltpu.roll(i0, 1, 0))
    left = pltpu.roll(jnp.concatenate([i1, side], 1), 1, 1)[:, :cols]
    div = i0 - up + i1 - left
    vo_ref[...] = c_ref[...] * vf_ref[0:rows, :cols] + e_ref[...] - b_ref[...] * div
    out2 = pltpu.make_async_copy(vo_ref, vo_hbm, sems.at[2])
    out2.start()
    for copy in (out0, out1, out2):
        copy.wait()


def swapped(x, axis, odd):
    sizes = lax.axis_size("row"), lax.axis_size("col")
    main = ("row", "col").index(axis)
    to = {}
    for at in itertools.product(range(sizes[0]), range(sizes[1])):
        along, other = at[main], at[1 - main]
        if along >= odd and (along ^ 1 if not odd else ((along - 1) ^ 1) + 1) < sizes[main]:
            along = along ^ 1 if not odd else ((along - 1) ^ 1) + 1
        elif other ^ 1 < sizes[1 - main]:
            other = other ^ 1
        else:
            continue
        there = (along, other) if main == 0 else (other, along)
        to[at[0] * sizes[1] + at[1]] = there[0] * sizes[1] + there[1]
    return lax.ppermute(x, ("row", "col"), list(to.items()))


def near(x):
    return pltpu.with_memory_space_constraint(x, pltpu.VMEM)


def call(kernel, outs, ins, scratch=(), specs=None, limit=16, out_specs=None, aliases=None):
    return pl.pallas_call(
        kernel,
        compiler_params=pltpu.CompilerParams(vmem_limit_bytes=limit << 20),
        out_shape=outs,
        in_specs=specs or [VMEM] * len(ins),
        out_specs=out_specs or jax.tree.map(lambda _: VMEM, outs),
        scratch_shapes=scratch,
        input_output_aliases=aliases or {},
    )(*ins)


def local(voltage, currents, resistance, inverse_cap, shunt, tap, pad, waveforms, k_window):
    rows, cols = voltage.shape
    s = Sizes(rows, cols, k_window.shape[1], waveforms.shape[1])
    sds = pltpu.VMEM
    k_window = k_window.transpose(1, 0, 2)
    block = sds((rows, cols), F32)
    half = sds((s.edge, LANES), BF16)
    pair = sds((2, rows, cols), F32)
    whole = sds((rows, cols), jnp.int32)
    waveforms = pltpu.with_memory_space_constraint(waveforms, pltpu.HBM)
    one, two, v_near, i_near, r_near, cap_near, shunt_near, tap_near, pad_near, k_near = call(
        functools.partial(first_kernel, s=s),
        (half, half, block, pair, pair, block, block, whole, whole, sds(k_window.shape, BF16)),
        [pltpu.with_memory_space_constraint(x, pltpu.HBM)
         for x in (voltage, currents, resistance, inverse_cap, shunt, tap, pad)]
        + [waveforms, pltpu.with_memory_space_constraint(k_window, pltpu.HBM)],
        specs=[FAR] * 9,
        scratch=[pltpu.SMEM(waveforms.shape, F32), pltpu.SemaphoreType.DMA((9,))])
    square = pltpu.VMEM((LANES, LANES), F32)
    d, a, b, c, e, tables = call(
        functools.partial(own_kernel, s=s),
        (sds((2, rows, cols), BF16), block, block, block, block, sds((2, s.pairs, 288, 2 * LANES), BF16)),
        (v_near, i_near, r_near, cap_near, shunt_near, tap_near, pad_near, k_near, waveforms),
        specs=[VMEM] * 8 + [FAR],
        scratch=[pltpu.SMEM(waveforms.shape, F32), square, pltpu.SemaphoreType.DMA((1,))])
    one, two = near(swapped(one, "col", 0)), near(swapped(two, "col", 1))
    pay = sds((s.payload, s.lanes), BF16)
    df, side, one, two = call(
        functools.partial(second_kernel, s=s),
        (sds((2, rows, s.lanes), BF16), sds((7, rows, LANES), BF16), pay, pay),
        (d, v_near, i_near, r_near, a, b, one, two))
    one, two = swapped(one, "row", 0), swapped(two, "row", 1)
    f = sds((s.fields, s.lanes), F32)
    f2 = sds((2, s.fields, s.lanes), F32)
    i_frame, r_frame, a_frame, b_frame, shifted, borders = call(
        functools.partial(middle_kernel, s=s),
        (f2, f2, f, f, sds((2, s.group, 4 * TILE, s.lanes), BF16),
         sds((2, s.span3, 192, 2 * LANES), BF16)),
        (df, i_near, r_near, a, b, side, tables, k_near),
        scratch=[pltpu.VMEM((2, rows, s.lanes), BF16), square])
    outs = call(
        functools.partial(last_kernel, s=s),
        (jax.ShapeDtypeStruct((rows, cols), F32), jax.ShapeDtypeStruct((2, rows, cols), F32), f2, f2, f, f),
        (df, v_near, b, c, e, side, tables, borders, shifted, near(one), near(two), i_frame, r_frame, a_frame, b_frame),
        scratch=[pltpu.VMEM((2, s.frame, s.lanes), BF16), pltpu.VMEM((s.fields, s.lanes), F32),
                 pltpu.VMEM((rows, cols), F32), pltpu.VMEM((2, rows, cols), F32), pltpu.SemaphoreType.DMA((3,))],
        out_specs=(FAR, FAR, VMEM, VMEM, VMEM, VMEM), aliases={11: 2, 12: 3, 13: 4, 14: 5})
    return outs[0], outs[1]


def solution(mesh):
    grid = P("row", "col")
    pair = P(None, "row", "col")

    return jax.shard_map(
        local,
        mesh=mesh,
        in_specs=(grid, pair, pair, grid, grid, grid, grid, P(), P()),
        out_specs=(grid, pair),
        check_vma=False,
    )
```

time: 23.6 us -> 18.8 us (0.80)
  starting transfers between devices: 8.5 us -> 4.76 us
  waiting for transfers between devices: 6.49 us -> 2.96 us
  Pallas kernels: 7.74 us -> 10.2 us
    ppermute x4, starting transfers between devices: 8.5 us -> 4.76 us  [swapped(): return lax.ppermute(x, ('row', 'col'), list(to.items()))]
    ppermute x4, waiting for transfers between devices: 6.49 us -> 2.96 us  [swapped(): return lax.ppermute(x, ('row', 'col'), list(to.items()))]
    pallas_call x4 -> x5, Pallas kernels: 7.74 us -> 10.2 us  [call(): pl.pallas_call(kernel, compiler_params=pltpu.CompilerParams(vmem_limit_by...]
  transfers between devices with their start and end apart: 4 -> 4, of which waited for: 2 -> 3; matrix products, arithmetic and copies ran while one was open for 0% -> 0% of each run, Pallas kernels for 3% -> 23%
where the time goes in v4:
time: 18.8 us; the launch traced here: 18.6 us
  Pallas kernels  10.2 us (54%)
  starting transfers between devices  4.76 us (25%)
  waiting for transfers between devices  2.96 us (16%)
  between operations  0.67 us (4%)
    pallas_call x5, Pallas kernels, call(): pl.pallas_call(kernel, compiler_params=pltpu.CompilerParams(vmem_limit_by...  10.2 us
    ppermute x4, starting transfers between devices, swapped(): return lax.ppermute(x, ('row', 'col'), list(to.items()))  4.76 us
    ppermute x4, waiting for transfers between devices, swapped(): return lax.ppermute(x, ('row', 'col'), list(to.items()))  2.96 us
  transfers between devices with their start and end apart: 4, of which 3 were waited for; matrix products, arithmetic and copies ran while one was open for 0% of the time, Pallas kernels for 23%

profile of v4, /device:TPU:25, one launch (start us, length us, event | category | flops | bytes accessed | tf_op | source)
XLA Modules:
  0.0 18.6 jit_solution(12523597623080021539)
XLA Ops:
  0.6 1.7 %shard_map.104 = (bf16[208,128]{1,0:T(8,128)(2,1)S(1)}, bf16[208,128]{1,0:T(8,128)(2,1)S(1)}, f32[128,256]{1,0:T(8,128)S(1)}, f32[2,128,256]{2,1,0:T(8,128)S(1)}...) custom-call(f32[128,256]{1,0:T(8,128)} %v_hbm.1, ...), custom_call_target="tpu_custom_call" | custom-call | tf_op jit(solution)/shard_map/pallas_call | solution.py:514
  2.3 1.3 %collective-permute-start = (bf16[208,128]{1,0:T(8,128)(2,1)S(1)}, bf16[208,128]{1,0:T(8,128)(2,1)S(1)}, u32[]{:S(2)}, u32[]{:S(2)}) collective-permute-start(bf16[208,128]{1,0:T(8,128)(2,1)S(1)} %get-tuple-element.41), channel_id=1, source_target_pairs={{0,1},{1,0},{2,3},{3,2},{4,5},{5,4},{6,7},{7,6},{8,9},{9,8},{10,11... | collective-permute-start | bytes 159752 | tf_op jit(solution)/shard_map/ppermute | solution.py:506
  3.6 0.1 collective-permute-start.1
  3.7 1.5 %shard_map.105 = (bf16[2,128,256]{2,1,0:T(8,128)(2,1)S(1)}, f32[128,256]{1,0:T(8,128)S(1)}, f32[128,256]{1,0:T(8,128)S(1)}, f32[128,256]{1,0:T(8,128)S(1)}, f32[...) custom-call(f32[128,256]{1,0:T(8,128)S(1)} %get-tuple-element.30.v_ref, ...), custom_call_target="tpu_custom_call" | custom-call | tf_op jit(solution)/shard_map/pallas_call | solution.py:514
  5.2 0.1 collective-permute-done.one_ref
  5.4 2.1 %collective-permute-done.1.two_ref = bf16[208,128]{1,0:T(8,128)(2,1)S(1)} collective-permute-done((bf16[208,128]{1,0:T(8,128)(2,1)S(1)}, bf16[208,128]{1,0:T(8,128)(2,1)S(1)}, u32[]{:S(2)}, u32[]{:S(2)}) %collective-permute-start.1) | collective-permute-done | bytes 53280 | tf_op jit(solution)/shard_map/ppermute | solution.py:506
  7.5 0.3 %shard_map.106 = (bf16[2,128,384]{2,1,0:T(8,128)(2,1)S(1)}, bf16[7,128,128]{2,1,0:T(8,128)(2,1)S(1)}, bf16[176,384]{1,0:T(8,128)(2,1)S(1)}, bf16[176,384]{1,0:T(8,128)(2,1)S(1)}) custom-call(bf16[2,128,256]{2,1,0:T(8,128)(2,1)S(1)} %get-tuple-element.38.d_ref, f32[128,256]{1,0:T(8,128)S(1)} %get-tuple-element.30.v_ref, ...), custom_call_target="tpu_custom_call" | custom-call | tf_op jit(solution)/shard_map/pallas_call | solution.py:514
  7.9 2.2 %collective-permute-start.2 = (bf16[176,384]{1,0:T(8,128)(2,1)S(1)}, bf16[176,384]{1,0:T(8,128)(2,1)S(1)}, u32[]{:S(2)}, u32[]{:S(2)}) collective-permute-start(bf16[176,384]{1,0:T(8,128)(2,1)S(1)} %get-tuple-element.50), channel_id=1, source_target_pairs={{0,8},{1,9},{2,10},{3,11},{4,12},{5,13},{6,14},{7,15},{8,0},{9,1},... | collective-permute-start | bytes 405512 | tf_op jit(solution)/shard_map/ppermute | solution.py:506
  10.0 1.2 %collective-permute-start.3 = (bf16[176,384]{1,0:T(8,128)(2,1)S(1)}, bf16[176,384]{1,0:T(8,128)(2,1)S(1)}, u32[]{:S(2)}, u32[]{:S(2)}) collective-permute-start(bf16[176,384]{1,0:T(8,128)(2,1)S(1)} %get-tuple-element.51), channel_id=1, source_target_pairs={{0,1},{1,0},{2,3},{3,2},{4,5},{5,4},{6,7},{7,6},{8,16},{9,17},{10,... | collective-permute-start | bytes 405512 | tf_op jit(solution)/shard_map/ppermute | solution.py:506
  11.2 2.8 %shard_map.107 = (f32[2,176,384]{2,1,0:T(8,128)S(1)}, f32[2,176,384]{2,1,0:T(8,128)S(1)}, f32[176,384]{1,0:T(8,128)S(1)}, f32[176,384]{1,0:T(8,128)S(1)}, bf16[2...) custom-call(bf16[2,128,384]{2,1,0:T(8,128)(2,1)S(1)} %get-tuple-element.43.df_ref, ...), custom_call_target="tpu_custom_call" | custom-call | tf_op jit(solution)/shard_map/pallas_call | solution.py:514
  14.0 0.0 collective-permute-done.2.one_ref
  14.0 0.7 %collective-permute-done.3.two_ref = bf16[176,384]{1,0:T(8,128)(2,1)S(1)} collective-permute-done((bf16[176,384]{1,0:T(8,128)(2,1)S(1)}, bf16[176,384]{1,0:T(8,128)(2,1)S(1)}, u32[]{:S(2)}, u32[]{:S(2)}) %collective-permute-start.3) | collective-permute-done | bytes 135200 | tf_op jit(solution)/shard_map/ppermute | solution.py:506
  14.7 3.9 %shard_map.108 = (f32[128,256]{1,0:T(8,128)}, f32[2,128,256]{2,1,0:T(8,128)}, f32[2,176,384]{2,1,0:T(8,128)S(1)}, f32[2,176,384]{2,1,0:T(8,128)S(1)}, f32[176,384]{1,0:T(8,128)S(1)}, /*index=5*/f32[176,384]{1,0:T(8,128)S(1)}) custom-call(bf16[2,128,384]{2,1,0:T(8,128)(2,1)S(1)} %get-tuple-elem, ...), custom_call_target="tpu_custom_call", output_to_operand_aliasing={{2}: (11, {}), {3}: (12, {}), {4}: (13, {}), {5}: (14, {})} | custom-call | tf_op jit(solution)/shard_map/pallas_call | solution.py:514
Async XLA Ops:
  2.3 3.0 %collective-permute-start = (bf16[208,128]{1,0:T(8,128)(2,1)S(1)}, bf16[208,128]{1,0:T(8,128)(2,1)S(1)}, u32[]{:S(2)}, u32[]{:S(2)}) collective-permute-start(bf16[208,128]{1,0:T(8,128)(2,1)S(1)} %get-tuple-element.41), channel_id=1, source_target_pairs={{0,1},{1,0},{2,3},{3,2},{4,5},{5,4},{6,7},{7,6},{8,9},{9,8},{10,11... | collective-permute-start | bytes 159752 | tf_op jit(solution)/shard_map/ppermute | solution.py:506
  3.6 3.9 %collective-permute-start.1 = (bf16[208,128]{1,0:T(8,128)(2,1)S(1)}, bf16[208,128]{1,0:T(8,128)(2,1)S(1)}, u32[]{:S(2)}, u32[]{:S(2)}) collective-permute-start(bf16[208,128]{1,0:T(8,128)(2,1)S(1)} %get-tuple-element.42), channel_id=1, source_target_pairs={{0,8},{1,2},{2,1},{3,4},{4,3},{5,6},{6,5},{7,15},{8,0},{9,10},{10,... | collective-permute-start | bytes 159752 | tf_op jit(solution)/shard_map/ppermute | solution.py:506
  7.9 6.2 %collective-permute-start.2 = (bf16[176,384]{1,0:T(8,128)(2,1)S(1)}, bf16[176,384]{1,0:T(8,128)(2,1)S(1)}, u32[]{:S(2)}, u32[]{:S(2)}) collective-permute-start(bf16[176,384]{1,0:T(8,128)(2,1)S(1)} %get-tuple-element.50), channel_id=1, source_target_pairs={{0,8},{1,9},{2,10},{3,11},{4,12},{5,13},{6,14},{7,15},{8,0},{9,1},... | collective-permute-start | bytes 405512 | tf_op jit(solution)/shard_map/ppermute | solution.py:506
  10.0 4.7 %collective-permute-start.3 = (bf16[176,384]{1,0:T(8,128)(2,1)S(1)}, bf16[176,384]{1,0:T(8,128)(2,1)S(1)}, u32[]{:S(2)}, u32[]{:S(2)}) collective-permute-start(bf16[176,384]{1,0:T(8,128)(2,1)S(1)} %get-tuple-element.51), channel_id=1, source_target_pairs={{0,1},{1,0},{2,3},{3,2},{4,5},{5,4},{6,7},{7,6},{8,16},{9,17},{10,... | collective-permute-start | bytes 405512 | tf_op jit(solution)/shard_map/ppermute | solution.py:506

commit v5 on v4

--- a/solution.py
+++ b/solution.py
@@ -31,7 +31,10 @@
         self.fields = rows + 3 * TILE
         self.up_d = 2 * self.half
         self.up_f = self.half
-        self.payload = 2 * self.up_d + 6 * self.up_f + TILE
+        self.tail = 2 * self.up_d + 6 * self.up_f
+        self.main = self.tail + TILE
+        self.payload = self.main + 3 * TILE
+        self.slide = self.far + self.near
         far, near = self.far, self.near
         self.slots = (
             ((far, 0, 0), (far, far, far), (near, 2 * far, far + near),
@@ -74,47 +77,42 @@
                 t_ref[c, p, q * 96 : (q + 1) * 96, at * LANES : (at + 1) * LANES] = band
 
 
-def border_tables(k_ref, e_ref, pad_ref, s):
+def border_tables(t_ref, e_ref, s):
     window = 5 * TILE
-    blank = jnp.zeros((1, LANES), F32)
+    over = 2 * window - LANES
     for c in range(2):
-        turned = turn(k_ref, pad_ref, c, s)
         n = border_rows(c)
         late = 1 - c
+        lane = lane_of((n, LANES))
         for g in range(s.span3):
             for q in range(3):
-                row = jnp.zeros((1, 2 * LANES), F32)
-                for at in range(3):
-                    r = 3 * g + at
-                    if r < s.group:
-                        b = s.group * q + r
-                        wide = jnp.concatenate([turned[b : b + 1, :], blank], 1)
-                        shift = (window * at - late) % (2 * LANES)
-                        row = row + (pltpu.roll(wide, shift, 1) if shift else wide)
-                row = jnp.broadcast_to(row, (n, 2 * LANES))
-                band = pltpu.roll(row, 0, 1, stride=1, stride_axis=0)
+                def piece(at):
+                    p, half = divmod(3 * g + at, 2)
+                    return t_ref[c, p, 96 * q : 96 * q + n, half * LANES : (half + 1) * LANES]
+
+                first = rolled(piece(0), (-late) % LANES).astype(F32)
+                second = rolled(piece(1), window - late).astype(F32)
+                third = rolled(piece(2), over - late).astype(F32)
+                low = jnp.where(lane < window, first, second)
+                high = jnp.where(lane < over, second, third)
                 if late:
-                    lane = lane_of(band.shape)
-                    kept = lane == s.span - 2
-                    for at in range(1, 3):
-                        kept = kept | (lane == window * at + s.span - 2)
-                    band = jnp.where((row_of(band.shape) > 0) | kept, band, 0.0)
-                e_ref[c, g, q * n : (q + 1) * n, :] = band.astype(BF16)
-
-
-def load_of(tap, wave_ref, step, s):
+                    later = row_of(lane.shape) > 0
+                    last = s.span - 2
+                    low = jnp.where(later | (lane == last) | (lane == last + window), low, 0.0)
+                    high = jnp.where(later | (lane == last + over), high, 0.0)
+                e_ref[c, g, q * n : (q + 1) * n, :LANES] = low.astype(BF16)
+                e_ref[c, g, q * n : (q + 1) * n, LANES:] = high.astype(BF16)
+
+
+def load_of(tap, wave, s):
     total = jnp.zeros(tap.shape, F32)
     for n in range(s.waves):
-        total = jnp.where(tap == n, wave_ref[step, n], total)
+        total = jnp.where(tap == n, wave(n), total)
     return total
 
 
-def border_rows(c):
-    return 64 if c == 0 else 48
-
-
 def first_kernel(v_hbm, i_hbm, r_hbm, cap_hbm, shunt_hbm, tap_hbm, pad_hbm, wave_hbm, k_hbm,
-                 one_ref, two_ref, v_ref, i_ref, r_ref, cap_ref, shunt_ref, tap_ref, pad_ref, k_ref,
+                 one_ref, two_ref, v_ref, i_ref, r_ref, cap_ref, shunt_ref, tap_ref, pad_ref, k_ref, w_ref,
                  wave_ref, sems, *, s):
     sources = (wave_hbm, tap_hbm, pad_hbm, cap_hbm, shunt_hbm, v_hbm, i_hbm, r_hbm, k_hbm)
     targets = (wave_ref, tap_ref, pad_ref, cap_ref, shunt_ref, v_ref, i_ref, r_ref, k_ref)
@@ -131,7 +129,10 @@
 
     for copy in copies[:2]:
         copy.wait()
-    load = load_of(ends(tap_ref), wave_ref, 0, s)
+    load = load_of(ends(tap_ref), lambda n: wave_ref[0, n], s)
+    for step in range(2):
+        for n in range(s.waves):
+            w_ref[step, n : n + 1, :] = jnp.full((1, LANES), wave_ref[step, n], F32)
     for copy in copies[2:5]:
         copy.wait()
     keep = ends(pad_ref) != 1
@@ -176,11 +177,10 @@
     return (lane < off) | (lane >= LANES + off - n)
 
 
-def own_kernel(v_ref, i_ref, r_ref, cap_ref, shunt_ref, tap_ref, pad_ref, k_ref, wave_hbm,
-               d_ref, a_ref, b_ref, c_ref, e_ref, t_ref, wave_ref, square_ref, sem, *, s):
-    copy = pltpu.make_async_copy(wave_hbm, wave_ref, sem.at[0])
-    copy.start()
+def own_kernel(v_ref, i_ref, r_ref, cap_ref, shunt_ref, tap_ref, pad_ref, k_ref, w_ref,
+               d_ref, a_ref, b_ref, c_ref, e_ref, t_ref, bor_ref, square_ref, *, s):
     main_tables(k_ref, t_ref, square_ref, s)
+    border_tables(t_ref, bor_ref, s)
     volt = v_ref[...]
     rows, cols = volt.shape
     below = jnp.where(row_of(volt.shape) == rows - 1, 0.0, pltpu.roll(volt, rows - 1, 0))
@@ -191,9 +191,11 @@
     b = jnp.where(keep, cap_ref[...], 0.0)
     c = jnp.where(keep, 1.0, 0.0) - b * shunt_ref[...]
     b_ref[...], c_ref[...] = b, c
-    copy.wait()
-    a_ref[...] = c * volt + b * load_of(tap_ref[...], wave_ref, 0, s)
-    e_ref[...] = b * load_of(tap_ref[...], wave_ref, 1, s)
+    for at in range(0, cols, LANES):
+        at = slice(at, at + LANES)
+        first, second = [load_of(tap_ref[:, at], lambda n: w_ref[step, n : n + 1, :], s) for step in range(2)]
+        a_ref[:, at] = c[:, at] * volt[:, at] + b[:, at] * first
+        e_ref[:, at] = b[:, at] * second
 
 
 def second_kernel(d_ref, v_ref, i_ref, r_ref, a_ref, b_ref, one_ref, two_ref,
@@ -257,17 +259,30 @@
         x = t_ref[n - 2, at : at + TILE, :].astype(F32)
         return jnp.concatenate([source[start : start + size, :], x[start - at : start - at + size]], 1)
 
+    lane16 = lane_of((TILE, LANES))
+    wide = (lane16 < s.far) | (lane16 >= LANES - s.far)
+
     def pack(ref, down):
         at = 0
         dstart = rows - s.up_d if down else 0
         fstart = rows - s.up_f if down else 0
+
+        def corner(k, x):
+            ref[s.main + k // 2 * TILE : s.main + (k // 2 + 1) * TILE, k % 2 * LANES : (k % 2 + 1) * LANES] = x.astype(BF16)
+
+        def field_side(n):
+            return t_ref[n, fstart : fstart + s.up_f, :].astype(F32)
+
         for c in range(2):
-            ref[at : at + s.up_d, :] = df_ref[c, dstart : dstart + s.up_d, :]
+            ref[at : at + s.up_d, :] = df_ref[c, dstart : dstart + s.up_d, :cols]
             at += s.up_d
-        for n, field in enumerate(own):
-            ref[at : at + s.up_f, :cols] = field[fstart : fstart + s.up_f, :].astype(BF16)
-            ref[at : at + s.up_f, cols:] = t_ref[n, fstart : fstart + s.up_f, :]
+            for h in range(2):
+                x = df_ref[c, dstart + h * TILE : dstart + (h + 1) * TILE, cols:].astype(F32)
+                corner(2 * c + h, jnp.where(wide, x, pltpu.roll(field_side(2 * c + h), s.slide, 1)))
+        for field in own:
+            ref[at : at + s.up_f, :] = field[fstart : fstart + s.up_f, :].astype(BF16)
             at += s.up_f
+        corner(4, jnp.where(wide, field_side(4), pltpu.roll(field_side(5), s.slide, 1)))
         eight = row_of((8, s.lanes))
         halves = [jnp.zeros((8, s.lanes), F32), jnp.zeros((8, s.lanes), F32)]
         for n in range(8):
@@ -282,7 +297,9 @@
         if not down:
             x = pltpu.roll(rows_of(8, 0, 8), 1, 0)
             halves[0] = jnp.where(eight == 1, x, halves[0])
-        ref[at : at + TILE, :] = jnp.concatenate(halves, 0).astype(BF16)
+        extra = jnp.concatenate(halves, 0)
+        ref[at : at + TILE, :] = extra[:, :cols].astype(BF16)
+        corner(5, extra[:, cols:])
 
     @pl.when(above)
     def _():
@@ -340,9 +357,8 @@
     return parts[0] + parts[1] + parts[2]
 
 
-def middle_kernel(df_ref, i_ref, r_ref, a_ref, b_ref, side_ref, tab_ref, k_ref,
-                  if_ref, rf_ref, af_ref, bf_ref, x_ref, bor_ref, z_ref, square_ref, *, s):
-    border_tables(k_ref, bor_ref, square_ref, s)
+def middle_kernel(df_ref, i_ref, r_ref, a_ref, b_ref, side_ref, tab_ref,
+                  if_ref, rf_ref, af_ref, bf_ref, x_ref, z_ref, *, s):
     rows, cols, lanes = s.rows, s.cols, s.lanes
     own = (i_ref.at[0], i_ref.at[1], r_ref.at[0], r_ref.at[1], a_ref, b_ref)
     frames = (if_ref.at[0], if_ref.at[1], rf_ref.at[0], rf_ref.at[1], af_ref, bf_ref)
@@ -409,27 +425,45 @@
     low = jnp.where(index < lax.axis_size("row") - 1, low, jnp.zeros_like(low))
     high = jnp.where(index > 0, high, jnp.zeros_like(high))
     ud, uf, full = s.up_d, s.up_f, s.fields
-    tail = 2 * ud + 6 * uf
-    low_rest, high_rest = low[tail:, :].astype(F32), high[tail:, :].astype(F32)
+    lane = lane_of((TILE, LANES))
+
+    def corner(x, k):
+        return x[s.main + k // 2 * TILE : s.main + (k // 2 + 1) * TILE, k % 2 * LANES : (k % 2 + 1) * LANES].astype(F32)
+
+    def rest(x):
+        return jnp.concatenate([x[s.tail : s.main, :].astype(F32), corner(x, 5)], 1)
+
+    def field(x, n):
+        at = 2 * ud + n * uf
+        side = corner(x, min(n, 4))
+        if n != 4:
+            side = pltpu.roll(side, LANES - s.slide, 1)
+        side = jnp.where((lane < s.near) | (lane >= LANES - s.near), side, 0.0)
+        return jnp.concatenate([x[at : at + uf, :].astype(F32), side], 1)
+
+    def driving(x, c):
+        sides = [jnp.where((lane < s.far) | (lane >= LANES - s.far), corner(x, 2 * c + h), 0.0) for h in range(2)]
+        return jnp.concatenate([x[c * ud : (c + 1) * ud, :], jnp.concatenate(sides, 0).astype(BF16)], 1)
+
+    low_rest, high_rest = rest(low), rest(high)
     eight = row_of((8, lanes))
     frames = (if_ref.at[0], if_ref.at[1], rf_ref.at[0], rf_ref.at[1], af_ref, bf_ref)
     for n, dst in enumerate(frames):
-        at = 2 * ud + n * uf
         half, slot = divmod(4 + 2 * n, 8)
         extra_low = pltpu.roll(low_rest[8 * half : 8 * half + 8], (8 - slot) % 8, 0)
         extra_high = pltpu.roll(high_rest[8 * half : 8 * half + 8], 6 - slot, 0)
-        dst[rows : rows + uf, :] = low[at : at + uf, :].astype(F32)
+        dst[rows : rows + uf, :] = field(low, n)
         dst[rows + uf : rows + uf + 8, :] = jnp.where(eight == 0, extra_low, 0.0)
         dst[full - uf - 8 : full - uf, :] = jnp.where(eight >= 6, extra_high, 0.0)
-        dst[full - uf : full, :] = high[at : at + uf, :].astype(F32)
+        dst[full - uf : full, :] = field(high, n)
     v_next = low_rest[1:2, :]
     v_first = jnp.concatenate([v_ref[0:8, :][0:1, :], side_ref[6, 0:TILE, :].astype(F32)[0:1, :]], 1)
     gap = rows + ud
     shape = (TILE, lanes)
     for c in range(2):
         d_ref[c, 0:rows, :] = df_ref[c]
-        d_ref[c, rows:gap, :] = low[c * ud : (c + 1) * ud, :]
-        d_ref[c, gap + TILE :, :] = high[c * ud : (c + 1) * ud, :]
+        d_ref[c, rows:gap, :] = driving(low, c)
+        d_ref[c, gap + TILE :, :] = driving(high, c)
         extra_low = pltpu.roll(low_rest[0:8], (8 - 2 * c) % 8, 0)
         extra_high = pltpu.roll(high_rest[0:8], 6 - 2 * c, 0)
         d_ref[c, gap : gap + TILE, :] = jnp.concatenate(
@@ -531,24 +565,23 @@
     half = sds((s.edge, LANES), BF16)
     pair = sds((2, rows, cols), F32)
     whole = sds((rows, cols), jnp.int32)
-    waveforms = pltpu.with_memory_space_constraint(waveforms, pltpu.HBM)
-    one, two, v_near, i_near, r_near, cap_near, shunt_near, tap_near, pad_near, k_near = call(
+    one, two, v_near, i_near, r_near, cap_near, shunt_near, tap_near, pad_near, k_near, w_near = call(
         functools.partial(first_kernel, s=s),
-        (half, half, block, pair, pair, block, block, whole, whole, sds(k_window.shape, BF16)),
+        (half, half, block, pair, pair, block, block, whole, whole, sds(k_window.shape, BF16),
+         sds((2, s.waves, LANES), F32)),
         [pltpu.with_memory_space_constraint(x, pltpu.HBM)
-         for x in (voltage, currents, resistance, inverse_cap, shunt, tap, pad)]
-        + [waveforms, pltpu.with_memory_space_constraint(k_window, pltpu.HBM)],
+         for x in (voltage, currents, resistance, inverse_cap, shunt, tap, pad, waveforms, k_window)],
         specs=[FAR] * 9,
         scratch=[pltpu.SMEM(waveforms.shape, F32), pltpu.SemaphoreType.DMA((9,))])
     square = pltpu.VMEM((LANES, LANES), F32)
-    d, a, b, c, e, tables = call(
+    d, a, b, c, e, tables, borders = call(
         functools.partial(own_kernel, s=s),
-        (sds((2, rows, cols), BF16), block, block, block, block, sds((2, s.pairs, 288, 2 * LANES), BF16)),
-        (v_near, i_near, r_near, cap_near, shunt_near, tap_near, pad_near, k_near, waveforms),
-        specs=[VMEM] * 8 + [FAR],
-        scratch=[pltpu.SMEM(waveforms.shape, F32), square, pltpu.SemaphoreType.DMA((1,))])
+        (sds((2, rows, cols), BF16), block, block, block, block, sds((2, s.pairs, 288, 2 * LANES), BF16),
+         sds((2, s.span3, 192, 2 * LANES), BF16)),
+        (v_near, i_near, r_near, cap_near, shunt_near, tap_near, pad_near, k_near, w_near),
+        scratch=[square])
     one, two = near(swapped(one, "col", 0)), near(swapped(two, "col", 1))
-    pay = sds((s.payload, s.lanes), BF16)
+    pay = sds((s.payload, cols), BF16)
     df, side, one, two = call(
         functools.partial(second_kernel, s=s),
         (sds((2, rows, s.lanes), BF16), sds((7, rows, LANES), BF16), pay, pay),
@@ -556,12 +589,11 @@
     one, two = swapped(one, "row", 0), swapped(two, "row", 1)
     f = sds((s.fields, s.lanes), F32)
     f2 = sds((2, s.fields, s.lanes), F32)
-    i_frame, r_frame, a_frame, b_frame, shifted, borders = call(
+    i_frame, r_frame, a_frame, b_frame, shifted = call(
         functools.partial(middle_kernel, s=s),
-        (f2, f2, f, f, sds((2, s.group, 4 * TILE, s.lanes), BF16),
-         sds((2, s.span3, 192, 2 * LANES), BF16)),
-        (df, i_near, r_near, a, b, side, tables, k_near),
-        scratch=[pltpu.VMEM((2, rows, s.lanes), BF16), square])
+        (f2, f2, f, f, sds((2, s.group, 4 * TILE, s.lanes), BF16)),
+        (df, i_near, r_near, a, b, side, tables),
+        scratch=[pltpu.VMEM((2, rows, s.lanes), BF16)])
     outs = call(
         functools.partial(last_kernel, s=s),
         (jax.ShapeDtypeStruct((rows, cols), F32), jax.ShapeDtypeStruct((2, rows, cols), F32), f2, f2, f, f),

time: 18.8 us -> 18.6 us (0.989)
  Pallas kernels: 10.2 us -> 8.25 us
  waiting for transfers between devices: 2.96 us -> 4.72 us
    pallas_call x5, Pallas kernels: 10.2 us -> 8.25 us  [call(): pl.pallas_call(kernel, compiler_params=pltpu.CompilerParams(vmem_limit_by...]
    ppermute x4, waiting for transfers between devices: 2.96 us -> 4.72 us  [swapped(): return lax.ppermute(x, ('row', 'col'), list(to.items()))]
  transfers between devices with their start and end apart: 4 -> 4, of which waited for: 3 -> 3; matrix products, arithmetic and copies ran while one was open for 0% -> 0% of each run, Pallas kernels for 23% -> 13%
where the time goes in v5:
time: 18.6 us; the launch traced here: 18.4 us
  Pallas kernels  8.25 us (44%)
  starting transfers between devices  4.76 us (26%)
  waiting for transfers between devices  4.72 us (25%)
  between operations  0.68 us (4%)
    pallas_call x5, Pallas kernels, call(): pl.pallas_call(kernel, compiler_params=pltpu.CompilerParams(vmem_limit_by...  8.25 us
    ppermute x4, starting transfers between devices, swapped(): return lax.ppermute(x, ('row', 'col'), list(to.items()))  4.76 us
    ppermute x4, waiting for transfers between devices, swapped(): return lax.ppermute(x, ('row', 'col'), list(to.items()))  4.72 us
  transfers between devices with their start and end apart: 4, of which 3 were waited for; matrix products, arithmetic and copies ran while one was open for 0% of the time, Pallas kernels for 13%

profile of v5, /device:TPU:25, one launch (start us, length us, event | category | flops | bytes accessed | tf_op | source)
XLA Modules:
  0.0 18.4 jit_solution(6796314012053009413)
XLA Ops:
  0.6 1.7 %shard_map.104 = (bf16[208,128]{1,0:T(8,128)(2,1)S(1)}, bf16[208,128]{1,0:T(8,128)(2,1)S(1)}, f32[128,256]{1,0:T(8,128)S(1)}, f32[2,128,256]{2,1,0:T(8,128)S(1)}...) custom-call(f32[128,256]{1,0:T(8,128)} %v_hbm.1, ...), custom_call_target="tpu_custom_call" | custom-call | tf_op jit(solution)/shard_map/pallas_call | solution.py:548
  2.3 1.3 %collective-permute-start = (bf16[208,128]{1,0:T(8,128)(2,1)S(1)}, bf16[208,128]{1,0:T(8,128)(2,1)S(1)}, u32[]{:S(2)}, u32[]{:S(2)}) collective-permute-start(bf16[208,128]{1,0:T(8,128)(2,1)S(1)} %get-tuple-element.43), channel_id=1, source_target_pairs={{0,1},{1,0},{2,3},{3,2},{4,5},{5,4},{6,7},{7,6},{8,9},{9,8},{10,11... | collective-permute-start | bytes 159752 | tf_op jit(solution)/shard_map/ppermute | solution.py:540
  3.6 0.1 collective-permute-start.1
  3.7 1.0 %shard_map.105 = (bf16[2,128,256]{2,1,0:T(8,128)(2,1)S(1)}, f32[128,256]{1,0:T(8,128)S(1)}, f32[128,256]{1,0:T(8,128)S(1)}, f32[128,256]{1,0:T(8,128)S(1)}, f32[...) custom-call(f32[128,256]{1,0:T(8,128)S(1)} %get-tuple-element.31.v_ref, ...), custom_call_target="tpu_custom_call" | custom-call | tf_op jit(solution)/shard_map/pallas_call | solution.py:548
  4.8 0.6 %collective-permute-done.one_ref = bf16[208,128]{1,0:T(8,128)(2,1)S(1)} collective-permute-done((bf16[208,128]{1,0:T(8,128)(2,1)S(1)}, bf16[208,128]{1,0:T(8,128)(2,1)S(1)}, u32[]{:S(2)}, u32[]{:S(2)}) %collective-permute-start) | collective-permute-done | bytes 53280 | tf_op jit(solution)/shard_map/ppermute | solution.py:540
  5.4 2.1 %collective-permute-done.1.two_ref = bf16[208,128]{1,0:T(8,128)(2,1)S(1)} collective-permute-done((bf16[208,128]{1,0:T(8,128)(2,1)S(1)}, bf16[208,128]{1,0:T(8,128)(2,1)S(1)}, u32[]{:S(2)}, u32[]{:S(2)}) %collective-permute-start.1) | collective-permute-done | bytes 53280 | tf_op jit(solution)/shard_map/ppermute | solution.py:540
  7.5 0.4 %shard_map.106 = (bf16[2,128,384]{2,1,0:T(8,128)(2,1)S(1)}, bf16[7,128,128]{2,1,0:T(8,128)(2,1)S(1)}, bf16[224,256]{1,0:T(8,128)(2,1)S(1)}, bf16[224,256]{1,0:T(8,128)(2,1)S(1)}) custom-call(bf16[2,128,256]{2,1,0:T(8,128)(2,1)S(1)} %get-tuple-element.40.d_ref, f32[128,256]{1,0:T(8,128)S(1)} %get-tuple-element.31.v_ref, ...), custom_call_target="tpu_custom_call" | custom-call | tf_op jit(solution)/shard_map/pallas_call | solution.py:548
  7.9 2.2 %collective-permute-start.2 = (bf16[224,256]{1,0:T(8,128)(2,1)S(1)}, bf16[224,256]{1,0:T(8,128)(2,1)S(1)}, u32[]{:S(2)}, u32[]{:S(2)}) collective-permute-start(bf16[224,256]{1,0:T(8,128)(2,1)S(1)} %get-tuple-element.52), channel_id=1, source_target_pairs={{0,8},{1,9},{2,10},{3,11},{4,12},{5,13},{6,14},{7,15},{8,0},{9,1},... | collective-permute-start | bytes 344072 | tf_op jit(solution)/shard_map/ppermute | solution.py:540
  10.1 1.2 %collective-permute-start.3 = (bf16[224,256]{1,0:T(8,128)(2,1)S(1)}, bf16[224,256]{1,0:T(8,128)(2,1)S(1)}, u32[]{:S(2)}, u32[]{:S(2)}) collective-permute-start(bf16[224,256]{1,0:T(8,128)(2,1)S(1)} %get-tuple-element.53), channel_id=1, source_target_pairs={{0,1},{1,0},{2,3},{3,2},{4,5},{5,4},{6,7},{7,6},{8,16},{9,17},{10,... | collective-permute-start | bytes 344072 | tf_op jit(solution)/shard_map/ppermute | solution.py:540
  11.3 1.3 %shard_map.107 = (f32[2,176,384]{2,1,0:T(8,128)S(1)}, f32[2,176,384]{2,1,0:T(8,128)S(1)}, f32[176,384]{1,0:T(8,128)S(1)}, f32[176,384]{1,0:T(8,128)S(1)}, bf16[2,11,64,384]{3,2,1,0:T(8,128)(2,1)S(1)}) custom-call(bf16[2,128,384]{2,1,0:T(8,128)(2,1)S(1)} %get-tuple-element.45.df_ref, f32[2,128,256]{2,1,0:T(8,128)S(1)} %get-tuple-element.32.i_ref, ...), custom_call_target="tpu_custom_call" | custom-call | tf_op jit(solution)/shard_map/pallas_call | solution.py:548
  12.6 0.0 collective-permute-done.2.one_ref
  12.6 2.0 %collective-permute-done.3.two_ref = bf16[224,256]{1,0:T(8,128)(2,1)S(1)} collective-permute-done((bf16[224,256]{1,0:T(8,128)(2,1)S(1)}, bf16[224,256]{1,0:T(8,128)(2,1)S(1)}, u32[]{:S(2)}, u32[]{:S(2)}) %collective-permute-start.3) | collective-permute-done | bytes 114720 | tf_op jit(solution)/shard_map/ppermute | solution.py:540
  14.6 3.9 %shard_map.108 = (f32[128,256]{1,0:T(8,128)}, f32[2,128,256]{2,1,0:T(8,128)}, f32[2,176,384]{2,1,0:T(8,128)S(1)}, f32[2,176,384]{2,1,0:T(8,128)S(1)}, f32[176,384]{1,0:T(8,128)S(1)}, /*index=5*/f32[176,384]{1,0:T(8,128)S(1)}) custom-call(bf16[2,128,384]{2,1,0:T(8,128)(2,1)S(1)} %get-tuple-elem, ...), custom_call_target="tpu_custom_call", output_to_operand_aliasing={{2}: (11, {}), {3}: (12, {}), {4}: (13, {}), {5}: (14, {})} | custom-call | tf_op jit(solution)/shard_map/pallas_call | solution.py:548
Async XLA Ops:
  2.3 3.0 %collective-permute-start = (bf16[208,128]{1,0:T(8,128)(2,1)S(1)}, bf16[208,128]{1,0:T(8,128)(2,1)S(1)}, u32[]{:S(2)}, u32[]{:S(2)}) collective-permute-start(bf16[208,128]{1,0:T(8,128)(2,1)S(1)} %get-tuple-element.43), channel_id=1, source_target_pairs={{0,1},{1,0},{2,3},{3,2},{4,5},{5,4},{6,7},{7,6},{8,9},{9,8},{10,11... | collective-permute-start | bytes 159752 | tf_op jit(solution)/shard_map/ppermute | solution.py:540
  3.6 3.9 %collective-permute-start.1 = (bf16[208,128]{1,0:T(8,128)(2,1)S(1)}, bf16[208,128]{1,0:T(8,128)(2,1)S(1)}, u32[]{:S(2)}, u32[]{:S(2)}) collective-permute-start(bf16[208,128]{1,0:T(8,128)(2,1)S(1)} %get-tuple-element.44), channel_id=1, source_target_pairs={{0,8},{1,2},{2,1},{3,4},{4,3},{5,6},{6,5},{7,15},{8,0},{9,10},{10,... | collective-permute-start | bytes 159752 | tf_op jit(solution)/shard_map/ppermute | solution.py:540
  7.9 4.7 %collective-permute-start.2 = (bf16[224,256]{1,0:T(8,128)(2,1)S(1)}, bf16[224,256]{1,0:T(8,128)(2,1)S(1)}, u32[]{:S(2)}, u32[]{:S(2)}) collective-permute-start(bf16[224,256]{1,0:T(8,128)(2,1)S(1)} %get-tuple-element.52), channel_id=1, source_target_pairs={{0,8},{1,9},{2,10},{3,11},{4,12},{5,13},{6,14},{7,15},{8,0},{9,1},... | collective-permute-start | bytes 344072 | tf_op jit(solution)/shard_map/ppermute | solution.py:540
  10.1 4.5 %collective-permute-start.3 = (bf16[224,256]{1,0:T(8,128)(2,1)S(1)}, bf16[224,256]{1,0:T(8,128)(2,1)S(1)}, u32[]{:S(2)}, u32[]{:S(2)}) collective-permute-start(bf16[224,256]{1,0:T(8,128)(2,1)S(1)} %get-tuple-element.53), channel_id=1, source_target_pairs={{0,1},{1,0},{2,3},{3,2},{4,5},{5,4},{6,7},{7,6},{8,16},{9,17},{10,... | collective-permute-start | bytes 344072 | tf_op jit(solution)/shard_map/ppermute | solution.py:540

commit v6 on v5

--- a/solution.py
+++ b/solution.py
@@ -114,8 +114,8 @@
 def first_kernel(v_hbm, i_hbm, r_hbm, cap_hbm, shunt_hbm, tap_hbm, pad_hbm, wave_hbm, k_hbm,
                  one_ref, two_ref, v_ref, i_ref, r_ref, cap_ref, shunt_ref, tap_ref, pad_ref, k_ref, w_ref,
                  wave_ref, sems, *, s):
-    sources = (wave_hbm, tap_hbm, pad_hbm, cap_hbm, shunt_hbm, v_hbm, i_hbm, r_hbm, k_hbm)
-    targets = (wave_ref, tap_ref, pad_ref, cap_ref, shunt_ref, v_ref, i_ref, r_ref, k_ref)
+    sources = (v_hbm, r_hbm, i_hbm, wave_hbm, tap_hbm, pad_hbm, cap_hbm, shunt_hbm, k_hbm)
+    targets = (v_ref, r_ref, i_ref, wave_ref, tap_ref, pad_ref, cap_ref, shunt_ref, k_ref)
     copies = [pltpu.make_async_copy(x, y, sems.at[n]) for n, (x, y) in enumerate(zip(sources, targets))]
     for copy in copies:
         copy.start()
@@ -127,22 +127,9 @@
     def ends(ref):
         return jnp.where(lane < LANES // 2, ref[:, :LANES], ref[:, cols - LANES :])
 
-    for copy in copies[:2]:
-        copy.wait()
-    load = load_of(ends(tap_ref), lambda n: wave_ref[0, n], s)
-    for step in range(2):
-        for n in range(s.waves):
-            w_ref[step, n : n + 1, :] = jnp.full((1, LANES), wave_ref[step, n], F32)
-    for copy in copies[2:5]:
-        copy.wait()
-    keep = ends(pad_ref) != 1
-    b = jnp.where(keep, ends(cap_ref), 0.0)
-    c = jnp.where(keep, 1.0, 0.0) - b * ends(shunt_ref)
-    a = b * load
-    for copy in copies[5:]:
+    for copy in copies[:3]:
         copy.wait()
     volt = ends(v_ref)
-    a = a + c * volt
     i0, i1, r0, r1 = ends(i_ref.at[0]), ends(i_ref.at[1]), ends(r_ref.at[0]), ends(r_ref.at[1])
     below = jnp.where(row == rows - 1, 0.0, pltpu.roll(volt, rows - 1, 0))
     beside = jnp.where(lane == LANES - 1, 0.0, pltpu.roll(volt, LANES - 1, 1))
@@ -155,7 +142,7 @@
         one_ref[at, :] = jnp.where(even, right, left).astype(BF16)
         two_ref[at, :] = jnp.where(even, left, right).astype(BF16)
 
-    for tile, (slots, fields) in enumerate(zip(s.slots, ((d0, d1, i0, i1, r0), (r1, a, b, volt)))):
+    def slotted(slots, fields):
         left = jnp.zeros(shape, F32)
         right = jnp.zeros(shape, F32)
         for (n, off, back), field in zip(slots, fields):
@@ -164,11 +151,24 @@
             if n > 1:
                 x = x if back == off else rolled(field, back)
                 right = jnp.where(before(lane, n, back), x, right)
-        if tile == 1:
-            left = left[:half] + pltpu.roll(left[half:], LANES // 2, 1)
-            right = right[:half] + pltpu.roll(right[half:], LANES // 2, 1)
-        put(tile * rows, left, right)
+        return left, right
+
+    put(0, *slotted(s.slots[0], (d0, d1, i0, i1, r0)))
     put(rows + half, v_ref[:TILE, :LANES], v_ref[:TILE, cols - LANES :])
+    for copy in copies[3:]:
+        copy.wait()
+    for step in range(2):
+        for n in range(s.waves):
+            w_ref[step, n : n + 1, :] = jnp.full((1, LANES), wave_ref[step, n], F32)
+    load = load_of(ends(tap_ref), lambda n: wave_ref[0, n], s)
+    keep = ends(pad_ref) != 1
+    b = jnp.where(keep, ends(cap_ref), 0.0)
+    c = jnp.where(keep, 1.0, 0.0) - b * ends(shunt_ref)
+    volt = ends(v_ref)
+    a = b * load + c * volt
+    folded = [x[:half] + pltpu.roll(x[half:], LANES // 2, 1)
+              for x in slotted(s.slots[1], (ends(r_ref.at[1]), a, b, volt))]
+    put(rows, *folded)
 
 
 def before(lane, n, off):
@@ -312,36 +312,38 @@
         pack(down_ref, True)
 
 
-def convolve(d_ref, t_ref, c, s, second=range(3, 11), low=0):
-    tiles = s.frame // TILE
-    lanes = s.lanes
-    first = [t % tiles for t in range(-3, 5)]
-    high = 96 - low
-    acc = [jnp.zeros((3 * high, 2 * LANES), F32) for _ in range(3)]
-    for p in range(s.pairs):
-        rhs1, rhs2, rhs3 = [], [], []
-        for r in (2 * p, 2 * p + 1):
-            shift = (s.half - s.group - r) % lanes if r < s.group else 0
-            x = d_ref[c]
-            x = pltpu.roll(x, shift, 1) if shift else x
-            rhs1 += [x[t * TILE : (t + 1) * TILE, : s.cols] for t in first]
-            rhs2 += [x[t * TILE : (t + 1) * TILE, : s.cols] for t in second]
-            rhs3 += [jnp.concatenate([x[t * TILE : (t + 1) * TILE, s.cols :], x[u * TILE : (u + 1) * TILE, s.cols :]], 1)
-                     for t, u in zip(first, second)]
-        lhs = jnp.concatenate([t_ref[c, p, 96 * q + low : 96 * q + 96, :] for q in range(3)], 0)
-        for n, rhs in enumerate((rhs1, rhs2, rhs3)):
-            acc[n] = acc[n] + jnp.dot(lhs, jnp.concatenate(rhs, 0), preferred_element_type=F32)
-
-    def total(n, start, stop):
-        parts = []
-        for q in range(3):
-            at = slice(high * q + start - low, high * q + stop - low)
-            x = jnp.concatenate([acc[n][at], acc[2][at, n * LANES : (n + 1) * LANES]], 1)
-            shift = (s.group - s.group * q) % lanes
-            parts.append(pltpu.roll(x, shift, 1) if shift else x)
-        return parts[0] + parts[1] + parts[2]
-
-    return total
+class Convolution:
+    def __init__(self, d_ref, t_ref, c, s, low):
+        self.s, self.high, self.low = s, 96 - low, low
+        self.acc = [jnp.zeros((3 * self.high, 2 * LANES), F32) for _ in range(3)]
+        self.late = []
+        tiles = s.frame // TILE
+        first = [t % tiles for t in range(-3, 5)]
+        second = range(1, 9)
+        for p in range(s.pairs):
+            rhs1, rhs2, rhs3 = [], [], []
+            for r in (2 * p, 2 * p + 1):
+                x = d_ref[c]
+                rhs1.append(d_ref[c, first[0] * TILE : (first[0] + 1) * TILE, : s.cols])
+                x = rolled(x, (s.half - s.group - r) % s.lanes) if r < s.group else x
+                rhs1 += [x[t * TILE : (t + 1) * TILE, : s.cols] for t in first[1:]]
+                rhs2 += [x[t * TILE : (t + 1) * TILE, : s.cols] for t in second]
+                rhs3 += [jnp.concatenate([x[t * TILE : (t + 1) * TILE, s.cols :], x[u * TILE : (u + 1) * TILE, s.cols :]], 1)
+                         for t, u in zip(first, second)]
+            lhs = jnp.concatenate([t_ref[c, p, 96 * q + low : 96 * q + 96, :] for q in range(3)], 0)
+            self.late.append((lhs, rhs2))
+            self.add(2, lhs, rhs3)
+            self.add(0, lhs, rhs1)
+
+    def add(self, n, lhs, rhs):
+        self.acc[n] = self.acc[n] + jnp.dot(lhs, jnp.concatenate(rhs, 0), preferred_element_type=F32)
+
+    def finish(self):
+        for lhs, rhs in self.late:
+            self.add(1, lhs, rhs)
+
+    def total(self, n, start, stop):
+        return gather(self.acc, n, self.high, start - self.low, stop - self.low, self.s)
 
 
 def rolled(x, shift):
@@ -498,28 +500,36 @@
         d_ref[c, 0 : rows + TILE, :] = x[0 : rows + TILE]
         d_ref[c, frame - 2 * TILE :, :] = x[full - 2 * TILE :]
 
-    total = convolve(d_ref, tab_ref, 0, s, range(1, 9), 16)
-    above = jnp.where(rf_ref[0, full - 8 :, :] > 0, if_ref[0, full - 8 :, :] + total(0, 24, 32), 0.0)[7:8, :cols]
-    for n in range(2):
-        at = slice(64 * n, 64 * n + 64)
-        io_ref[0, at, :] = (if_ref[0, at, :] + total(n, 32, 96))[:, :cols]
-    out0 = pltpu.make_async_copy(io_ref.at[0], io_hbm.at[0], sems.at[0])
-    out0.start()
-    total = convolve(d_ref, tab_ref, 1, s, range(1, 9), 32)
-    ends = jnp.concatenate([total(0, 32, 96), total(1, 32, 96)], 0)
-    ends = jnp.where(rf_ref[1, 0:rows, :] > 0, if_ref[1, 0:rows, :] + ends, 0.0)
-    io_ref[1] = ends[:, :cols]
-    out1 = pltpu.make_async_copy(io_ref.at[1], io_hbm.at[1], sems.at[1])
-    out1.start()
-    side = ends[:, cols:]
-    i0, i1 = io_ref[0], io_ref[1]
-    up = jnp.where(row_of((rows, cols)) == 0, above, pltpu.roll(i0, 1, 0))
-    left = pltpu.roll(jnp.concatenate([i1, side], 1), 1, 1)[:, :cols]
-    div = i0 - up + i1 - left
-    vo_ref[...] = c_ref[...] * vf_ref[0:rows, :cols] + e_ref[...] - b_ref[...] * div
-    out2 = pltpu.make_async_copy(vo_ref, vo_hbm, sems.at[2])
-    out2.start()
-    for copy in (out0, out1, out2):
+    copies = []
+
+    def send(src, dst):
+        copies.append(pltpu.make_async_copy(src, dst, sems.at[len(copies)]))
+        copies[-1].start()
+
+    def emit(n, above):
+        size = rows // 2
+        at = slice(size * n, size * n + size)
+        i0 = (if_ref[0, at, :] + parts[0].total(n, 32, 96))[:, :cols]
+        io_ref[0, at, :] = i0
+        send(io_ref.at[0, at], io_hbm.at[0, at])
+        ends = jnp.where(rf_ref[1, at, :] > 0, if_ref[1, at, :] + parts[1].total(n, 32, 96), 0.0)
+        i1 = ends[:, :cols]
+        io_ref[1, at, :] = i1
+        send(io_ref.at[1, at], io_hbm.at[1, at])
+        left = pltpu.roll(ends, 1, 1)[:, :cols]
+        up = jnp.where(row_of(i0.shape) == 0, above, pltpu.roll(i0, 1, 0))
+        div = i0 - up + i1 - left
+        vo_ref[at, :] = c_ref[at, :] * vf_ref[at, :cols] + e_ref[at, :] - b_ref[at, :] * div
+        send(vo_ref.at[at], vo_hbm.at[at])
+
+    parts = [Convolution(d_ref, tab_ref, 0, s, 16), Convolution(d_ref, tab_ref, 1, s, 32)]
+    above = if_ref[0, full - 8 :, :] + parts[0].total(0, 24, 32)
+    above = jnp.where(rf_ref[0, full - 8 :, :] > 0, above, 0.0)[7:8, :cols]
+    parts[0].finish()
+    emit(0, above)
+    parts[1].finish()
+    emit(1, io_ref[0, rows // 2 - 8 : rows // 2, :][7:8])
+    for copy in copies:
         copy.wait()
 
 
@@ -599,7 +609,7 @@
         (jax.ShapeDtypeStruct((rows, cols), F32), jax.ShapeDtypeStruct((2, rows, cols), F32), f2, f2, f, f),
         (df, v_near, b, c, e, side, tables, borders, shifted, near(one), near(two), i_frame, r_frame, a_frame, b_frame),
         scratch=[pltpu.VMEM((2, s.frame, s.lanes), BF16), pltpu.VMEM((s.fields, s.lanes), F32),
-                 pltpu.VMEM((rows, cols), F32), pltpu.VMEM((2, rows, cols), F32), pltpu.SemaphoreType.DMA((3,))],
+                 pltpu.VMEM((rows, cols), F32), pltpu.VMEM((2, rows, cols), F32), pltpu.SemaphoreType.DMA((6,))],
         out_specs=(FAR, FAR, VMEM, VMEM, VMEM, VMEM), aliases={11: 2, 12: 3, 13: 4, 14: 5})
     return outs[0], outs[1]
 

time: 18.6 us -> 18.2 us (0.978)
  Pallas kernels: 8.25 us -> 7.85 us
    pallas_call x5, Pallas kernels: 8.25 us -> 7.85 us  [call(): pl.pallas_call(kernel, compiler_params=pltpu.CompilerParams(vmem_limit_by...]
where the time goes in v6:
time: 18.2 us; the launch traced here: 18 us
  Pallas kernels  7.85 us (43%)
  starting transfers between devices  4.76 us (26%)
  waiting for transfers between devices  4.71 us (26%)
  between operations  0.68 us (4%)
    pallas_call x5, Pallas kernels, call(): pl.pallas_call(kernel, compiler_params=pltpu.CompilerParams(vmem_limit_by...  7.85 us
    ppermute x4, starting transfers between devices, swapped(): return lax.ppermute(x, ('row', 'col'), list(to.items()))  4.76 us
    ppermute x4, waiting for transfers between devices, swapped(): return lax.ppermute(x, ('row', 'col'), list(to.items()))  4.71 us
  transfers between devices with their start and end apart: 4, of which 3 were waited for; matrix products, arithmetic and copies ran while one was open for 0% of the time, Pallas kernels for 13%

profile of v6, /device:TPU:25, one launch (start us, length us, event | category | flops | bytes accessed | tf_op | source)
XLA Modules:
  0.0 18.0 jit_solution(17758819926113525773)
XLA Ops:
  0.6 1.6 %shard_map.104 = (bf16[208,128]{1,0:T(8,128)(2,1)S(1)}, bf16[208,128]{1,0:T(8,128)(2,1)S(1)}, f32[128,256]{1,0:T(8,128)S(1)}, f32[2,128,256]{2,1,0:T(8,128)S(1)}...) custom-call(f32[128,256]{1,0:T(8,128)} %v_hbm.1, ...), custom_call_target="tpu_custom_call" | custom-call | tf_op jit(solution)/shard_map/pallas_call | solution.py:558
  2.2 1.3 %collective-permute-start = (bf16[208,128]{1,0:T(8,128)(2,1)S(1)}, bf16[208,128]{1,0:T(8,128)(2,1)S(1)}, u32[]{:S(2)}, u32[]{:S(2)}) collective-permute-start(bf16[208,128]{1,0:T(8,128)(2,1)S(1)} %get-tuple-element.43), channel_id=1, source_target_pairs={{0,1},{1,0},{2,3},{3,2},{4,5},{5,4},{6,7},{7,6},{8,9},{9,8},{10,11... | collective-permute-start | bytes 159752 | tf_op jit(solution)/shard_map/ppermute | solution.py:550
  3.5 0.1 collective-permute-start.1
  3.6 1.0 %shard_map.105 = (bf16[2,128,256]{2,1,0:T(8,128)(2,1)S(1)}, f32[128,256]{1,0:T(8,128)S(1)}, f32[128,256]{1,0:T(8,128)S(1)}, f32[128,256]{1,0:T(8,128)S(1)}, f32[...) custom-call(f32[128,256]{1,0:T(8,128)S(1)} %get-tuple-element.31.v_ref, ...), custom_call_target="tpu_custom_call" | custom-call | tf_op jit(solution)/shard_map/pallas_call | solution.py:558
  4.7 0.6 %collective-permute-done.one_ref = bf16[208,128]{1,0:T(8,128)(2,1)S(1)} collective-permute-done((bf16[208,128]{1,0:T(8,128)(2,1)S(1)}, bf16[208,128]{1,0:T(8,128)(2,1)S(1)}, u32[]{:S(2)}, u32[]{:S(2)}) %collective-permute-start) | collective-permute-done | bytes 53280 | tf_op jit(solution)/shard_map/ppermute | solution.py:550
  5.3 2.1 %collective-permute-done.1.two_ref = bf16[208,128]{1,0:T(8,128)(2,1)S(1)} collective-permute-done((bf16[208,128]{1,0:T(8,128)(2,1)S(1)}, bf16[208,128]{1,0:T(8,128)(2,1)S(1)}, u32[]{:S(2)}, u32[]{:S(2)}) %collective-permute-start.1) | collective-permute-done | bytes 53280 | tf_op jit(solution)/shard_map/ppermute | solution.py:550
  7.4 0.4 %shard_map.106 = (bf16[2,128,384]{2,1,0:T(8,128)(2,1)S(1)}, bf16[7,128,128]{2,1,0:T(8,128)(2,1)S(1)}, bf16[224,256]{1,0:T(8,128)(2,1)S(1)}, bf16[224,256]{1,0:T(8,128)(2,1)S(1)}) custom-call(bf16[2,128,256]{2,1,0:T(8,128)(2,1)S(1)} %get-tuple-element.40.d_ref, f32[128,256]{1,0:T(8,128)S(1)} %get-tuple-element.31.v_ref, ...), custom_call_target="tpu_custom_call" | custom-call | tf_op jit(solution)/shard_map/pallas_call | solution.py:558
  7.8 2.2 %collective-permute-start.2 = (bf16[224,256]{1,0:T(8,128)(2,1)S(1)}, bf16[224,256]{1,0:T(8,128)(2,1)S(1)}, u32[]{:S(2)}, u32[]{:S(2)}) collective-permute-start(bf16[224,256]{1,0:T(8,128)(2,1)S(1)} %get-tuple-element.52), channel_id=1, source_target_pairs={{0,8},{1,9},{2,10},{3,11},{4,12},{5,13},{6,14},{7,15},{8,0},{9,1},... | collective-permute-start | bytes 344072 | tf_op jit(solution)/shard_map/ppermute | solution.py:550
  10.0 1.2 %collective-permute-start.3 = (bf16[224,256]{1,0:T(8,128)(2,1)S(1)}, bf16[224,256]{1,0:T(8,128)(2,1)S(1)}, u32[]{:S(2)}, u32[]{:S(2)}) collective-permute-start(bf16[224,256]{1,0:T(8,128)(2,1)S(1)} %get-tuple-element.53), channel_id=1, source_target_pairs={{0,1},{1,0},{2,3},{3,2},{4,5},{5,4},{6,7},{7,6},{8,16},{9,17},{10,... | collective-permute-start | bytes 344072 | tf_op jit(solution)/shard_map/ppermute | solution.py:550
  11.1 1.3 %shard_map.107 = (f32[2,176,384]{2,1,0:T(8,128)S(1)}, f32[2,176,384]{2,1,0:T(8,128)S(1)}, f32[176,384]{1,0:T(8,128)S(1)}, f32[176,384]{1,0:T(8,128)S(1)}, bf16[2,11,64,384]{3,2,1,0:T(8,128)(2,1)S(1)}) custom-call(bf16[2,128,384]{2,1,0:T(8,128)(2,1)S(1)} %get-tuple-element.45.df_ref, f32[2,128,256]{2,1,0:T(8,128)S(1)} %get-tuple-element.32.i_ref, ...), custom_call_target="tpu_custom_call" | custom-call | tf_op jit(solution)/shard_map/pallas_call | solution.py:558
  12.5 0.0 collective-permute-done.2.one_ref
  12.5 2.0 %collective-permute-done.3.two_ref = bf16[224,256]{1,0:T(8,128)(2,1)S(1)} collective-permute-done((bf16[224,256]{1,0:T(8,128)(2,1)S(1)}, bf16[224,256]{1,0:T(8,128)(2,1)S(1)}, u32[]{:S(2)}, u32[]{:S(2)}) %collective-permute-start.3) | collective-permute-done | bytes 114720 | tf_op jit(solution)/shard_map/ppermute | solution.py:550
  14.4 3.6 %shard_map.108 = (f32[128,256]{1,0:T(8,128)}, f32[2,128,256]{2,1,0:T(8,128)}, f32[2,176,384]{2,1,0:T(8,128)S(1)}, f32[2,176,384]{2,1,0:T(8,128)S(1)}, f32[176,384]{1,0:T(8,128)S(1)}, /*index=5*/f32[176,384]{1,0:T(8,128)S(1)}) custom-call(bf16[2,128,384]{2,1,0:T(8,128)(2,1)S(1)} %get-tuple-elem, ...), custom_call_target="tpu_custom_call", output_to_operand_aliasing={{2}: (11, {}), {3}: (12, {}), {4}: (13, {}), {5}: (14, {})} | custom-call | tf_op jit(solution)/shard_map/pallas_call | solution.py:558
Async XLA Ops:
  2.2 3.0 %collective-permute-start = (bf16[208,128]{1,0:T(8,128)(2,1)S(1)}, bf16[208,128]{1,0:T(8,128)(2,1)S(1)}, u32[]{:S(2)}, u32[]{:S(2)}) collective-permute-start(bf16[208,128]{1,0:T(8,128)(2,1)S(1)} %get-tuple-element.43), channel_id=1, source_target_pairs={{0,1},{1,0},{2,3},{3,2},{4,5},{5,4},{6,7},{7,6},{8,9},{9,8},{10,11... | collective-permute-start | bytes 159752 | tf_op jit(solution)/shard_map/ppermute | solution.py:550
  3.5 3.9 %collective-permute-start.1 = (bf16[208,128]{1,0:T(8,128)(2,1)S(1)}, bf16[208,128]{1,0:T(8,128)(2,1)S(1)}, u32[]{:S(2)}, u32[]{:S(2)}) collective-permute-start(bf16[208,128]{1,0:T(8,128)(2,1)S(1)} %get-tuple-element.44), channel_id=1, source_target_pairs={{0,8},{1,2},{2,1},{3,4},{4,3},{5,6},{6,5},{7,15},{8,0},{9,10},{10,... | collective-permute-start | bytes 159752 | tf_op jit(solution)/shard_map/ppermute | solution.py:550
  7.8 4.7 %collective-permute-start.2 = (bf16[224,256]{1,0:T(8,128)(2,1)S(1)}, bf16[224,256]{1,0:T(8,128)(2,1)S(1)}, u32[]{:S(2)}, u32[]{:S(2)}) collective-permute-start(bf16[224,256]{1,0:T(8,128)(2,1)S(1)} %get-tuple-element.52), channel_id=1, source_target_pairs={{0,8},{1,9},{2,10},{3,11},{4,12},{5,13},{6,14},{7,15},{8,0},{9,1},... | collective-permute-start | bytes 344072 | tf_op jit(solution)/shard_map/ppermute | solution.py:550
  10.0 4.5 %collective-permute-start.3 = (bf16[224,256]{1,0:T(8,128)(2,1)S(1)}, bf16[224,256]{1,0:T(8,128)(2,1)S(1)}, u32[]{:S(2)}, u32[]{:S(2)}) collective-permute-start(bf16[224,256]{1,0:T(8,128)(2,1)S(1)} %get-tuple-element.53), channel_id=1, source_target_pairs={{0,1},{1,0},{2,3},{3,2},{4,5},{5,4},{6,7},{7,6},{8,16},{9,17},{10,... | collective-permute-start | bytes 344072 | tf_op jit(solution)/shard_map/ppermute | solution.py:550

commit v7 on v6

--- a/solution.py
+++ b/solution.py
@@ -313,7 +313,7 @@
 
 
 class Convolution:
-    def __init__(self, d_ref, t_ref, c, s, low):
+    def __init__(self, d_ref, inner_ref, t_ref, c, s, low):
         self.s, self.high, self.low = s, 96 - low, low
         self.acc = [jnp.zeros((3 * self.high, 2 * LANES), F32) for _ in range(3)]
         self.late = []
@@ -323,13 +323,18 @@
         for p in range(s.pairs):
             rhs1, rhs2, rhs3 = [], [], []
             for r in (2 * p, 2 * p + 1):
-                x = d_ref[c]
-                rhs1.append(d_ref[c, first[0] * TILE : (first[0] + 1) * TILE, : s.cols])
-                x = rolled(x, (s.half - s.group - r) % s.lanes) if r < s.group else x
-                rhs1 += [x[t * TILE : (t + 1) * TILE, : s.cols] for t in first[1:]]
-                rhs2 += [x[t * TILE : (t + 1) * TILE, : s.cols] for t in second]
-                rhs3 += [jnp.concatenate([x[t * TILE : (t + 1) * TILE, s.cols :], x[u * TILE : (u + 1) * TILE, s.cols :]], 1)
-                         for t, u in zip(first, second)]
+                shift = (s.half - s.group - r) % s.lanes if r < s.group else 0
+                x = {}
+                for t in sorted(set(first[1:]) | set(second)):
+                    if 2 <= t < s.rows // TILE - 2:
+                        at = (t - 2) * TILE
+                        x[t] = inner_ref[c, r if r < s.group else 0, at : at + TILE, :]
+                    else:
+                        x[t] = rolled(d_ref[c, t * TILE : (t + 1) * TILE, :], shift)
+                x[first[0]] = d_ref[c, first[0] * TILE : (first[0] + 1) * TILE, :]
+                rhs1 += [x[t][:, : s.cols] for t in first]
+                rhs2 += [x[t][:, : s.cols] for t in second]
+                rhs3 += [jnp.concatenate([x[t][:, s.cols :], x[u][:, s.cols :]], 1) for t, u in zip(first, second)]
             lhs = jnp.concatenate([t_ref[c, p, 96 * q + low : 96 * q + 96, :] for q in range(3)], 0)
             self.late.append((lhs, rhs2))
             self.add(2, lhs, rhs3)
@@ -360,7 +365,7 @@
 
 
 def middle_kernel(df_ref, i_ref, r_ref, a_ref, b_ref, side_ref, tab_ref,
-                  if_ref, rf_ref, af_ref, bf_ref, x_ref, z_ref, *, s):
+                  if_ref, rf_ref, af_ref, bf_ref, x_ref, inner_ref, vm_ref, z_ref, *, s):
     rows, cols, lanes = s.rows, s.cols, s.lanes
     own = (i_ref.at[0], i_ref.at[1], r_ref.at[0], r_ref.at[1], a_ref, b_ref)
     frames = (if_ref.at[0], if_ref.at[1], rf_ref.at[0], rf_ref.at[1], af_ref, bf_ref)
@@ -386,6 +391,23 @@
         at = slice(s.half, rows - s.half)
         total = gather(acc, 0, 96, 0, 96, s)
         if_ref[c, at, :] = jnp.where(rf_ref[c, at, :] > 0, if_ref[c, at, :] + total, 0.0)
+    at = slice(2 * TILE - 8, rows - 2 * TILE + 8)
+    size = rows - 4 * TILE
+    i = [if_ref[c, at, :] for c in range(2)]
+    r = [rf_ref[c, at, :] for c in range(2)]
+    volt, drive = advance(i, r, af_ref[at, :], bf_ref[at, :])
+    vm_ref[...] = volt[8 : 8 + size, :cols]
+    for c in range(2):
+        x = drive[c][8 : 8 + size].astype(BF16)
+        for n in range(s.group):
+            inner_ref[c, n] = rolled(x, (s.half - s.group - n) % lanes)
+
+
+def advance(i, r, a, b):
+    rows, lanes = a.shape
+    volt = a - b * (i[0] - pltpu.roll(i[0], 1, 0) + i[1] - pltpu.roll(i[1], 1, 1))
+    drops = volt - pltpu.roll(volt, rows - 1, 0), volt - pltpu.roll(volt, lanes - 1, 1)
+    return volt, [jnp.where(r[c] > 0, drops[c] - r[c] * i[c], 0.0) for c in range(2)]
 
 
 def border(d_ref, x_ref, e_ref, c, s):
@@ -416,7 +438,8 @@
     return [gather(acc, k, n, 0, n, s) for k in range(2)]
 
 
-def last_kernel(df_ref, v_ref, b_ref, c_ref, e_ref, side_ref, tab_ref, bor_ref, x_ref, one_ref, two_ref,
+def last_kernel(df_ref, v_ref, b_ref, c_ref, e_ref, side_ref, tab_ref, bor_ref, x_ref, inner_ref, vm_ref,
+                one_ref, two_ref,
                 if_in, rf_in, af_in, bf_in, vo_hbm, io_hbm, if_ref, rf_ref, af_ref, bf_ref,
                 d_ref, vf_ref, vo_ref, io_ref, sems, *, s):
     even = lax.rem(lax.axis_index("row"), 2) == 0
@@ -463,7 +486,7 @@
     gap = rows + ud
     shape = (TILE, lanes)
     for c in range(2):
-        d_ref[c, 0:rows, :] = df_ref[c]
+        d_ref[c, rows - TILE : rows, :] = df_ref[c, rows - TILE : rows, :]
         d_ref[c, rows:gap, :] = driving(low, c)
         d_ref[c, gap + TILE :, :] = driving(high, c)
         extra_low = pltpu.roll(low_rest[0:8], (8 - 2 * c) % 8, 0)
@@ -488,17 +511,29 @@
         for dst, add in pieces:
             at = slice(dst, dst + add.shape[0])
             if_ref[c, at, :] = jnp.where(rf_ref[c, at, :] > 0, if_ref[c, at, :] + add, 0.0)
-    i0, i1 = if_ref[0], if_ref[1]
-    div = i0 - pltpu.roll(i0, 1, 0) + i1 - pltpu.roll(i1, 1, 1)
-    volt = af_ref[...] - bf_ref[...] * div
-    vf_ref[...] = volt
-    drop0 = volt - pltpu.roll(volt, full - 1, 0)
-    drop1 = volt - pltpu.roll(volt, lanes - 1, 1)
-    r0, r1 = rf_ref[0], rf_ref[1]
-    for c, (drop, r, i) in enumerate(((drop0, r0, i0), (drop1, r1, i1))):
-        x = jnp.where(r > 0, drop - r * i, 0.0).astype(BF16)
-        d_ref[c, 0 : rows + TILE, :] = x[0 : rows + TILE]
-        d_ref[c, frame - 2 * TILE :, :] = x[full - 2 * TILE :]
+    inset = 2 * TILE
+    vf_ref[inset : rows - inset, :] = vm_ref[...]
+
+    def upper(ref):
+        return jnp.concatenate([ref[full - 24 : full, :], ref[0 : inset + 8, :]], 0)
+
+    def lower(ref):
+        return ref[rows - inset - 8 : rows + 24, :]
+
+    for part in (upper, lower):
+        volt, drive = advance([part(if_ref.at[c]) for c in range(2)], [part(rf_ref.at[c]) for c in range(2)],
+                              part(af_ref), part(bf_ref))
+        if part is upper:
+            vf_ref[0:inset, :] = volt[24 : 24 + inset, :cols]
+        else:
+            vf_ref[rows - inset : rows, :] = volt[8 : 8 + inset, :cols]
+        for c in range(2):
+            if part is upper:
+                x = jnp.concatenate([jnp.zeros((8, lanes), F32), drive[c][: 24 + inset]], 0).astype(BF16)
+                d_ref[c, frame - 2 * TILE :, :] = x[: 2 * TILE]
+                d_ref[c, 0:inset, :] = x[2 * TILE :]
+            else:
+                d_ref[c, rows - inset : rows + TILE, :] = drive[c][8 : 8 + inset + TILE].astype(BF16)
 
     copies = []
 
@@ -519,10 +554,10 @@
         left = pltpu.roll(ends, 1, 1)[:, :cols]
         up = jnp.where(row_of(i0.shape) == 0, above, pltpu.roll(i0, 1, 0))
         div = i0 - up + i1 - left
-        vo_ref[at, :] = c_ref[at, :] * vf_ref[at, :cols] + e_ref[at, :] - b_ref[at, :] * div
+        vo_ref[at, :] = c_ref[at, :] * vf_ref[at, :] + e_ref[at, :] - b_ref[at, :] * div
         send(vo_ref.at[at], vo_hbm.at[at])
 
-    parts = [Convolution(d_ref, tab_ref, 0, s, 16), Convolution(d_ref, tab_ref, 1, s, 32)]
+    parts = [Convolution(d_ref, inner_ref, tab_ref, 0, s, 16), Convolution(d_ref, inner_ref, tab_ref, 1, s, 32)]
     above = if_ref[0, full - 8 :, :] + parts[0].total(0, 24, 32)
     above = jnp.where(rf_ref[0, full - 8 :, :] > 0, above, 0.0)[7:8, :cols]
     parts[0].finish()
@@ -599,18 +634,19 @@
     one, two = swapped(one, "row", 0), swapped(two, "row", 1)
     f = sds((s.fields, s.lanes), F32)
     f2 = sds((2, s.fields, s.lanes), F32)
-    i_frame, r_frame, a_frame, b_frame, shifted = call(
+    i_frame, r_frame, a_frame, b_frame, shifted, inner, v_inner = call(
         functools.partial(middle_kernel, s=s),
-        (f2, f2, f, f, sds((2, s.group, 4 * TILE, s.lanes), BF16)),
+        (f2, f2, f, f, sds((2, s.group, 4 * TILE, s.lanes), BF16),
+         sds((2, s.group, rows - 4 * TILE, s.lanes), BF16), sds((rows - 4 * TILE, cols), F32)),
         (df, i_near, r_near, a, b, side, tables),
         scratch=[pltpu.VMEM((2, rows, s.lanes), BF16)])
     outs = call(
         functools.partial(last_kernel, s=s),
         (jax.ShapeDtypeStruct((rows, cols), F32), jax.ShapeDtypeStruct((2, rows, cols), F32), f2, f2, f, f),
-        (df, v_near, b, c, e, side, tables, borders, shifted, near(one), near(two), i_frame, r_frame, a_frame, b_frame),
-        scratch=[pltpu.VMEM((2, s.frame, s.lanes), BF16), pltpu.VMEM((s.fields, s.lanes), F32),
+        (df, v_near, b, c, e, side, tables, borders, shifted, inner, v_inner, near(one), near(two), i_frame, r_frame, a_frame, b_frame),
+        scratch=[pltpu.VMEM((2, s.frame, s.lanes), BF16), pltpu.VMEM((rows, cols), F32),
                  pltpu.VMEM((rows, cols), F32), pltpu.VMEM((2, rows, cols), F32), pltpu.SemaphoreType.DMA((6,))],
-        out_specs=(FAR, FAR, VMEM, VMEM, VMEM, VMEM), aliases={11: 2, 12: 3, 13: 4, 14: 5})
+        out_specs=(FAR, FAR, VMEM, VMEM, VMEM, VMEM), aliases={13: 2, 14: 3, 15: 4, 16: 5})
     return outs[0], outs[1]
 
 

time: 18.2 us -> 18 us (0.989)
  waiting for transfers between devices: 4.71 us -> 4.32 us
  Pallas kernels: 7.85 us -> 8.11 us
    ppermute x4, waiting for transfers between devices: 4.71 us -> 4.32 us  [swapped(): return lax.ppermute(x, ('row', 'col'), list(to.items()))]
    pallas_call x5, Pallas kernels: 7.85 us -> 8.11 us  [call(): pl.pallas_call(kernel, compiler_params=pltpu.CompilerParams(vmem_limit_by...]
  transfers between devices with their start and end apart: 4 -> 4, of which waited for: 3 -> 3; matrix products, arithmetic and copies ran while one was open for 0% -> 0% of each run, Pallas kernels for 13% -> 15%
where the time goes in v7:
time: 18 us; the launch traced here: 17.9 us
  Pallas kernels  8.11 us (45%)
  starting transfers between devices  4.76 us (26%)
  waiting for transfers between devices  4.32 us (24%)
  between operations  0.67 us (4%)
    pallas_call x5, Pallas kernels, call(): pl.pallas_call(kernel, compiler_params=pltpu.CompilerParams(vmem_limit_by...  8.11 us
    ppermute x4, starting transfers between devices, swapped(): return lax.ppermute(x, ('row', 'col'), list(to.items()))  4.76 us
    ppermute x4, waiting for transfers between devices, swapped(): return lax.ppermute(x, ('row', 'col'), list(to.items()))  4.32 us
  transfers between devices with their start and end apart: 4, of which 3 were waited for; matrix products, arithmetic and copies ran while one was open for 0% of the time, Pallas kernels for 15%

profile of v7, /device:TPU:25, one launch (start us, length us, event | category | flops | bytes accessed | tf_op | source)
XLA Modules:
  0.0 17.9 jit_solution(5552622482643874813)
XLA Ops:
  0.6 1.6 %shard_map.104 = (bf16[208,128]{1,0:T(8,128)(2,1)S(1)}, bf16[208,128]{1,0:T(8,128)(2,1)S(1)}, f32[128,256]{1,0:T(8,128)S(1)}, f32[2,128,256]{2,1,0:T(8,128)S(1)}...) custom-call(f32[128,256]{1,0:T(8,128)} %v_hbm.1, ...), custom_call_target="tpu_custom_call" | custom-call | tf_op jit(solution)/shard_map/pallas_call | solution.py:593
  2.2 1.3 %collective-permute-start = (bf16[208,128]{1,0:T(8,128)(2,1)S(1)}, bf16[208,128]{1,0:T(8,128)(2,1)S(1)}, u32[]{:S(2)}, u32[]{:S(2)}) collective-permute-start(bf16[208,128]{1,0:T(8,128)(2,1)S(1)} %get-tuple-element.45), channel_id=1, source_target_pairs={{0,1},{1,0},{2,3},{3,2},{4,5},{5,4},{6,7},{7,6},{8,9},{9,8},{10,11... | collective-permute-start | bytes 159752 | tf_op jit(solution)/shard_map/ppermute | solution.py:585
  3.5 0.1 collective-permute-start.1
  3.6 1.0 %shard_map.105 = (bf16[2,128,256]{2,1,0:T(8,128)(2,1)S(1)}, f32[128,256]{1,0:T(8,128)S(1)}, f32[128,256]{1,0:T(8,128)S(1)}, f32[128,256]{1,0:T(8,128)S(1)}, f32[...) custom-call(f32[128,256]{1,0:T(8,128)S(1)} %get-tuple-element.33.v_ref, ...), custom_call_target="tpu_custom_call" | custom-call | tf_op jit(solution)/shard_map/pallas_call | solution.py:593
  4.7 0.6 %collective-permute-done.one_ref = bf16[208,128]{1,0:T(8,128)(2,1)S(1)} collective-permute-done((bf16[208,128]{1,0:T(8,128)(2,1)S(1)}, bf16[208,128]{1,0:T(8,128)(2,1)S(1)}, u32[]{:S(2)}, u32[]{:S(2)}) %collective-permute-start) | collective-permute-done | bytes 53280 | tf_op jit(solution)/shard_map/ppermute | solution.py:585
  5.3 2.1 %collective-permute-done.1.two_ref = bf16[208,128]{1,0:T(8,128)(2,1)S(1)} collective-permute-done((bf16[208,128]{1,0:T(8,128)(2,1)S(1)}, bf16[208,128]{1,0:T(8,128)(2,1)S(1)}, u32[]{:S(2)}, u32[]{:S(2)}) %collective-permute-start.1) | collective-permute-done | bytes 53280 | tf_op jit(solution)/shard_map/ppermute | solution.py:585
  7.4 0.4 %shard_map.106 = (bf16[2,128,384]{2,1,0:T(8,128)(2,1)S(1)}, bf16[7,128,128]{2,1,0:T(8,128)(2,1)S(1)}, bf16[224,256]{1,0:T(8,128)(2,1)S(1)}, bf16[224,256]{1,0:T(8,128)(2,1)S(1)}) custom-call(bf16[2,128,256]{2,1,0:T(8,128)(2,1)S(1)} %get-tuple-element.42.d_ref, f32[128,256]{1,0:T(8,128)S(1)} %get-tuple-element.33.v_ref, ...), custom_call_target="tpu_custom_call" | custom-call | tf_op jit(solution)/shard_map/pallas_call | solution.py:593
  7.8 2.2 %collective-permute-start.2 = (bf16[224,256]{1,0:T(8,128)(2,1)S(1)}, bf16[224,256]{1,0:T(8,128)(2,1)S(1)}, u32[]{:S(2)}, u32[]{:S(2)}) collective-permute-start(bf16[224,256]{1,0:T(8,128)(2,1)S(1)} %get-tuple-element.56), channel_id=1, source_target_pairs={{0,8},{1,9},{2,10},{3,11},{4,12},{5,13},{6,14},{7,15},{8,0},{9,1},... | collective-permute-start | bytes 344072 | tf_op jit(solution)/shard_map/ppermute | solution.py:585
  10.0 1.2 %collective-permute-start.3 = (bf16[224,256]{1,0:T(8,128)(2,1)S(1)}, bf16[224,256]{1,0:T(8,128)(2,1)S(1)}, u32[]{:S(2)}, u32[]{:S(2)}) collective-permute-start(bf16[224,256]{1,0:T(8,128)(2,1)S(1)} %get-tuple-element.57), channel_id=1, source_target_pairs={{0,1},{1,0},{2,3},{3,2},{4,5},{5,4},{6,7},{7,6},{8,16},{9,17},{10,... | collective-permute-start | bytes 344072 | tf_op jit(solution)/shard_map/ppermute | solution.py:585
  11.1 1.7 %shard_map.107 = (f32[2,176,384]{2,1,0:T(8,128)S(1)}, f32[2,176,384]{2,1,0:T(8,128)S(1)}, f32[176,384]{1,0:T(8,128)S(1)}, f32[176,384]{1,0:T(8,128)S(1)}, bf16[2...) custom-call(bf16[2,128,384]{2,1,0:T(8,128)(2,1)S(1)} %get-tuple-element.47.df_ref, ...), custom_call_target="tpu_custom_call" | custom-call | tf_op jit(solution)/shard_map/pallas_call | solution.py:593
  12.8 0.0 collective-permute-done.2.one_ref
  12.9 1.6 %collective-permute-done.3.two_ref = bf16[224,256]{1,0:T(8,128)(2,1)S(1)} collective-permute-done((bf16[224,256]{1,0:T(8,128)(2,1)S(1)}, bf16[224,256]{1,0:T(8,128)(2,1)S(1)}, u32[]{:S(2)}, u32[]{:S(2)}) %collective-permute-start.3) | collective-permute-done | bytes 114720 | tf_op jit(solution)/shard_map/ppermute | solution.py:585
  14.4 3.4 %shard_map.108 = (f32[128,256]{1,0:T(8,128)}, f32[2,128,256]{2,1,0:T(8,128)}, f32[2,176,384]{2,1,0:T(8,128)S(1)}, f32[2,176,384]{2,1,0:T(8,128)S(1)}, f32[176,384]{1,0:T(8,128)S(1)}, /*index=5*/f32[176,384]{1,0:T(8,128)S(1)}) custom-call(bf16[2,128,384]{2,1,0:T(8,128)(2,1)S(1)} %get-tuple-elem, ...), custom_call_target="tpu_custom_call", output_to_operand_aliasing={{2}: (13, {}), {3}: (14, {}), {4}: (15, {}), {5}: (16, {})} | custom-call | tf_op jit(solution)/shard_map/pallas_call | solution.py:593
Async XLA Ops:
  2.2 3.0 %collective-permute-start = (bf16[208,128]{1,0:T(8,128)(2,1)S(1)}, bf16[208,128]{1,0:T(8,128)(2,1)S(1)}, u32[]{:S(2)}, u32[]{:S(2)}) collective-permute-start(bf16[208,128]{1,0:T(8,128)(2,1)S(1)} %get-tuple-element.45), channel_id=1, source_target_pairs={{0,1},{1,0},{2,3},{3,2},{4,5},{5,4},{6,7},{7,6},{8,9},{9,8},{10,11... | collective-permute-start | bytes 159752 | tf_op jit(solution)/shard_map/ppermute | solution.py:585
  3.5 3.9 %collective-permute-start.1 = (bf16[208,128]{1,0:T(8,128)(2,1)S(1)}, bf16[208,128]{1,0:T(8,128)(2,1)S(1)}, u32[]{:S(2)}, u32[]{:S(2)}) collective-permute-start(bf16[208,128]{1,0:T(8,128)(2,1)S(1)} %get-tuple-element.46), channel_id=1, source_target_pairs={{0,8},{1,2},{2,1},{3,4},{4,3},{5,6},{6,5},{7,15},{8,0},{9,10},{10,... | collective-permute-start | bytes 159752 | tf_op jit(solution)/shard_map/ppermute | solution.py:585
  7.8 5.1 %collective-permute-start.2 = (bf16[224,256]{1,0:T(8,128)(2,1)S(1)}, bf16[224,256]{1,0:T(8,128)(2,1)S(1)}, u32[]{:S(2)}, u32[]{:S(2)}) collective-permute-start(bf16[224,256]{1,0:T(8,128)(2,1)S(1)} %get-tuple-element.56), channel_id=1, source_target_pairs={{0,8},{1,9},{2,10},{3,11},{4,12},{5,13},{6,14},{7,15},{8,0},{9,1},... | collective-permute-start | bytes 344072 | tf_op jit(solution)/shard_map/ppermute | solution.py:585
  10.0 4.5 %collective-permute-start.3 = (bf16[224,256]{1,0:T(8,128)(2,1)S(1)}, bf16[224,256]{1,0:T(8,128)(2,1)S(1)}, u32[]{:S(2)}, u32[]{:S(2)}) collective-permute-start(bf16[224,256]{1,0:T(8,128)(2,1)S(1)} %get-tuple-element.57), channel_id=1, source_target_pairs={{0,1},{1,0},{2,3},{3,2},{4,5},{5,4},{6,7},{7,6},{8,16},{9,17},{10,... | collective-permute-start | bytes 344072 | tf_op jit(solution)/shard_map/ppermute | solution.py:585

commit v8 on v7

--- a/solution.py
+++ b/solution.py
@@ -28,6 +28,7 @@
         self.group = -(-span // 3)
         self.pairs = (self.group + 1) // 2
         self.span3 = -(-self.group // 3)
+        self.quads = -(-self.group // 4)
         self.fields = rows + 3 * TILE
         self.up_d = 2 * self.half
         self.up_f = self.half
@@ -43,6 +44,9 @@
         )
         self.edge = rows + rows // 2 + TILE
 
+    def turn(self, r):
+        return (self.half - self.group - r) % self.lanes if r < self.group else 0
+
 
 def lane_of(shape):
     return lax.broadcasted_iota(jnp.int32, shape, len(shape) - 1)
@@ -102,6 +106,25 @@
                     high = jnp.where(later | (lane == last + over), high, 0.0)
                 e_ref[c, g, q * n : (q + 1) * n, :LANES] = low.astype(BF16)
                 e_ref[c, g, q * n : (q + 1) * n, LANES:] = high.astype(BF16)
+
+
+def quarter_tables(t_ref, e_ref, start, stop, offset, kept, s):
+    n = stop - start
+    lane = lane_of((n, LANES))
+    half = LANES // 2
+    for c in range(2):
+        for g in range(s.quads):
+            for q in range(3):
+                pieces = []
+                for at in range(4):
+                    p, side = divmod(4 * g + at, 2)
+                    x = t_ref[c, p, 96 * q + start : 96 * q + stop, side * LANES : (side + 1) * LANES]
+                    pieces.append(rolled(x, (half * side - offset) % LANES).astype(F32))
+                for h in range(2):
+                    x = jnp.where(lane < half, pieces[2 * h], pieces[2 * h + 1])
+                    if kept < half:
+                        x = jnp.where((lane < kept) | ((lane >= half) & (lane < half + kept)), x, 0.0)
+                    e_ref[c, g, q * n : (q + 1) * n, h * LANES : (h + 1) * LANES] = x.astype(BF16)
 
 
 def load_of(tap, wave, s):
@@ -178,9 +201,12 @@
 
 
 def own_kernel(v_ref, i_ref, r_ref, cap_ref, shunt_ref, tap_ref, pad_ref, k_ref, w_ref,
-               d_ref, a_ref, b_ref, c_ref, e_ref, t_ref, bor_ref, square_ref, *, s):
+               d_ref, a_ref, b_ref, c_ref, e_ref, t_ref, bor_ref, mid_ref, up_ref, down_ref, square_ref, *, s):
     main_tables(k_ref, t_ref, square_ref, s)
     border_tables(t_ref, bor_ref, s)
+    quarter_tables(t_ref, mid_ref, 0, 96, 32, 64, s)
+    quarter_tables(t_ref, up_ref, 16, 80, 16, 64, s)
+    quarter_tables(t_ref, down_ref, 48, 96, 80, 48, s)
     volt = v_ref[...]
     rows, cols = volt.shape
     below = jnp.where(row_of(volt.shape) == rows - 1, 0.0, pltpu.roll(volt, rows - 1, 0))
@@ -313,42 +339,41 @@
 
 
 class Convolution:
-    def __init__(self, d_ref, inner_ref, t_ref, c, s, low):
-        self.s, self.high, self.low = s, 96 - low, low
-        self.acc = [jnp.zeros((3 * self.high, 2 * LANES), F32) for _ in range(3)]
+    def __init__(self, d_ref, up_ref, down_ref, c, s):
+        self.s, self.c, self.down_ref = s, c, down_ref
+        self.acc = [None] * 4
+        tiles = s.frame // TILE
+        above = [tiles - 2, tiles - 1, 0, 1]
+        last = s.rows // TILE
+        below = [last - 2, last - 1, last, last]
         self.late = []
-        tiles = s.frame // TILE
-        first = [t % tiles for t in range(-3, 5)]
-        second = range(1, 9)
-        for p in range(s.pairs):
-            rhs1, rhs2, rhs3 = [], [], []
-            for r in (2 * p, 2 * p + 1):
-                shift = (s.half - s.group - r) % s.lanes if r < s.group else 0
-                x = {}
-                for t in sorted(set(first[1:]) | set(second)):
-                    if 2 <= t < s.rows // TILE - 2:
-                        at = (t - 2) * TILE
-                        x[t] = inner_ref[c, r if r < s.group else 0, at : at + TILE, :]
-                    else:
-                        x[t] = rolled(d_ref[c, t * TILE : (t + 1) * TILE, :], shift)
-                x[first[0]] = d_ref[c, first[0] * TILE : (first[0] + 1) * TILE, :]
-                rhs1 += [x[t][:, : s.cols] for t in first]
-                rhs2 += [x[t][:, : s.cols] for t in second]
-                rhs3 += [jnp.concatenate([x[t][:, s.cols :], x[u][:, s.cols :]], 1) for t, u in zip(first, second)]
-            lhs = jnp.concatenate([t_ref[c, p, 96 * q + low : 96 * q + 96, :] for q in range(3)], 0)
-            self.late.append((lhs, rhs2))
-            self.add(2, lhs, rhs3)
-            self.add(0, lhs, rhs1)
+        for g in range(s.quads):
+            upper, lower = [], []
+            for at in range(4):
+                shift = s.turn(4 * g + at)
+                upper += [rolled(d_ref[c, t * TILE : (t + 1) * TILE, :], shift) for t in above]
+                x = [rolled(d_ref[c, t * TILE : (t + 1) * TILE, :], shift) for t in below[:3]]
+                lower += x + x[2:]
+            upper, lower = jnp.concatenate(upper, 0), jnp.concatenate(lower, 0)
+            lhs = up_ref[c, g]
+            self.add(0, lhs, upper[:, : s.cols])
+            self.add(1, lhs, upper[:, s.cols :])
+            self.late.append(lower)
 
     def add(self, n, lhs, rhs):
-        self.acc[n] = self.acc[n] + jnp.dot(lhs, jnp.concatenate(rhs, 0), preferred_element_type=F32)
+        x = jnp.dot(lhs, rhs, preferred_element_type=F32)
+        self.acc[n] = x if self.acc[n] is None else self.acc[n] + x
 
     def finish(self):
-        for lhs, rhs in self.late:
-            self.add(1, lhs, rhs)
-
-    def total(self, n, start, stop):
-        return gather(self.acc, n, self.high, start - self.low, stop - self.low, self.s)
+        for g, lower in enumerate(self.late):
+            lhs = self.down_ref[self.c, g]
+            self.add(2, lhs, lower[:, : self.s.cols])
+            self.add(3, lhs, lower[:, self.s.cols :])
+
+    def total(self, n):
+        acc = [self.acc[2 * n], None, self.acc[2 * n + 1]]
+        size = acc[0].shape[0] // 3
+        return gather(acc, 0, size, 0, size, self.s)
 
 
 def rolled(x, shift):
@@ -364,8 +389,8 @@
     return parts[0] + parts[1] + parts[2]
 
 
-def middle_kernel(df_ref, i_ref, r_ref, a_ref, b_ref, side_ref, tab_ref,
-                  if_ref, rf_ref, af_ref, bf_ref, x_ref, inner_ref, vm_ref, z_ref, *, s):
+def middle_kernel(df_ref, i_ref, r_ref, a_ref, b_ref, side_ref, tab_ref, mid_ref,
+                  if_ref, rf_ref, af_ref, bf_ref, x_ref, vm_ref, part_ref, z_ref, *, s):
     rows, cols, lanes = s.rows, s.cols, s.lanes
     own = (i_ref.at[0], i_ref.at[1], r_ref.at[0], r_ref.at[1], a_ref, b_ref)
     frames = (if_ref.at[0], if_ref.at[1], rf_ref.at[0], rf_ref.at[1], af_ref, bf_ref)
@@ -399,8 +424,13 @@
     vm_ref[...] = volt[8 : 8 + size, :cols]
     for c in range(2):
         x = drive[c][8 : 8 + size].astype(BF16)
-        for n in range(s.group):
-            inner_ref[c, n] = rolled(x, (s.half - s.group - n) % lanes)
+        acc = [jnp.zeros((288, cols), F32), None, jnp.zeros((288, LANES), F32)]
+        for g in range(s.quads):
+            pieces = [rolled(x, s.turn(4 * g + at)) for at in range(4)]
+            rhs = jnp.concatenate(pieces, 0)
+            acc[0] = acc[0] + jnp.dot(mid_ref[c, g], rhs[:, :cols], preferred_element_type=F32)
+            acc[2] = acc[2] + jnp.dot(mid_ref[c, g], rhs[:, cols:], preferred_element_type=F32)
+        part_ref[c] = gather(acc, 0, 96, 0, 96, s)
 
 
 def advance(i, r, a, b):
@@ -438,7 +468,7 @@
     return [gather(acc, k, n, 0, n, s) for k in range(2)]
 
 
-def last_kernel(df_ref, v_ref, b_ref, c_ref, e_ref, side_ref, tab_ref, bor_ref, x_ref, inner_ref, vm_ref,
+def last_kernel(df_ref, v_ref, b_ref, c_ref, e_ref, side_ref, up_ref, down_ref, bor_ref, x_ref, vm_ref, part_ref,
                 one_ref, two_ref,
                 if_in, rf_in, af_in, bf_in, vo_hbm, io_hbm, if_ref, rf_ref, af_ref, bf_ref,
                 d_ref, vf_ref, vo_ref, io_ref, sems, *, s):
@@ -541,13 +571,13 @@
         copies.append(pltpu.make_async_copy(src, dst, sems.at[len(copies)]))
         copies[-1].start()
 
-    def emit(n, above):
+    def emit(n, above, adds):
         size = rows // 2
         at = slice(size * n, size * n + size)
-        i0 = (if_ref[0, at, :] + parts[0].total(n, 32, 96))[:, :cols]
+        i0 = (if_ref[0, at, :] + adds[0])[:, :cols]
         io_ref[0, at, :] = i0
         send(io_ref.at[0, at], io_hbm.at[0, at])
-        ends = jnp.where(rf_ref[1, at, :] > 0, if_ref[1, at, :] + parts[1].total(n, 32, 96), 0.0)
+        ends = jnp.where(rf_ref[1, at, :] > 0, if_ref[1, at, :] + adds[1], 0.0)
         i1 = ends[:, :cols]
         io_ref[1, at, :] = i1
         send(io_ref.at[1, at], io_hbm.at[1, at])
@@ -557,13 +587,18 @@
         vo_ref[at, :] = c_ref[at, :] * vf_ref[at, :] + e_ref[at, :] - b_ref[at, :] * div
         send(vo_ref.at[at], vo_hbm.at[at])
 
-    parts = [Convolution(d_ref, inner_ref, tab_ref, 0, s, 16), Convolution(d_ref, inner_ref, tab_ref, 1, s, 32)]
-    above = if_ref[0, full - 8 :, :] + parts[0].total(0, 24, 32)
+    parts = [Convolution(d_ref, up_ref, down_ref, c, s) for c in range(2)]
+    tops = [part.total(0) for part in parts]
+    above = if_ref[0, full - 8 :, :] + tops[0][8:16]
     above = jnp.where(rf_ref[0, full - 8 :, :] > 0, above, 0.0)[7:8, :cols]
     parts[0].finish()
-    emit(0, above)
+    emit(0, above, [jnp.concatenate([tops[c][16:32], tops[c][32:64] + part_ref[c, 0:32, :], part_ref[c, 32:48, :]], 0)
+                    for c in range(2)])
     parts[1].finish()
-    emit(1, io_ref[0, rows // 2 - 8 : rows // 2, :][7:8])
+    ends = [part.total(1) for part in parts]
+    emit(1, io_ref[0, rows // 2 - 8 : rows // 2, :][7:8],
+         [jnp.concatenate([part_ref[c, 48:64, :], part_ref[c, 64:96, :] + ends[c][0:32], ends[c][32:48]], 0)
+          for c in range(2)])
     for copy in copies:
         copy.wait()
 
@@ -619,10 +654,10 @@
         specs=[FAR] * 9,
         scratch=[pltpu.SMEM(waveforms.shape, F32), pltpu.SemaphoreType.DMA((9,))])
     square = pltpu.VMEM((LANES, LANES), F32)
-    d, a, b, c, e, tables, borders = call(
+    d, a, b, c, e, tables, borders, mids, uppers, lowers = call(
         functools.partial(own_kernel, s=s),
         (sds((2, rows, cols), BF16), block, block, block, block, sds((2, s.pairs, 288, 2 * LANES), BF16),
-         sds((2, s.span3, 192, 2 * LANES), BF16)),
+         sds((2, s.span3, 192, 2 * LANES), BF16), *[sds((2, s.quads, 3 * n, 2 * LANES), BF16) for n in (96, 64, 48)]),
         (v_near, i_near, r_near, cap_near, shunt_near, tap_near, pad_near, k_near, w_near),
         scratch=[square])
     one, two = near(swapped(one, "col", 0)), near(swapped(two, "col", 1))
@@ -634,19 +669,19 @@
     one, two = swapped(one, "row", 0), swapped(two, "row", 1)
     f = sds((s.fields, s.lanes), F32)
     f2 = sds((2, s.fields, s.lanes), F32)
-    i_frame, r_frame, a_frame, b_frame, shifted, inner, v_inner = call(
+    i_frame, r_frame, a_frame, b_frame, shifted, v_inner, partial = call(
         functools.partial(middle_kernel, s=s),
         (f2, f2, f, f, sds((2, s.group, 4 * TILE, s.lanes), BF16),
-         sds((2, s.group, rows - 4 * TILE, s.lanes), BF16), sds((rows - 4 * TILE, cols), F32)),
-        (df, i_near, r_near, a, b, side, tables),
+         sds((rows - 4 * TILE, cols), F32), sds((2, 96, s.lanes), F32)),
+        (df, i_near, r_near, a, b, side, tables, mids),
         scratch=[pltpu.VMEM((2, rows, s.lanes), BF16)])
     outs = call(
         functools.partial(last_kernel, s=s),
         (jax.ShapeDtypeStruct((rows, cols), F32), jax.ShapeDtypeStruct((2, rows, cols), F32), f2, f2, f, f),
-        (df, v_near, b, c, e, side, tables, borders, shifted, inner, v_inner, near(one), near(two), i_frame, r_frame, a_frame, b_frame),
+        (df, v_near, b, c, e, side, uppers, lowers, borders, shifted, v_inner, partial, near(one), near(two), i_frame, r_frame, a_frame, b_frame),
         scratch=[pltpu.VMEM((2, s.frame, s.lanes), BF16), pltpu.VMEM((rows, cols), F32),
                  pltpu.VMEM((rows, cols), F32), pltpu.VMEM((2, rows, cols), F32), pltpu.SemaphoreType.DMA((6,))],
-        out_specs=(FAR, FAR, VMEM, VMEM, VMEM, VMEM), aliases={13: 2, 14: 3, 15: 4, 16: 5})
+        out_specs=(FAR, FAR, VMEM, VMEM, VMEM, VMEM), aliases={14: 2, 15: 3, 16: 4, 17: 5})
     return outs[0], outs[1]
 
 

time: 18 us -> 17.6 us (0.978)
  waiting for transfers between devices: 4.32 us -> 2.87 us
  Pallas kernels: 8.11 us -> 9.16 us
    ppermute x4, waiting for transfers between devices: 4.32 us -> 2.87 us  [swapped(): return lax.ppermute(x, ('row', 'col'), list(to.items()))]
    pallas_call x5, Pallas kernels: 8.11 us -> 9.16 us  [call(): pl.pallas_call(kernel, compiler_params=pltpu.CompilerParams(vmem_limit_by...]
  transfers between devices with their start and end apart: 4 -> 4, of which waited for: 3 -> 2; matrix products, arithmetic and copies ran while one was open for 0% -> 0% of each run, Pallas kernels for 15% -> 24%
where the time goes in v8:
time: 17.6 us; the launch traced here: 17.5 us
  Pallas kernels  9.16 us (52%)
  starting transfers between devices  4.76 us (27%)
  waiting for transfers between devices  2.87 us (16%)
  between operations  0.68 us (4%)
    pallas_call x5, Pallas kernels, call(): pl.pallas_call(kernel, compiler_params=pltpu.CompilerParams(vmem_limit_by...  9.16 us
    ppermute x4, starting transfers between devices, swapped(): return lax.ppermute(x, ('row', 'col'), list(to.items()))  4.76 us
    ppermute x4, waiting for transfers between devices, swapped(): return lax.ppermute(x, ('row', 'col'), list(to.items()))  2.87 us
  transfers between devices with their start and end apart: 4, of which 2 were waited for; matrix products, arithmetic and copies ran while one was open for 0% of the time, Pallas kernels for 24%

profile of v8, /device:TPU:25, one launch (start us, length us, event | category | flops | bytes accessed | tf_op | source)
XLA Modules:
  0.0 17.5 jit_solution(4700001451052982984)
XLA Ops:
  0.6 1.6 %shard_map.104 = (bf16[208,128]{1,0:T(8,128)(2,1)S(1)}, bf16[208,128]{1,0:T(8,128)(2,1)S(1)}, f32[128,256]{1,0:T(8,128)S(1)}, f32[2,128,256]{2,1,0:T(8,128)S(1)}...) custom-call(f32[128,256]{1,0:T(8,128)} %v_hbm.1, ...), custom_call_target="tpu_custom_call" | custom-call | tf_op jit(solution)/shard_map/pallas_call | solution.py:628
  2.2 1.3 %collective-permute-start = (bf16[208,128]{1,0:T(8,128)(2,1)S(1)}, bf16[208,128]{1,0:T(8,128)(2,1)S(1)}, u32[]{:S(2)}, u32[]{:S(2)}) collective-permute-start(bf16[208,128]{1,0:T(8,128)(2,1)S(1)} %get-tuple-element.48), channel_id=1, source_target_pairs={{0,1},{1,0},{2,3},{3,2},{4,5},{5,4},{6,7},{7,6},{8,9},{9,8},{10,11... | collective-permute-start | bytes 159752 | tf_op jit(solution)/shard_map/ppermute | solution.py:620
  3.5 0.1 collective-permute-start.1
  3.6 2.0 %shard_map.105 = (bf16[2,128,256]{2,1,0:T(8,128)(2,1)S(1)}, f32[128,256]{1,0:T(8,128)S(1)}, f32[128,256]{1,0:T(8,128)S(1)}, f32[128,256]{1,0:T(8,128)S(1)}, f32[...) custom-call(f32[128,256]{1,0:T(8,128)S(1)} %get-tuple-element.36.v_r, ...), custom_call_target="tpu_custom_call" | custom-call | tf_op jit(solution)/shard_map/pallas_call | solution.py:628
  5.7 0.0 collective-permute-done.one_ref
  5.7 1.7 %collective-permute-done.1.two_ref = bf16[208,128]{1,0:T(8,128)(2,1)S(1)} collective-permute-done((bf16[208,128]{1,0:T(8,128)(2,1)S(1)}, bf16[208,128]{1,0:T(8,128)(2,1)S(1)}, u32[]{:S(2)}, u32[]{:S(2)}) %collective-permute-start.1) | collective-permute-done | bytes 53280 | tf_op jit(solution)/shard_map/ppermute | solution.py:620
  7.4 0.4 %shard_map.106 = (bf16[2,128,384]{2,1,0:T(8,128)(2,1)S(1)}, bf16[7,128,128]{2,1,0:T(8,128)(2,1)S(1)}, bf16[224,256]{1,0:T(8,128)(2,1)S(1)}, bf16[224,256]{1,0:T(8,128)(2,1)S(1)}) custom-call(bf16[2,128,256]{2,1,0:T(8,128)(2,1)S(1)} %get-tuple-element.45.d_ref, f32[128,256]{1,0:T(8,128)S(1)} %get-tuple-element.36.v_ref, ...), custom_call_target="tpu_custom_call" | custom-call | tf_op jit(solution)/shard_map/pallas_call | solution.py:628
  7.8 2.2 %collective-permute-start.2 = (bf16[224,256]{1,0:T(8,128)(2,1)S(1)}, bf16[224,256]{1,0:T(8,128)(2,1)S(1)}, u32[]{:S(2)}, u32[]{:S(2)}) collective-permute-start(bf16[224,256]{1,0:T(8,128)(2,1)S(1)} %get-tuple-element.62), channel_id=1, source_target_pairs={{0,8},{1,9},{2,10},{3,11},{4,12},{5,13},{6,14},{7,15},{8,0},{9,1},... | collective-permute-start | bytes 344072 | tf_op jit(solution)/shard_map/ppermute | solution.py:620
  10.0 1.2 %collective-permute-start.3 = (bf16[224,256]{1,0:T(8,128)(2,1)S(1)}, bf16[224,256]{1,0:T(8,128)(2,1)S(1)}, u32[]{:S(2)}, u32[]{:S(2)}) collective-permute-start(bf16[224,256]{1,0:T(8,128)(2,1)S(1)} %get-tuple-element.63), channel_id=1, source_target_pairs={{0,1},{1,0},{2,3},{3,2},{4,5},{5,4},{6,7},{7,6},{8,16},{9,17},{10,... | collective-permute-start | bytes 344072 | tf_op jit(solution)/shard_map/ppermute | solution.py:620
  11.1 2.2 %shard_map.107 = (f32[2,176,384]{2,1,0:T(8,128)S(1)}, f32[2,176,384]{2,1,0:T(8,128)S(1)}, f32[176,384]{1,0:T(8,128)S(1)}, f32[176,384]{1,0:T(8,128)S(1)}, bf16[2...) custom-call(bf16[2,128,384]{2,1,0:T(8,128)(2,1)S(1)} %get-tuple-element.50.df_ref, ...), custom_call_target="tpu_custom_call" | custom-call | tf_op jit(solution)/shard_map/pallas_call | solution.py:628
  13.3 0.0 collective-permute-done.2.one_ref
  13.3 1.1 %collective-permute-done.3.two_ref = bf16[224,256]{1,0:T(8,128)(2,1)S(1)} collective-permute-done((bf16[224,256]{1,0:T(8,128)(2,1)S(1)}, bf16[224,256]{1,0:T(8,128)(2,1)S(1)}, u32[]{:S(2)}, u32[]{:S(2)}) %collective-permute-start.3) | collective-permute-done | bytes 114720 | tf_op jit(solution)/shard_map/ppermute | solution.py:620
  14.4 3.0 %shard_map.108 = (f32[128,256]{1,0:T(8,128)}, f32[2,128,256]{2,1,0:T(8,128)}, f32[2,176,384]{2,1,0:T(8,128)S(1)}, f32[2,176,384]{2,1,0:T(8,128)S(1)}, f32[176,384]{1,0:T(8,128)S(1)}, /*index=5*/f32[176,384]{1,0:T(8,128)S(1)}) custom-call(bf16[2,128,384]{2,1,0:T(8,128)(2,1)S(1)} %get-tuple-elem, ...), custom_call_target="tpu_custom_call", output_to_operand_aliasing={{2}: (14, {}), {3}: (15, {}), {4}: (16, {}), {5}: (17, {})} | custom-call | tf_op jit(solution)/shard_map/pallas_call | solution.py:628
Async XLA Ops:
  2.2 3.4 %collective-permute-start = (bf16[208,128]{1,0:T(8,128)(2,1)S(1)}, bf16[208,128]{1,0:T(8,128)(2,1)S(1)}, u32[]{:S(2)}, u32[]{:S(2)}) collective-permute-start(bf16[208,128]{1,0:T(8,128)(2,1)S(1)} %get-tuple-element.48), channel_id=1, source_target_pairs={{0,1},{1,0},{2,3},{3,2},{4,5},{5,4},{6,7},{7,6},{8,9},{9,8},{10,11... | collective-permute-start | bytes 159752 | tf_op jit(solution)/shard_map/ppermute | solution.py:620
  3.5 3.9 %collective-permute-start.1 = (bf16[208,128]{1,0:T(8,128)(2,1)S(1)}, bf16[208,128]{1,0:T(8,128)(2,1)S(1)}, u32[]{:S(2)}, u32[]{:S(2)}) collective-permute-start(bf16[208,128]{1,0:T(8,128)(2,1)S(1)} %get-tuple-element.49), channel_id=1, source_target_pairs={{0,8},{1,2},{2,1},{3,4},{4,3},{5,6},{6,5},{7,15},{8,0},{9,10},{10,... | collective-permute-start | bytes 159752 | tf_op jit(solution)/shard_map/ppermute | solution.py:620
  7.8 5.5 %collective-permute-start.2 = (bf16[224,256]{1,0:T(8,128)(2,1)S(1)}, bf16[224,256]{1,0:T(8,128)(2,1)S(1)}, u32[]{:S(2)}, u32[]{:S(2)}) collective-permute-start(bf16[224,256]{1,0:T(8,128)(2,1)S(1)} %get-tuple-element.62), channel_id=1, source_target_pairs={{0,8},{1,9},{2,10},{3,11},{4,12},{5,13},{6,14},{7,15},{8,0},{9,1},... | collective-permute-start | bytes 344072 | tf_op jit(solution)/shard_map/ppermute | solution.py:620
  10.0 4.5 %collective-permute-start.3 = (bf16[224,256]{1,0:T(8,128)(2,1)S(1)}, bf16[224,256]{1,0:T(8,128)(2,1)S(1)}, u32[]{:S(2)}, u32[]{:S(2)}) collective-permute-start(bf16[224,256]{1,0:T(8,128)(2,1)S(1)} %get-tuple-element.63), channel_id=1, source_target_pairs={{0,1},{1,0},{2,3},{3,2},{4,5},{5,4},{6,7},{7,6},{8,16},{9,17},{10,... | collective-permute-start | bytes 344072 | tf_op jit(solution)/shard_map/ppermute | solution.py:620

commit v9 on v8

--- a/solution.py
+++ b/solution.py
@@ -21,6 +21,7 @@
     def __init__(self, rows, cols, span, waves):
         self.rows, self.cols, self.span, self.waves = rows, cols, span, waves
         self.half = (span - 1) // 2
+        assert rows == LANES and self.half == TILE and cols % LANES == 0
         self.far = 2 * self.half + 2
         self.near = self.half + 2
         self.lanes = cols + LANES
@@ -611,7 +612,9 @@
         along, other = at[main], at[1 - main]
         if along >= odd and (along ^ 1 if not odd else ((along - 1) ^ 1) + 1) < sizes[main]:
             along = along ^ 1 if not odd else ((along - 1) ^ 1) + 1
-        elif other ^ 1 < sizes[1 - main]:
+        elif main == 0 and other ^ 2 < sizes[1]:
+            other = other ^ 2
+        elif main == 1 and other ^ 1 < sizes[0]:
             other = other ^ 1
         else:
             continue

time: 17.6 us -> 18.4 us (1.045)
  the two profiles are of different devices: /device:TPU:25 before, /device:TPU:0 now
where the time goes in v9:
time: 18.4 us; the launch traced here: 18.2 us
  Pallas kernels  9.16 us (50%)
  starting transfers between devices  7.68 us (42%)
  waiting for transfers between devices  0.72 us (4%)
  between operations  0.68 us (4%)
    pallas_call x5, Pallas kernels, call(): pl.pallas_call(kernel, compiler_params=pltpu.CompilerParams(vmem_limit_by...  9.16 us
    ppermute x4, starting transfers between devices, swapped(): return lax.ppermute(x, ('row', 'col'), list(to.items()))  7.68 us
    ppermute x4, waiting for transfers between devices, swapped(): return lax.ppermute(x, ('row', 'col'), list(to.items()))  0.72 us
  transfers between devices with their start and end apart: 4, of which 2 were waited for; matrix products, arithmetic and copies ran while one was open for 0% of the time, Pallas kernels for 23%

profile of v9, /device:TPU:0, one launch (start us, length us, event | category | flops | bytes accessed | tf_op | source)
XLA Modules:
  0.0 18.2 jit_solution(8409944158575430997)
XLA Ops:
  0.6 1.6 %shard_map.104 = (bf16[208,128]{1,0:T(8,128)(2,1)S(1)}, bf16[208,128]{1,0:T(8,128)(2,1)S(1)}, f32[128,256]{1,0:T(8,128)S(1)}, f32[2,128,256]{2,1,0:T(8,128)S(1)}...) custom-call(f32[128,256]{1,0:T(8,128)} %v_hbm.1, ...), custom_call_target="tpu_custom_call" | custom-call | tf_op jit(solution)/shard_map/pallas_call | solution.py:631
  2.2 3.1 %collective-permute-start = (bf16[208,128]{1,0:T(8,128)(2,1)S(1)}, bf16[208,128]{1,0:T(8,128)(2,1)S(1)}, u32[]{:S(2)}, u32[]{:S(2)}) collective-permute-start(bf16[208,128]{1,0:T(8,128)(2,1)S(1)} %get-tuple-element.48), channel_id=1, source_target_pairs={{0,1},{1,0},{2,3},{3,2},{4,5},{5,4},{6,7},{7,6},{8,9},{9,8},{10,11... | collective-permute-start | bytes 159752 | tf_op jit(solution)/shard_map/ppermute | solution.py:623
  5.3 0.0 collective-permute-start.1
  5.3 2.0 %shard_map.105 = (bf16[2,128,256]{2,1,0:T(8,128)(2,1)S(1)}, f32[128,256]{1,0:T(8,128)S(1)}, f32[128,256]{1,0:T(8,128)S(1)}, f32[128,256]{1,0:T(8,128)S(1)}, f32[...) custom-call(f32[128,256]{1,0:T(8,128)S(1)} %get-tuple-element.36.v_r, ...), custom_call_target="tpu_custom_call" | custom-call | tf_op jit(solution)/shard_map/pallas_call | solution.py:631
  7.3 0.1 collective-permute-done.one_ref
  7.4 0.0 collective-permute-done.1.two_ref
  7.4 0.4 %shard_map.106 = (bf16[2,128,384]{2,1,0:T(8,128)(2,1)S(1)}, bf16[7,128,128]{2,1,0:T(8,128)(2,1)S(1)}, bf16[224,256]{1,0:T(8,128)(2,1)S(1)}, bf16[224,256]{1,0:T(8,128)(2,1)S(1)}) custom-call(bf16[2,128,256]{2,1,0:T(8,128)(2,1)S(1)} %get-tuple-element.45.d_ref, f32[128,256]{1,0:T(8,128)S(1)} %get-tuple-element.36.v_ref, ...), custom_call_target="tpu_custom_call" | custom-call | tf_op jit(solution)/shard_map/pallas_call | solution.py:631
  7.8 0.5 %collective-permute-start.2 = (bf16[224,256]{1,0:T(8,128)(2,1)S(1)}, bf16[224,256]{1,0:T(8,128)(2,1)S(1)}, u32[]{:S(2)}, u32[]{:S(2)}) collective-permute-start(bf16[224,256]{1,0:T(8,128)(2,1)S(1)} %get-tuple-element.62), channel_id=1, source_target_pairs={{0,8},{1,9},{2,10},{3,11},{4,12},{5,13},{6,14},{7,15},{8,0},{9,1},... | collective-permute-start | bytes 344072 | tf_op jit(solution)/shard_map/ppermute | solution.py:623
  8.3 4.1 %collective-permute-start.3 = (bf16[224,256]{1,0:T(8,128)(2,1)S(1)}, bf16[224,256]{1,0:T(8,128)(2,1)S(1)}, u32[]{:S(2)}, u32[]{:S(2)}) collective-permute-start(bf16[224,256]{1,0:T(8,128)(2,1)S(1)} %get-tuple-element.63), channel_id=1, source_target_pairs={{0,2},{1,3},{2,0},{3,1},{4,6},{5,7},{6,4},{7,5},{8,16},{9,17},{10,... | collective-permute-start | bytes 344072 | tf_op jit(solution)/shard_map/ppermute | solution.py:623
  12.4 2.1 %shard_map.107 = (f32[2,176,384]{2,1,0:T(8,128)S(1)}, f32[2,176,384]{2,1,0:T(8,128)S(1)}, f32[176,384]{1,0:T(8,128)S(1)}, f32[176,384]{1,0:T(8,128)S(1)}, bf16[2...) custom-call(bf16[2,128,384]{2,1,0:T(8,128)(2,1)S(1)} %get-tuple-element.50.df_ref, ...), custom_call_target="tpu_custom_call" | custom-call | tf_op jit(solution)/shard_map/pallas_call | solution.py:631
  14.6 0.0 collective-permute-done.2.one_ref
  14.6 0.6 %collective-permute-done.3.two_ref = bf16[224,256]{1,0:T(8,128)(2,1)S(1)} collective-permute-done((bf16[224,256]{1,0:T(8,128)(2,1)S(1)}, bf16[224,256]{1,0:T(8,128)(2,1)S(1)}, u32[]{:S(2)}, u32[]{:S(2)}) %collective-permute-start.3) | collective-permute-done | bytes 114720 | tf_op jit(solution)/shard_map/ppermute | solution.py:623
  15.2 3.0 %shard_map.108 = (f32[128,256]{1,0:T(8,128)}, f32[2,128,256]{2,1,0:T(8,128)}, f32[2,176,384]{2,1,0:T(8,128)S(1)}, f32[2,176,384]{2,1,0:T(8,128)S(1)}, f32[176,384]{1,0:T(8,128)S(1)}, /*index=5*/f32[176,384]{1,0:T(8,128)S(1)}) custom-call(bf16[2,128,384]{2,1,0:T(8,128)(2,1)S(1)} %get-tuple-elem, ...), custom_call_target="tpu_custom_call", output_to_operand_aliasing={{2}: (14, {}), {3}: (15, {}), {4}: (16, {}), {5}: (17, {})} | custom-call | tf_op jit(solution)/shard_map/pallas_call | solution.py:631
Async XLA Ops:
  2.2 5.2 %collective-permute-start = (bf16[208,128]{1,0:T(8,128)(2,1)S(1)}, bf16[208,128]{1,0:T(8,128)(2,1)S(1)}, u32[]{:S(2)}, u32[]{:S(2)}) collective-permute-start(bf16[208,128]{1,0:T(8,128)(2,1)S(1)} %get-tuple-element.48), channel_id=1, source_target_pairs={{0,1},{1,0},{2,3},{3,2},{4,5},{5,4},{6,7},{7,6},{8,9},{9,8},{10,11... | collective-permute-start | bytes 159752 | tf_op jit(solution)/shard_map/ppermute | solution.py:623
  5.3 2.1 %collective-permute-start.1 = (bf16[208,128]{1,0:T(8,128)(2,1)S(1)}, bf16[208,128]{1,0:T(8,128)(2,1)S(1)}, u32[]{:S(2)}, u32[]{:S(2)}) collective-permute-start(bf16[208,128]{1,0:T(8,128)(2,1)S(1)} %get-tuple-element.49), channel_id=1, source_target_pairs={{0,8},{1,2},{2,1},{3,4},{4,3},{5,6},{6,5},{7,15},{8,0},{9,10},{10,... | collective-permute-start | bytes 159752 | tf_op jit(solution)/shard_map/ppermute | solution.py:623
  7.8 6.8 %collective-permute-start.2 = (bf16[224,256]{1,0:T(8,128)(2,1)S(1)}, bf16[224,256]{1,0:T(8,128)(2,1)S(1)}, u32[]{:S(2)}, u32[]{:S(2)}) collective-permute-start(bf16[224,256]{1,0:T(8,128)(2,1)S(1)} %get-tuple-element.62), channel_id=1, source_target_pairs={{0,8},{1,9},{2,10},{3,11},{4,12},{5,13},{6,14},{7,15},{8,0},{9,1},... | collective-permute-start | bytes 344072 | tf_op jit(solution)/shard_map/ppermute | solution.py:623
  8.3 6.9 %collective-permute-start.3 = (bf16[224,256]{1,0:T(8,128)(2,1)S(1)}, bf16[224,256]{1,0:T(8,128)(2,1)S(1)}, u32[]{:S(2)}, u32[]{:S(2)}) collective-permute-start(bf16[224,256]{1,0:T(8,128)(2,1)S(1)} %get-tuple-element.63), channel_id=1, source_target_pairs={{0,2},{1,3},{2,0},{3,1},{4,6},{5,7},{6,4},{7,5},{8,16},{9,17},{10,... | collective-permute-start | bytes 344072 | tf_op jit(solution)/shard_map/ppermute | solution.py:623
